TPU v7x, 32 devices: a whole 2x2x4 slice. The times are simulated.
32 devices in a mesh: section: 4 (over y, core), tensor: 2 (over x), dp: 4 (over z).
Axes of the slice: x: 2, y: 2, z: 4, core: 2. Of those that a mesh axis runs over, the one named last changes fastest.
Arguments:
- acts: bfloat16 [4, 8, 256, 2048], P('section', 'dp', 'tensor'), parts along dimension 1, may hold values from -6 to 6
- fresh: bfloat16 [8, 256, 2048], P('dp', 'tensor'), parts along dimension 0, may hold values from -6 to 6
- order: int32 [4, 2], P('section'), may hold values from 0 to 1
- ln_gain: float32 [4, 2048], P('section'), may hold values from 0.1 to 1.9
- ln_bias: float32 [4, 2048], P('section'), may hold values from -3 to 3
- wqkv: bfloat16 [4, 2048, 6144], P('section', None, 'tensor'), may hold values from -4 to 4
- wo: bfloat16 [4, 2048, 2048], P('section', 'tensor'), may hold values from -0.125 to 0.125
Outputs:
- section_out: bfloat16 [8, 4, 256, 2048], P('dp', 'section', 'tensor'), parts along dimension 0
- held: bfloat16 [4, 8, 256, 2048], P('section', 'dp', 'tensor'), parts along dimension 1
There are 4 independent parts, one for each index of `dp`. A program takes and returns all parts, laid end to end along the dimension named above; an argument that names none is the same for every part. Nothing has to cross between parts.
All inputs are finite; a program needn't handle non-finite values.
Results may differ from a plain program's by a relative error of at most 0.017.
Values may be sent and summed in bfloat16 or wider, within the bound.
No kernel may reach another device: no remote copies, remote signals or barrier semaphores. Data moves between devices by JAX's collectives and lax.ppermute only.
A program may use at most 64 MiB of HBM per device.

v0:
```python
import jax
import jax.numpy as jnp
from jax import lax
from jax.sharding import PartitionSpec as P

HD = 128
TICKS = 2


def from_behind(block, axis, distance):
    devices = range(lax.axis_size(axis))
    route = [(i - distance, i) for i in devices if i - distance in devices]
    return lax.ppermute(block, axis, route)


def normed(rows, gain, bias):
    values = rows.astype(jnp.float32)
    centred = values - jnp.mean(values, axis=-1, keepdims=True)
    spread = jnp.mean(centred * centred, axis=-1, keepdims=True)
    return (centred * lax.rsqrt(spread + 1e-06) * gain + bias).astype(jnp.bfloat16)


def attend(qkv):
    length = qkv.shape[0]
    local_heads = qkv.shape[1] // (3 * HD)
    grid = qkv.reshape(length, local_heads, 3, HD)
    scores = jnp.einsum(
        "qhe,khe->hqk", grid[:, :, 0], grid[:, :, 1], preferred_element_type=jnp.float32
    )
    scores = scores / jnp.sqrt(jnp.float32(HD))
    probs = jax.nn.softmax(scores, axis=-1).astype(jnp.bfloat16)
    mixed = jnp.einsum("hqk,khe->qhe", probs, grid[:, :, 2], preferred_element_type=jnp.float32)
    return mixed.astype(jnp.bfloat16).reshape(length, local_heads * HD)


def body(acts, fresh, order, ln_gain, ln_bias, wqkv, wo):
    gain = ln_gain[0]
    bias = ln_bias[0]
    w_in = wqkv[0]
    w_out = wo[0]
    first = lax.axis_index("section") == 0
    slot_ids = jnp.arange(acts.shape[1], dtype=jnp.int32)
    outputs = []
    slots = acts[0]
    for tick in range(TICKS):
        chosen = order[0, tick]
        current = lax.dynamic_index_in_dim(slots, chosen, 0, keepdims=False)
        qkv = jnp.dot(
            normed(lax.all_gather(current, "tensor", axis=0, tiled=True), gain, bias),
            w_in,
            preferred_element_type=jnp.float32,
        ).astype(jnp.bfloat16)
        mixed = attend(qkv)
        total = lax.psum_scatter(
            jnp.dot(mixed, w_out, preferred_element_type=jnp.float32).astype(jnp.bfloat16),
            "tensor",
            scatter_dimension=0,
            tiled=True,
        ).astype(jnp.float32)
        result = (current.astype(jnp.float32) + total).astype(jnp.bfloat16)
        outputs.append(result)
        arriving = from_behind(result, "section", 1)
        arriving = jnp.where(first, fresh[tick], arriving)
        slots = jnp.where((slot_ids == chosen)[:, None, None], arriving[None], slots)
    return (jnp.stack(outputs, axis=0)[:, None], slots[None])


def solution(mesh):
    return jax.shard_map(
        body,
        mesh=mesh,
        in_specs=(
            P("section", "dp", "tensor", None),
            P("dp", "tensor", None),
            P("section", None),
            P("section", None),
            P("section", None),
            P("section", None, "tensor"),
            P("section", "tensor", None),
        ),
        out_specs=(P("dp", "section", "tensor", None), P("section", "dp", "tensor", None)),
        check_vma=False,
    )
```

profile of v0, /device:TPU:1, one launch (start us, length us, event | category | flops | bytes accessed | tf_op | source)
XLA Modules:
  0.0 174.5 jit_solution(7933763739888886498)
XLA Ops:
  7.2 1.3 fusion.70
  10.5 1.9 %constant_dynamic-slice_fusion = bf16[1,1,128,2048]{3,2,1,0:T(8,128)(2,1)} fusion(bf16[1,2,128,2048]{3,2,1,0:T(8,128)(2,1)} %param.7, s32[]{:T(128)S(6)} %select_n.30), kind=kLoop, calls=%fused_computation.77 | loop fusion | bytes 1048580 | tf_op jit(solution)/shard_map/jit(dynamic_index_in_dim)/dynamic_slice | solution.py:47
  12.4 23.3 %all-gather.5.cloned.1.call-done = bf16[1,1,256,2048]{3,2,1,0:T(8,128)(2,1)} async-done(((bf16[1,1,128,2048]{3,2,1,0:T(8,128)(2,1)}), bf16[1,1,256,2048]{3,2,1,0:T(8,128)(2,1)}) %all-gather.5.cloned.1.call-update) | async-done | bytes 1048592 | tf_op jit(solution)/shard_map/all_gather | solution.py:49
  35.7 1.5 convert_reduce_fusion.1
  37.2 1.6 fusion.25
  38.9 8.2 %fusion.10 = bf16[256,3072]{1,0:T(8,128)(2,1)S(1)} fusion(bf16[1,2048,3072]{2,1,0:T(8,128)(2,1)} %param.12, bf16[1,1,256,2048]{3,2,1,0:T(8,128)(2,1)S(1)} %copy-done.2, f32[2048]{0:T(1024)S(1)} %bitcast.164, f32[2048]{0:T(1024)S(1)} %bitcast.166, f32[256]{0:T(256)S(1)} %add_rsqrt_fusion.1, f32[256]{0:T(256)S(1)} %broadcast_multiply_fusion.1), kind=kOutput, calls=%fused_computation.10 | convolution fusion | flops 3225157632 | bytes 15222784 | tf_op jit(solution)/shard_map/dot_general | solution.py:48
  49.8 4.5 %fusion.16 = bf16[256,2048]{1,0:T(8,128)(2,1)} fusion(bf16[256,1024]{0,1:T(8,128)(2,1)S(1)} %bitcast.168, bf16[1,1024,2048]{2,1,0:T(8,128)(2,1)} %param.13), kind=kOutput, calls=%fused_computation.16 | convolution fusion | flops 1074266112 | bytes 5767168 | tf_op jit(solution)/shard_map/dot_general | solution.py:55
  54.4 20.5 %reduce-scatter.3.cloned.1.call-done = bf16[128,2048]{1,0:T(8,128)(2,1)} async-done(((bf16[256,2048]{1,0:T(8,128)(2,1)}), bf16[128,2048]{1,0:T(8,128)(2,1)}) %reduce-scatter.3.cloned.1.call-update) | async-done | bytes 524304 | tf_op jit(solution)/shard_map/reduce_scatter | solution.py:54
  76.0 3.8 %collective-permute-start = (bf16[128,2048]{1,0:T(8,128)(2,1)S(1)}, bf16[128,2048]{1,0:T(8,128)(2,1)}, u32[]{:S(2)}, u32[]{:S(2)}) collective-permute-start(bf16[128,2048]{1,0:T(8,128)(2,1)S(1)} %fusion.41), channel_id=1, source_target_pairs={{0,8},{8,16},{16,24},{1,9},{9,17},{17,25},{2,10},{10,18},{18,26},{... | collective-permute-start | bytes 1572872 | tf_op jit(solution)/shard_map/ppermute | solution.py:13
  82.8 3.2 %collective-permute-done = bf16[128,2048]{1,0:T(8,128)(2,1)} collective-permute-done((bf16[128,2048]{1,0:T(8,128)(2,1)S(1)}, bf16[128,2048]{1,0:T(8,128)(2,1)}, u32[]{:S(2)}, u32[]{:S(2)}) %collective-permute-start) | collective-permute-done | bytes 524320 | tf_op jit(solution)/shard_map/ppermute | solution.py:13
  87.1 1.5 dynamic-slice_select_fusion
  88.9 21.9 %all-gather.7.cloned.1.call-done = bf16[1,256,2048]{2,1,0:T(8,128)(2,1)} async-done(((bf16[1,128,2048]{2,1,0:T(8,128)(2,1)}), bf16[1,256,2048]{2,1,0:T(8,128)(2,1)}) %all-gather.7.cloned.1.call-update) | async-done | bytes 1048592 | tf_op jit(solution)/shard_map/all_gather | solution.py:49
  110.7 1.5 convert_reduce_fusion
  112.3 1.6 fusion.32
  113.9 9.4 %fusion.13 = bf16[256,3072]{1,0:T(8,128)(2,1)} fusion(bf16[1,2048,3072]{2,1,0:T(8,128)(2,1)} %param.12, bf16[1,256,2048]{2,1,0:T(8,128)(2,1)S(1)} %copy-done.3, f32[256]{0:T(256)S(1)} %add_rsqrt_fusion, f32[256]{0:T(256)S(1)} %broadcast_multiply_fusion, f32[2048]{0:T(1024)S(1)} %bitcast.165, f32[2048]{0:T(1024)S(1)} %bitcast.167), kind=kOutput, calls=%fused_computation.11 | convolution fusion | flops 3225157632 | bytes 15222784 | tf_op jit(solution)/shard_map/dot_general | solution.py:48
  123.4 2.6 %copy.23 = bf16[256,3072]{0,1:T(8,128)(2,1)} copy(bf16[256,3072]{1,0:T(8,128)(2,1)} %fusion.13) | data formatting | bytes 3145728 | tf_op jit(solution)/shard_map/convert_element_type | solution.py:52
  126.0 2.0 %fusion.72 = f32[8,256]{1,0:T(8,128)S(1)} fusion(bf16[256,8,3,128]{0,3,2,1:T(8,128)(2,1)} %bitcast.162), kind=kOutput, calls=%fused_computation.84 | convolution fusion | flops 135790848 | bytes 1056768 | tf_op jit(solution)/shard_map/sub | solution.py:31
  128.0 2.5 %convolution_convert_fusion = bf16[8,128,256]{2,1,0:T(8,128)(2,1)S(1)} fusion(f32[8,256]{1,0:T(8,128)S(1)} %fusion.72, bf16[256,8,3,128]{0,3,2,1:T(8,128)(2,1)} %bitcast.163), kind=kOutput, calls=%fused_computation.40 | convolution fusion | flops 270797056 | bytes 2105344 | tf_op jit(solution)/shard_map/hqk,khe->qhe/dot_general | solution.py:32
  130.5 4.5 %fusion.19 = bf16[256,2048]{1,0:T(8,128)(2,1)} fusion(bf16[256,1024]{0,1:T(8,128)(2,1)S(1)} %bitcast.169, bf16[1,1024,2048]{2,1,0:T(8,128)(2,1)} %param.13), kind=kOutput, calls=%fused_computation.17 | convolution fusion | flops 1074266112 | bytes 5767168 | tf_op jit(solution)/shard_map/dot_general | solution.py:55
  135.0 20.6 %reduce-scatter.5.cloned.1.call-done = bf16[128,2048]{1,0:T(8,128)(2,1)} async-done(((bf16[256,2048]{1,0:T(8,128)(2,1)}), bf16[128,2048]{1,0:T(8,128)(2,1)}) %reduce-scatter.5.cloned.1.call-update) | async-done | bytes 524304 | tf_op jit(solution)/shard_map/reduce_scatter | solution.py:54
  155.6 1.3 fusion.40
  156.8 3.8 %collective-permute-start.1 = (bf16[128,2048]{1,0:T(8,128)(2,1)S(1)}, bf16[128,2048]{1,0:T(8,128)(2,1)S(1)}, u32[]{:S(2)}, u32[]{:S(2)}) collective-permute-start(bf16[128,2048]{1,0:T(8,128)(2,1)S(1)} %fusion.40), channel_id=1, source_target_pairs={{0,8},{8,16},{16,24},{1,9},{9,17},{17,25},{2,10},{10,18},{18,26},{... | collective-permute-start | bytes 1572872 | tf_op jit(solution)/shard_map/ppermute | solution.py:13
  162.3 4.5 %collective-permute-done.1 = bf16[128,2048]{1,0:T(8,128)(2,1)S(1)} collective-permute-done((bf16[128,2048]{1,0:T(8,128)(2,1)S(1)}, bf16[128,2048]{1,0:T(8,128)(2,1)S(1)}, u32[]{:S(2)}, u32[]{:S(2)}) %collective-permute-start.1) | collective-permute-done | bytes 524320 | tf_op jit(solution)/shard_map/ppermute | solution.py:13
  166.8 1.2 select_select_fusion
  (38 shorter events, 8.3 us)
Async XLA Ops:
  7.2 31.7 %copy-start.6 = (f32[1,2048]{1,0:T(1,128)S(1)}, f32[1,2048]{1,0:T(1,128)}, u32[]{:S(2)}) copy-start(f32[1,2048]{1,0:T(1,128)} %param.11) | copy-start | bytes 24580
  7.2 31.7 %copy-start.7 = (f32[1,2048]{1,0:T(1,128)S(1)}, f32[1,2048]{1,0:T(1,128)}, u32[]{:S(2)}) copy-start(f32[1,2048]{1,0:T(1,128)} %param.10) | copy-start | bytes 24580
  7.2 28.5 %all-gather.5.cloned.1.call-start = ((), (), s32[]{:S(2)}) async-start(), calls=%async_computation.4 | async-start | bytes 1572864 | tf_op jit(solution)/shard_map/all_gather | solution.py:49
  12.4 62.5 %reduce-scatter.3.cloned.1.call-start = ((), (), s32[]{:S(2)}) async-start(), calls=%async_computation.2 | async-start | bytes 1572864 | tf_op jit(solution)/shard_map/reduce_scatter | solution.py:54
  35.7 3.2 %copy-start.2 = (bf16[1,1,256,2048]{3,2,1,0:T(8,128)(2,1)S(1)}, bf16[1,1,256,2048]{3,2,1,0:T(8,128)(2,1)}, u32[]{:S(2)}) copy-start(bf16[1,1,256,2048]{3,2,1,0:T(8,128)(2,1)} %all-gather.5.cloned.1.call-done) | copy-start | bytes 3145732
  49.8 25.1 %copy-start = (bf16[1,2,128,2048]{3,2,1,0:T(8,128)(2,1)S(1)}, bf16[1,2,128,2048]{3,2,1,0:T(8,128)(2,1)}, u32[]{:S(2)}) copy-start(bf16[1,2,128,2048]{3,2,1,0:T(8,128)(2,1)} %param.7) | copy-start | bytes 3145732
  54.3 31.7 %copy-start.4 = (bf16[2,128,2048]{2,1,0:T(8,128)(2,1)S(1)}, bf16[2,128,2048]{2,1,0:T(8,128)(2,1)}, u32[]{:S(2)}) copy-start(bf16[2,128,2048]{2,1,0:T(8,128)(2,1)} %param.8) | copy-start | bytes 3145732
  54.3 56.4 %all-gather.7.cloned.1.call-start = ((), (), s32[]{:S(2)}) async-start(), calls=%async_computation.5 | async-start | bytes 1572864 | tf_op jit(solution)/shard_map/all_gather | solution.py:49
  76.0 10.0 %collective-permute-start = (bf16[128,2048]{1,0:T(8,128)(2,1)S(1)}, bf16[128,2048]{1,0:T(8,128)(2,1)}, u32[]{:S(2)}, u32[]{:S(2)}) collective-permute-start(bf16[128,2048]{1,0:T(8,128)(2,1)S(1)} %fusion.41), channel_id=1, source_target_pairs={{0,8},{8,16},{16,24},{1,9},{9,17},{17,25},{2,10},{10,18},{18,26},{... | collective-permute-start | bytes 1572872 | tf_op jit(solution)/shard_map/ppermute | solution.py:13
  88.6 66.9 %reduce-scatter.5.cloned.1.call-start = ((), (), s32[]{:S(2)}) async-start(), calls=%async_computation.3 | async-start | bytes 1572864 | tf_op jit(solution)/shard_map/reduce_scatter | solution.py:54
  110.7 3.2 %copy-start.3 = (bf16[1,256,2048]{2,1,0:T(8,128)(2,1)S(1)}, bf16[1,256,2048]{2,1,0:T(8,128)(2,1)}, u32[]{:S(2)}) copy-start(bf16[1,256,2048]{2,1,0:T(8,128)(2,1)} %all-gather.7.cloned.1.call-done) | copy-start | bytes 3145732
  130.5 25.1 %copy-start.1 = (bf16[1,128,2048]{2,1,0:T(8,128)(2,1)S(1)}, bf16[1,128,2048]{2,1,0:T(8,128)(2,1)}, u32[]{:S(2)}) copy-start(bf16[1,128,2048]{2,1,0:T(8,128)(2,1)} %dynamic-slice_select_fusion) | copy-start | bytes 1572868
  155.6 11.2 %copy-start.5 = (bf16[2,128,2048]{2,1,0:T(8,128)(2,1)S(1)}, bf16[2,128,2048]{2,1,0:T(8,128)(2,1)}, u32[]{:S(2)}) copy-start(bf16[2,128,2048]{2,1,0:T(8,128)(2,1)} %param.8) | copy-start | bytes 3145732
  156.8 9.9 %collective-permute-start.1 = (bf16[128,2048]{1,0:T(8,128)(2,1)S(1)}, bf16[128,2048]{1,0:T(8,128)(2,1)S(1)}, u32[]{:S(2)}, u32[]{:S(2)}) collective-permute-start(bf16[128,2048]{1,0:T(8,128)(2,1)S(1)} %fusion.40), channel_id=1, source_target_pairs={{0,8},{8,16},{16,24},{1,9},{9,17},{17,25},{2,10},{10,18},{18,26},{... | collective-permute-start | bytes 1572872 | tf_op jit(solution)/shard_map/ppermute | solution.py:13
Sparse Core Ops, SparseCore 0:
  12.5 23.1 all-gather.4
  54.5 20.3 reduce-scatter.2
  88.8 21.9 all-gather.6
  135.1 20.3 reduce-scatter.4
where the time goes:
time: 175 us
  waiting for transfers between devices  94 us (54%)
  matrix products  33.1 us (19%)
  between operations  17.5 us (10%)
  other arithmetic  14.9 us (9%)
  starting transfers between devices  8 us (5%)
  local copies, waits for them, and re-layouts  7.08 us (4%)
    all_gather x2, waiting for transfers between devices, body(): lax.all_gather(current, 'tensor', axis=0, tiled=True)  45.1 us
    reduce_scatter x2, waiting for transfers between devices, body(): lax.psum_scatter(jnp.dot(mixed, w_out, preferred_element_type=jnp.float32...  41 us
    dot_general x2, matrix products, body(): jnp.dot(normed(lax.all_gather(current, 'tensor', axis=0, tiled=True), gai...  17.6 us
    dot_general x2, matrix products, body(): jnp.dot(mixed, w_out, preferred_element_type=jnp.float32)  9 us
    ppermute x2, waiting for transfers between devices, from_behind(): return lax.ppermute(block, axis, route)  7.71 us
    ppermute x2, starting transfers between devices, from_behind(): return lax.ppermute(block, axis, route)  7.66 us
    dot_general x2, matrix products, attend(): jnp.einsum('hqk,khe->qhe', probs, grid[:, :, 2], preferred_element_type=j...  3.6 us
  transfers between devices with their start and end apart: 6, of which 6 were waited for; matrix products, arithmetic and copies ran while one was open for 2% of the time, Pallas kernels for 0%

commit v1 on v0

v1 whole, which is shorter than its diff:
```python
import jax
import jax.numpy as jnp
from jax import lax
from jax.sharding import PartitionSpec as P

HD = 128
TICKS = 2


def from_behind(block, axis, distance):
    devices = range(lax.axis_size(axis))
    route = [(i - distance, i) for i in devices if i - distance in devices]
    return lax.ppermute(block, axis, route)


def rotate(block, axis, shift):
    size = lax.axis_size(axis)
    return lax.ppermute(block, axis, [(i, (i + shift) % size) for i in range(size)])


def normed(rows, gain, bias):
    values = rows.astype(jnp.float32)
    centred = values - jnp.mean(values, axis=-1, keepdims=True)
    spread = jnp.mean(centred * centred, axis=-1, keepdims=True)
    return (centred * lax.rsqrt(spread + 1e-06) * gain + bias).astype(jnp.bfloat16)


def attend(queries, keys):
    local_heads = queries.shape[1] // (3 * HD)
    q = queries.reshape(queries.shape[0], local_heads, 3, HD)[:, :, 0]
    grid = keys.reshape(keys.shape[0], local_heads, 3, HD)
    scores = jnp.einsum("qhe,khe->hqk", q, grid[:, :, 1], preferred_element_type=jnp.float32)
    scores = scores / jnp.sqrt(jnp.float32(HD))
    probs = jax.nn.softmax(scores, axis=-1).astype(jnp.bfloat16)
    mixed = jnp.einsum("hqk,khe->qhe", probs, grid[:, :, 2], preferred_element_type=jnp.float32)
    return mixed.astype(jnp.bfloat16).reshape(queries.shape[0], local_heads * HD)


def layer(current, gain, bias, w_in, w_out):
    size = lax.axis_size("tensor")
    blocks = [current] + [rotate(current, "tensor", j) for j in range(1, size)]
    parts = [
        jnp.dot(normed(b, gain, bias), w_in, preferred_element_type=jnp.float32).astype(jnp.bfloat16)
        for b in blocks
    ]
    keys = jnp.concatenate(parts, axis=0)
    total = current.astype(jnp.float32)
    sums = []
    for j in list(range(1, size)) + [0]:
        mixed = attend(parts[j], keys)
        piece = jnp.dot(mixed, w_out, preferred_element_type=jnp.float32).astype(jnp.bfloat16)
        sums.append(rotate(piece, "tensor", -j) if j else piece)
    added = sum(s.astype(jnp.float32) for s in sums)
    return (total + added).astype(jnp.bfloat16)


def body(acts, fresh, order, ln_gain, ln_bias, wqkv, wo):
    first = lax.axis_index("section") == 0
    slot_ids = jnp.arange(acts.shape[1], dtype=jnp.int32)
    outputs = []
    slots = acts[0]
    for tick in range(TICKS):
        chosen = order[0, tick]
        current = lax.dynamic_index_in_dim(slots, chosen, 0, keepdims=False)
        result = layer(current, ln_gain[0], ln_bias[0], wqkv[0], wo[0])
        outputs.append(result)
        arriving = from_behind(result, "section", 1)
        arriving = jnp.where(first, fresh[tick], arriving)
        slots = jnp.where((slot_ids == chosen)[:, None, None], arriving[None], slots)
    return (jnp.stack(outputs, axis=0)[:, None], slots[None])


def solution(mesh):
    return jax.shard_map(
        body,
        mesh=mesh,
        in_specs=(
            P("section", "dp", "tensor", None),
            P("dp", "tensor", None),
            P("section", None),
            P("section", None),
            P("section", None),
            P("section", None, "tensor"),
            P("section", "tensor", None),
        ),
        out_specs=(P("dp", "section", "tensor", None), P("section", "dp", "tensor", None)),
        check_vma=False,
    )
```

time: 175 us -> 130 us (0.74)
  waiting for transfers between devices: 94 us -> 16.8 us
  matrix products: 33.1 us -> 70.8 us
  between operations: 17.5 us -> 4.62 us
  starting transfers between devices: 8 us -> 14.4 us
  other arithmetic: 14.9 us -> 10.8 us
  local copies, waits for them, and re-layouts: 7.08 us -> 11 us
    all_gather x2 -> x0, waiting for transfers between devices: 45.1 us -> none  [body(): lax.all_gather(current, 'tensor', axis=0, tiled=True)]
    reduce_scatter x2 -> x0, waiting for transfers between devices: 41 us -> none  [body(): lax.psum_scatter(jnp.dot(mixed, w_out, preferred_element_type=jnp.float32...]
    dot_general x4 -> x12, matrix products: 26.6 us -> 49.8 us  [the longest x4 26.8 us: layer(): jnp.dot(normed(b, gain, bias), w_in, preferred_element_type=jnp.float32)]
    dot_general x2 -> x4, matrix products: 3.6 us -> 14.5 us  [attend(): jnp.einsum('hqk,khe->qhe', probs, grid[:, :, 2], preferred_element_type=j...]
    ppermute x0 -> x4, waiting for transfers between devices: none -> 9.39 us  [rotate(): lax.ppermute(block, axis, [(i, (i + shift) % size) for i in range(size)])]
    ppermute x0 -> x4, starting transfers between devices: none -> 5.27 us  [rotate(): lax.ppermute(block, axis, [(i, (i + shift) % size) for i in range(size)])]
    concatenate x0 -> x2, local copies, waits for them, and re-layouts: none -> 4.37 us  [layer(): keys = jnp.concatenate(parts, axis=0)]
    sub x2 -> x4, matrix products: 2.87 us -> 6.58 us  [attend(): probs = jax.nn.softmax(scores, axis=-1).astype(jnp.bfloat16)]
  transfers between devices with their start and end apart: 6 -> 6, of which waited for: 6 -> 5; matrix products, arithmetic and copies ran while one was open for 2% -> 27% of each run, Pallas kernels for 0% -> 0%
where the time goes in v1:
time: 130 us; the launch traced here: 129 us
  matrix products  70.8 us (54%)
  waiting for transfers between devices  16.8 us (13%)
  starting transfers between devices  14.4 us (11%)
  local copies, waits for them, and re-layouts  11 us (8%)
  other arithmetic  10.8 us (8%)
  between operations  4.62 us (4%)
    dot_general x4, matrix products, layer(): jnp.dot(normed(b, gain, bias), w_in, preferred_element_type=jnp.float32)  26.8 us
    dot_general x4, matrix products, attend(): jnp.einsum('hqk,khe->qhe', probs, grid[:, :, 2], preferred_element_type=j...  14.5 us
    dot_general x4, matrix products, layer(): jnp.dot(mixed, w_out, preferred_element_type=jnp.float32)  13.6 us
    ppermute x4, waiting for transfers between devices, rotate(): lax.ppermute(block, axis, [(i, (i + shift) % size) for i in range(size)])  9.39 us
    dot_general x4, matrix products, attend(): jnp.einsum('qhe,khe->hqk', q, grid[:, :, 1], preferred_element_type=jnp.f...  9.29 us
    ppermute x2, starting transfers between devices, from_behind(): return lax.ppermute(block, axis, route)  9.15 us
    ppermute x2, waiting for transfers between devices, from_behind(): return lax.ppermute(block, axis, route)  7.43 us
    sub x4, matrix products, attend(): probs = jax.nn.softmax(scores, axis=-1).astype(jnp.bfloat16)  6.58 us
  transfers between devices with their start and end apart: 6, of which 5 were waited for; matrix products, arithmetic and copies ran while one was open for 27% of the time, Pallas kernels for 0%

profile of v1, /device:TPU:1, one launch (start us, length us, event | category | flops | bytes accessed | tf_op | source)
XLA Modules:
  0.0 128.5 jit_solution(13724723932273864875)
XLA Ops:
  5.2 2.1 %collective-permute-start = (bf16[128,2048]{1,0:T(8,128)(2,1)S(1)}, bf16[128,2048]{1,0:T(8,128)(2,1)S(1)}, u32[]{:S(2)}, u32[]{:S(2)}) collective-permute-start(bf16[128,2048]{1,0:T(8,128)(2,1)S(1)} %get-tuple-element.9), channel_id=1, source_target_pairs={{0,4},{4,0},{1,5},{5,1},{2,6},{6,2},{3,7},{7,3},{8,12},{12,8},{9,1... | collective-permute-start | bytes 1572872 | tf_op jit(solution)/shard_map/ppermute | solution.py:18
  7.6 6.5 %fusion.20 = bf16[128,3072]{1,0:T(8,128)(2,1)S(1)} fusion(bf16[1,2048,3072]{2,1,0:T(8,128)(2,1)} %param.12, f32[2048]{0:T(1024)S(1)} %bitcast.191, f32[2048]{0:T(1024)S(1)} %bitcast.195, f32[128]{0:T(128)S(1)} %add_rsqrt_fusion.3, f32[128]{0:T(128)S(1)} %broadcast_multiply_fusion.3, bf16[1,2,128,2048]{3,2,1,0:T(8,128)(2,1)S(1)} %copy-done, s32[]{:T(128)S(6)} %select_n.30), kind=kOutput, calls=%fused_computation.20 | convolution fusion | flops 1612578816 | bytes 13911044 | tf_op jit(solution)/shard_map/dot_general | solution.py:43
  15.3 3.6 %collective-permute-done = bf16[128,2048]{1,0:T(8,128)(2,1)S(1)} collective-permute-done((bf16[128,2048]{1,0:T(8,128)(2,1)S(1)}, bf16[128,2048]{1,0:T(8,128)(2,1)S(1)}, u32[]{:S(2)}, u32[]{:S(2)}) %collective-permute-start) | collective-permute-done | bytes 524320 | tf_op jit(solution)/shard_map/ppermute | solution.py:18
  19.4 6.5 %fusion.23 = bf16[128,3072]{1,0:T(8,128)(2,1)S(1)} fusion(bf16[1,2048,3072]{2,1,0:T(8,128)(2,1)} %param.12, bf16[128,2048]{1,0:T(8,128)(2,1)S(1)} %collective-permute-done, f32[2048]{0:T(1024)S(1)} %bitcast.192, f32[2048]{0:T(1024)S(1)} %bitcast.196, f32[128]{0:T(128)S(1)} %add_rsqrt_fusion.2, f32[128]{0:T(128)S(1)} %broadcast_multiply_fusion.2), kind=kOutput, calls=%fused_computation.21 | convolution fusion | flops 1612578816 | bytes 13911040 | tf_op jit(solution)/shard_map/dot_general | solution.py:43
  31.7 2.3 %convolution_multiply_fusion.3 = f32[8,128,256]{2,1,0:T(8,128)} fusion(bf16[256,8,3,128]{0,3,2,1:T(8,128)(2,1)S(1)} %bitcast.170, bf16[128,8,3,128]{0,3,2,1:T(8,128)(2,1)} %bitcast.188), kind=kOutput, calls=%fused_computation.49 | convolution fusion | flops 67371008 | bytes 1835008 | tf_op jit(solution)/shard_map/qhe,khe->hqk/dot_general | solution.py:32
  33.9 3.5 %convolution_convert_fusion.3 = bf16[8,128,128]{2,1,0:T(8,128)(2,1)S(1)} fusion(f32[8,128]{1,0:T(8,128)S(1)} %fusion.118, bf16[256,8,3,128]{0,3,2,1:T(8,128)(2,1)S(1)} %bitcast.171, f32[8,128,256]{2,1,0:T(8,128)} %convolution_multiply_fusion.3), kind=kOutput, calls=%fused_computation.61 | convolution fusion | flops 68027648 | bytes 2887680 | tf_op jit(solution)/shard_map/hqk,khe->qhe/dot_general | solution.py:35
  37.5 3.7 %fusion.32 = bf16[128,2048]{1,0:T(8,128)(2,1)} fusion(bf16[128,1024]{0,1:T(8,128)(2,1)S(1)} %bitcast.201, bf16[1,1024,2048]{2,1,0:T(8,128)(2,1)} %param.13), kind=kOutput, calls=%fused_computation.24 | convolution fusion | flops 537133056 | bytes 4980736 | tf_op jit(solution)/shard_map/dot_general | solution.py:51
  44.0 2.3 %convolution_multiply_fusion.2 = f32[8,128,256]{2,1,0:T(8,128)} fusion(bf16[256,8,3,128]{0,3,2,1:T(8,128)(2,1)S(1)} %bitcast.173, bf16[128,8,3,128]{0,3,2,1:T(8,128)(2,1)} %bitcast.184), kind=kOutput, calls=%fused_computation.48 | convolution fusion | flops 67371008 | bytes 1835008 | tf_op jit(solution)/shard_map/qhe,khe->hqk/dot_general | solution.py:32
  46.3 3.5 %convolution_convert_fusion.2 = bf16[8,128,128]{2,1,0:T(8,128)(2,1)S(1)} fusion(f32[8,128]{1,0:T(8,128)S(1)} %fusion.117, bf16[256,8,3,128]{0,3,2,1:T(8,128)(2,1)S(1)} %bitcast.174, f32[8,128,256]{2,1,0:T(8,128)} %convolution_multiply_fusion.2), kind=kOutput, calls=%fused_computation.60 | convolution fusion | flops 68027648 | bytes 2887680 | tf_op jit(solution)/shard_map/hqk,khe->qhe/dot_general | solution.py:35
  49.9 3.9 %collective-permute-done.1 = bf16[128,2048]{1,0:T(8,128)(2,1)} collective-permute-done((bf16[128,2048]{1,0:T(8,128)(2,1)}, bf16[128,2048]{1,0:T(8,128)(2,1)}, u32[]{:S(2)}, u32[]{:S(2)}) %collective-permute-start.1) | collective-permute-done | bytes 524320 | tf_op jit(solution)/shard_map/ppermute | solution.py:18
  53.8 3.1 %fusion.72 = bf16[128,2048]{1,0:T(8,128)(2,1)S(1)} fusion(bf16[128,2048]{1,0:T(8,128)(2,1)S(1)} %copy-done.2, bf16[128,2048]{1,0:T(8,128)(2,1)} %collective-permute-done.1, bf16[128,1024]{0,1:T(8,128)(2,1)S(1)} %bitcast.199, bf16[1,1024,2048]{2,1,0:T(8,128)(2,1)} %param.13), kind=kOutput, calls=%fused_computation.72 | convolution fusion | flops 538705920 | bytes 6029312 | tf_op jit(solution)/shard_map/dot_general | solution.py:51
  56.9 5.3 %collective-permute-start.2 = (bf16[128,2048]{1,0:T(8,128)(2,1)S(1)}, bf16[128,2048]{1,0:T(8,128)(2,1)S(1)}, u32[]{:S(2)}, u32[]{:S(2)}) collective-permute-start(bf16[128,2048]{1,0:T(8,128)(2,1)S(1)} %fusion.72), channel_id=1, source_target_pairs={{0,8},{8,16},{16,24},{1,9},{9,17},{17,25},{2,10},{10,18},{18,26},{... | collective-permute-start | bytes 1572872 | tf_op jit(solution)/shard_map/ppermute | solution.py:13
  65.1 3.0 %collective-permute-done.2 = bf16[128,2048]{1,0:T(8,128)(2,1)S(1)} collective-permute-done((bf16[128,2048]{1,0:T(8,128)(2,1)S(1)}, bf16[128,2048]{1,0:T(8,128)(2,1)S(1)}, u32[]{:S(2)}, u32[]{:S(2)}) %collective-permute-start.2) | collective-permute-done | bytes 524320 | tf_op jit(solution)/shard_map/ppermute | solution.py:13
  71.7 7.2 %fusion.26 = bf16[128,3072]{1,0:T(8,128)(2,1)S(1)} fusion(bf16[1,2048,3072]{2,1,0:T(8,128)(2,1)} %param.12, f32[2048]{0:T(1024)S(1)} %bitcast.193, f32[2048]{0:T(1024)S(1)} %bitcast.197, f32[128]{0:T(128)S(1)} %add_rsqrt_fusion.1, f32[128]{0:T(128)S(1)} %broadcast_multiply_fusion.1, bf16[2,128,2048]{2,1,0:T(8,128)(2,1)S(1)} %bitcast.168, s32[]{:T(128)S(6)} %select_n.34, ...), kind=kOutput, calls=%fused_computation.22 | convolution fusion | flops 1612840960 | bytes 14435333 | tf_op jit(solution)/shard_map/dot_general | solution.py:43
  80.6 6.6 %fusion.29 = bf16[128,3072]{1,0:T(8,128)(2,1)S(1)} fusion(bf16[1,2048,3072]{2,1,0:T(8,128)(2,1)} %param.12, bf16[128,2048]{1,0:T(8,128)(2,1)S(1)} %collective-permute-done.3, f32[128]{0:T(128)S(1)} %add_rsqrt_fusion, f32[128]{0:T(128)S(1)} %broadcast_multiply_fusion, f32[2048]{0:T(1024)S(1)} %bitcast.194, f32[2048]{0:T(1024)S(1)} %bitcast.198), kind=kOutput, calls=%fused_computation.23 | convolution fusion | flops 1612578816 | bytes 13911040 | tf_op jit(solution)/shard_map/dot_general | solution.py:43
  89.6 2.7 %copy.25 = bf16[256,3072]{0,1:T(8,128)(2,1)} copy(bf16[256,3072]{1,0:T(8,128)(2,1)} %pad_maximum_fusion.1) | data formatting | bytes 3145728 | tf_op jit(solution)/shard_map/concatenate | solution.py:46
  94.0 2.4 %convolution_multiply_fusion.1 = f32[8,128,256]{2,1,0:T(8,128)} fusion(bf16[256,8,3,128]{0,3,2,1:T(8,128)(2,1)} %bitcast.176, bf16[128,8,3,128]{0,3,2,1:T(8,128)(2,1)S(1)} %bitcast.190), kind=kOutput, calls=%fused_computation.47 | convolution fusion | flops 67371008 | bytes 1835008 | tf_op jit(solution)/shard_map/qhe,khe->hqk/dot_general | solution.py:32
  96.3 3.7 %convolution_convert_fusion.1 = bf16[8,128,128]{2,1,0:T(8,128)(2,1)S(1)} fusion(f32[8,128]{1,0:T(8,128)S(1)} %fusion.120, bf16[256,8,3,128]{0,3,2,1:T(8,128)(2,1)} %bitcast.177, f32[8,128,256]{2,1,0:T(8,128)} %convolution_multiply_fusion.1), kind=kOutput, calls=%fused_computation.59 | convolution fusion | flops 68027648 | bytes 2887680 | tf_op jit(solution)/shard_map/hqk,khe->qhe/dot_general | solution.py:35
  100.0 3.8 %fusion.41 = bf16[128,2048]{1,0:T(8,128)(2,1)} fusion(bf16[128,1024]{0,1:T(8,128)(2,1)S(1)} %bitcast.202, bf16[1,1024,2048]{2,1,0:T(8,128)(2,1)} %param.13), kind=kOutput, calls=%fused_computation.27 | convolution fusion | flops 537133056 | bytes 4980736 | tf_op jit(solution)/shard_map/dot_general | solution.py:51
  106.3 2.4 %convolution_multiply_fusion = f32[8,128,256]{2,1,0:T(8,128)} fusion(bf16[256,8,3,128]{0,3,2,1:T(8,128)(2,1)} %bitcast.179, bf16[128,8,3,128]{0,3,2,1:T(8,128)(2,1)S(1)} %bitcast.186), kind=kOutput, calls=%fused_computation.46 | convolution fusion | flops 67371008 | bytes 1835008 | tf_op jit(solution)/shard_map/qhe,khe->hqk/dot_general | solution.py:32
  108.6 3.7 %convolution_convert_fusion = bf16[8,128,128]{2,1,0:T(8,128)(2,1)S(1)} fusion(f32[8,128]{1,0:T(8,128)S(1)} %fusion.119, bf16[256,8,3,128]{0,3,2,1:T(8,128)(2,1)} %bitcast.180, f32[8,128,256]{2,1,0:T(8,128)} %convolution_multiply_fusion), kind=kOutput, calls=%fused_computation.58 | convolution fusion | flops 68027648 | bytes 2887680 | tf_op jit(solution)/shard_map/hqk,khe->qhe/dot_general | solution.py:35
  114.2 3.0 %fusion.75 = bf16[128,2048]{1,0:T(8,128)(2,1)S(1)} fusion(bf16[128,2048]{1,0:T(8,128)(2,1)S(1)} %get-tuple-element.7, bf16[128,2048]{1,0:T(8,128)(2,1)S(1)} %collective-permute-done.4, bf16[128,1024]{0,1:T(8,128)(2,1)S(1)} %bitcast.200, bf16[1,1024,2048]{2,1,0:T(8,128)(2,1)} %param.13), kind=kOutput, calls=%fused_computation.75 | convolution fusion | flops 538705920 | bytes 6029312 | tf_op jit(solution)/shard_map/dot_general | solution.py:51
  117.2 3.8 %collective-permute-start.5 = (bf16[128,2048]{1,0:T(8,128)(2,1)S(1)}, bf16[128,2048]{1,0:T(8,128)(2,1)S(1)}, u32[]{:S(2)}, u32[]{:S(2)}) collective-permute-start(bf16[128,2048]{1,0:T(8,128)(2,1)S(1)} %fusion.75), channel_id=1, source_target_pairs={{0,8},{8,16},{16,24},{1,9},{9,17},{17,25},{2,10},{10,18},{18,26},{... | collective-permute-start | bytes 1572872 | tf_op jit(solution)/shard_map/ppermute | solution.py:13
  122.7 4.5 %collective-permute-done.5 = bf16[128,2048]{1,0:T(8,128)(2,1)S(1)} collective-permute-done((bf16[128,2048]{1,0:T(8,128)(2,1)S(1)}, bf16[128,2048]{1,0:T(8,128)(2,1)S(1)}, u32[]{:S(2)}, u32[]{:S(2)}) %collective-permute-start.5) | collective-permute-done | bytes 524320 | tf_op jit(solution)/shard_map/ppermute | solution.py:13
  (64 shorter events, 30.8 us)
Async XLA Ops:
  0.6 7.0 %copy-start = (bf16[1,2,128,2048]{3,2,1,0:T(8,128)(2,1)S(1)}, bf16[1,2,128,2048]{3,2,1,0:T(8,128)(2,1)}, u32[]{:S(2)}) copy-start(bf16[1,2,128,2048]{3,2,1,0:T(8,128)(2,1)} %param.7) | copy-start | bytes 3145732
  0.6 7.0 %copy-start.10 = (f32[1,2048]{1,0:T(1,128)S(1)}, f32[1,2048]{1,0:T(1,128)}, u32[]{:S(2)}) copy-start(f32[1,2048]{1,0:T(1,128)} %param.11) | copy-start | bytes 24580
  0.7 7.0 %copy-start.11 = (f32[1,2048]{1,0:T(1,128)S(1)}, f32[1,2048]{1,0:T(1,128)}, u32[]{:S(2)}) copy-start(f32[1,2048]{1,0:T(1,128)} %param.10) | copy-start | bytes 24580
  5.2 9.0 %copy-start.1 = (bf16[128,2048]{1,0:T(8,128)(2,1)}, bf16[128,2048]{1,0:T(8,128)(2,1)S(1)}, u32[]{:S(2)}) copy-start(bf16[128,2048]{1,0:T(8,128)(2,1)S(1)} %get-tuple-element.9) | copy-start | bytes 1572868
  5.2 13.7 %collective-permute-start = (bf16[128,2048]{1,0:T(8,128)(2,1)S(1)}, bf16[128,2048]{1,0:T(8,128)(2,1)S(1)}, u32[]{:S(2)}, u32[]{:S(2)}) collective-permute-start(bf16[128,2048]{1,0:T(8,128)(2,1)S(1)} %get-tuple-element.9), channel_id=1, source_target_pairs={{0,4},{4,0},{1,5},{5,1},{2,6},{6,2},{3,7},{7,3},{8,12},{12,8},{9,1... | collective-permute-start | bytes 1572872 | tf_op jit(solution)/shard_map/ppermute | solution.py:18
  41.2 12.5 %collective-permute-start.1 = (bf16[128,2048]{1,0:T(8,128)(2,1)}, bf16[128,2048]{1,0:T(8,128)(2,1)}, u32[]{:S(2)}, u32[]{:S(2)}) collective-permute-start(bf16[128,2048]{1,0:T(8,128)(2,1)} %fusion.32), channel_id=1, source_target_pairs={{0,4},{4,0},{1,5},{5,1},{2,6},{6,2},{3,7},{7,3},{8,12},{12,8},{9,1... | collective-permute-start | bytes 1572872 | tf_op jit(solution)/shard_map/ppermute | solution.py:18
  46.3 7.5 %copy-start.2 = (bf16[128,2048]{1,0:T(8,128)(2,1)S(1)}, bf16[128,2048]{1,0:T(8,128)(2,1)}, u32[]{:S(2)}) copy-start(bf16[128,2048]{1,0:T(8,128)(2,1)} %copy-done.1) | copy-start | bytes 1572868
  56.9 13.2 %copy-start.5 = (bf16[128,2048]{1,0:T(8,128)(2,1)}, bf16[128,2048]{1,0:T(8,128)(2,1)S(1)}, u32[]{:S(2)}) copy-start(bf16[128,2048]{1,0:T(8,128)(2,1)S(1)} %fusion.72) | copy-start | bytes 1572868
  56.9 11.2 %collective-permute-start.2 = (bf16[128,2048]{1,0:T(8,128)(2,1)S(1)}, bf16[128,2048]{1,0:T(8,128)(2,1)S(1)}, u32[]{:S(2)}, u32[]{:S(2)}) collective-permute-start(bf16[128,2048]{1,0:T(8,128)(2,1)S(1)} %fusion.72), channel_id=1, source_target_pairs={{0,8},{8,16},{16,24},{1,9},{9,17},{17,25},{2,10},{10,18},{18,26},{... | collective-permute-start | bytes 1572872 | tf_op jit(solution)/shard_map/ppermute | solution.py:13
  70.1 10.0 %collective-permute-start.3 = (bf16[128,2048]{1,0:T(8,128)(2,1)S(1)}, bf16[128,2048]{1,0:T(8,128)(2,1)S(1)}, u32[]{:S(2)}, u32[]{:S(2)}) collective-permute-start(bf16[128,2048]{1,0:T(8,128)(2,1)S(1)} %get-tuple-element.7), channel_id=1, source_target_pairs={{0,4},{4,0},{1,5},{5,1},{2,6},{6,2},{3,7},{7,3},{8,12},{12,8},{9,1... | collective-permute-start | bytes 1572872 | tf_op jit(solution)/shard_map/ppermute | solution.py:18
  78.9 1.7 %copy-start.3 = (bf16[128,3072]{1,0:T(8,128)(2,1)}, bf16[128,3072]{1,0:T(8,128)(2,1)S(1)}, u32[]{:S(2)}) copy-start(bf16[128,3072]{1,0:T(8,128)(2,1)S(1)} %fusion.26) | copy-start | bytes 2359300
  80.6 6.6 %copy-start.4 = (bf16[128,3072]{1,0:T(8,128)(2,1)S(1)}, bf16[128,3072]{1,0:T(8,128)(2,1)}, u32[]{:S(2)}) copy-start(bf16[128,3072]{1,0:T(8,128)(2,1)} %copy-done.3) | copy-start | bytes 2359300
  89.6 2.7 %copy-start.8 = (bf16[128,3072]{0,1:T(8,128)(2,1)S(1)}, bf16[128,3072]{0,1:T(8,128)(2,1)}, u32[]{:S(2)}) copy-start(bf16[128,3072]{0,1:T(8,128)(2,1)} %copy.27) | copy-start | bytes 2359300
  100.0 4.5 %copy-start.7 = (bf16[128,3072]{0,1:T(8,128)(2,1)S(1)}, bf16[128,3072]{0,1:T(8,128)(2,1)}, u32[]{:S(2)}) copy-start(bf16[128,3072]{0,1:T(8,128)(2,1)} %copy.30) | copy-start | bytes 2359300
  103.9 10.3 %collective-permute-start.4 = (bf16[128,2048]{1,0:T(8,128)(2,1)}, bf16[128,2048]{1,0:T(8,128)(2,1)S(1)}, u32[]{:S(2)}, u32[]{:S(2)}) collective-permute-start(bf16[128,2048]{1,0:T(8,128)(2,1)} %fusion.41), channel_id=1, source_target_pairs={{0,4},{4,0},{1,5},{5,1},{2,6},{6,2},{3,7},{7,3},{8,12},{12,8},{9,1... | collective-permute-start | bytes 1572872 | tf_op jit(solution)/shard_map/ppermute | solution.py:18
  114.2 7.5 %copy-start.6 = (bf16[128,2048]{1,0:T(8,128)(2,1)S(1)}, bf16[128,2048]{1,0:T(8,128)(2,1)}, u32[]{:S(2)}) copy-start(bf16[128,2048]{1,0:T(8,128)(2,1)} %copy-done.5) | copy-start | bytes 1572868
  117.2 10.0 %copy-start.9 = (bf16[2,128,2048]{2,1,0:T(8,128)(2,1)S(1)}, bf16[2,128,2048]{2,1,0:T(8,128)(2,1)}, u32[]{:S(2)}) copy-start(bf16[2,128,2048]{2,1,0:T(8,128)(2,1)} %param.8) | copy-start | bytes 3145732
  117.2 10.0 %collective-permute-start.5 = (bf16[128,2048]{1,0:T(8,128)(2,1)S(1)}, bf16[128,2048]{1,0:T(8,128)(2,1)S(1)}, u32[]{:S(2)}, u32[]{:S(2)}) collective-permute-start(bf16[128,2048]{1,0:T(8,128)(2,1)S(1)} %fusion.75), channel_id=1, source_target_pairs={{0,8},{8,16},{16,24},{1,9},{9,17},{17,25},{2,10},{10,18},{18,26},{... | collective-permute-start | bytes 1572872 | tf_op jit(solution)/shard_map/ppermute | solution.py:13

commit v2 on v1

v2 whole, which is shorter than its diff:
```python
import functools

import jax
import jax.numpy as jnp
from jax import lax
from jax.experimental import pallas as pl
from jax.experimental.pallas import tpu as pltpu
from jax.sharding import PartitionSpec as P

HD = 128
PARTS = 2
MIB = 1 << 20
F32 = jnp.float32
BF16 = jnp.bfloat16

VMEM = pl.BlockSpec(memory_space=pltpu.VMEM)
SMEM = pl.BlockSpec(memory_space=pltpu.SMEM)
ANY = pl.BlockSpec(memory_space=pl.ANY)


def inner(shape, dtype=BF16):
    return pltpu.VMEM(tuple(shape), dtype)


def held_inside(block):
    return pltpu.with_memory_space_constraint(block, pltpu.VMEM)


def call(kernel, name, outs, out_specs, in_specs, args, flops=0, scratch=(), aliases=None, limit=16):
    return pl.pallas_call(
        kernel,
        name=name,
        out_shape=outs,
        out_specs=out_specs,
        in_specs=in_specs,
        scratch_shapes=list(scratch),
        input_output_aliases=aliases or {},
        compiler_params=pltpu.CompilerParams(vmem_limit_bytes=limit * MIB),
        cost_estimate=pl.CostEstimate(flops=max(flops, 1 << 20), bytes_accessed=1 << 16, transcendentals=0),
    )(*args)


def from_behind(block, axis):
    size = lax.axis_size(axis)
    return lax.ppermute(block, axis, [(i, i + 1) for i in range(size - 1)])


def rotate(block, axis, shift):
    size = lax.axis_size(axis)
    return lax.ppermute(block, axis, [(i, (i + shift) % size) for i in range(size)])


def pick_kernel(order, acts, current, sem):
    copy = pltpu.make_async_copy(acts.at[0, order[0, 0]], current, sem)
    copy.start()
    copy.wait()


def weights_kernel(w_in, w_out, in_inside, out_inside, sems):
    copies = []
    pieces = 4
    step = w_in.shape[1] // pieces
    for i in range(pieces):
        rows = pl.ds(i * step, step)
        copies.append(pltpu.make_async_copy(w_in.at[0, rows], in_inside.at[rows], sems.at[i]))
    copies.append(pltpu.make_async_copy(w_out.at[0], out_inside, sems.at[pieces]))
    for copy in copies:
        copy.start()
    for copy in copies:
        copy.wait()


def other_kernel(order, acts, fresh, other, sems):
    first = lax.axis_index("section") == 0
    repeated = order[0, 0] == order[0, 1]
    copy = pltpu.make_async_copy(acts.at[0, order[0, 1]], other, sems.at[0])
    copy.start()
    copy.wait()

    @pl.when(jnp.logical_and(first, repeated))
    def _():
        again = pltpu.make_async_copy(fresh.at[0], other, sems.at[1])
        again.start()
        again.wait()


def normed(rows, gain, bias):
    values = rows.astype(F32)
    centred = values - jnp.mean(values, axis=-1, keepdims=True)
    spread = jnp.mean(centred * centred, axis=-1, keepdims=True)
    return (centred * lax.rsqrt(spread + 1e-06) * gain + bias).astype(BF16)


def project(rows, weights, target, width=1024):
    for start in range(0, weights.shape[1], width):
        columns = slice(start, min(start + width, weights.shape[1]))
        target[:, columns] = jnp.dot(rows, weights[:, columns], preferred_element_type=F32).astype(BF16)


def attend(q, blocks, rows, mixed):
    heads = q.shape[1] // (3 * HD)
    for head in range(heads):
        at = [slice((head * 3 + j) * HD, (head * 3 + j + 1) * HD) for j in range(3)]
        query = q[rows, at[0]]
        keys = jnp.concatenate([b[:, at[1]] for b in blocks], axis=0)
        values = jnp.concatenate([b[:, at[2]] for b in blocks], axis=0)
        scores = lax.dot_general(query, keys, (((1,), (1,)), ((), ())), preferred_element_type=F32)
        scores = scores * (1.0 / HD**0.5)
        powers = jnp.exp(scores - jnp.max(scores, axis=-1, keepdims=True))
        probs = (powers / jnp.sum(powers, axis=-1, keepdims=True)).astype(BF16)
        out = jnp.dot(probs, values, preferred_element_type=F32)
        mixed[rows, head * HD : (head + 1) * HD] = out.astype(BF16)


def own_qkv_kernel(parts, *refs):
    chunks, (gain, bias, weights, qkv, hidden) = refs[:parts], refs[parts:]
    at = 0
    for chunk in chunks:
        rows = chunk.shape[0]
        hidden[at : at + rows] = normed(chunk[...], gain[...], bias[...])
        at += rows
    project(hidden[...], weights, qkv)


def others_kernel(parts, pieces, *refs):
    chunks = refs[:parts]
    gain, bias, w_in, w_out, mine = refs[parts : parts + 5]
    qkv = refs[parts + 5]
    outs = refs[parts + 6 : parts + 6 + pieces]
    hidden, mixed = refs[parts + 6 + pieces :]
    at = 0
    for chunk in chunks:
        rows = chunk.shape[0]
        hidden[at : at + rows] = normed(chunk[...], gain[...], bias[...])
        at += rows
    project(hidden[...], w_in, qkv)
    at = 0
    for out in outs:
        rows = slice(at, at + out.shape[0])
        attend(qkv, (mine, qkv), rows, mixed)
        project(mixed[rows], w_out, out)
        at += out.shape[0]


def own_kernel(mine, theirs, w_out, out, mixed):
    attend(mine, (mine, theirs), slice(0, mine.shape[0]), mixed)
    project(mixed[...], w_out, out)


def combine_kernel(start, *refs):
    current, own, got, result = refs[0], refs[1], refs[2:-1], refs[-1]
    rows = slice(start, start + result.shape[0])
    total = own[rows].astype(F32)
    for piece in got:
        total = total + piece[...].astype(F32)
    result[...] = (current[...].astype(F32) + total).astype(BF16)


def next_kernel(start, order, arriving, other, following):
    first = lax.axis_index("section") == 0
    take = jnp.logical_and(order[0, 0] == order[0, 1], jnp.logical_not(first))
    rows = slice(start, start + following.shape[0])
    following[...] = jnp.where(take, arriving[...], other[rows])


def held_kernel(parts, order, acts, fresh, *refs):
    arrived, held = refs[:parts], refs[parts]
    first = lax.axis_index("section") == 0
    for slot in range(acts.shape[1]):
        old, new = order[0, 0] == slot, order[0, 1] == slot
        at = 0
        for chunk in arrived:
            rows = slice(at, at + chunk.shape[0])
            value = jnp.where(first, fresh[0, rows], chunk[...])
            value = jnp.where(old, value, acts[0, slot, rows])
            held[0, slot, rows] = jnp.where(new, fresh[1, rows], value)
            at += chunk.shape[0]


def put_kernel(tick, parts, *refs):
    chunks, out, sems = refs[:parts], refs[-2], refs[-1]
    copies = []
    at = 0
    for i, chunk in enumerate(chunks):
        rows = pl.ds(at, chunk.shape[0])
        copies.append(pltpu.make_async_copy(chunk, out.at[tick, 0, rows], sems.at[i]))
        at += chunk.shape[0]
    for copy in copies:
        copy.start()
    for copy in copies:
        copy.wait()


def last_kernel(parts, order, *refs):
    chunks, out, sems = refs[:parts], refs[-2], refs[-1]
    first = lax.axis_index("section") == 0

    @pl.when(jnp.logical_not(first))
    def _():
        copies = []
        at = 0
        for i, chunk in enumerate(chunks):
            rows = pl.ds(at, chunk.shape[0])
            target = out.at[0, order[0, 1], rows]
            copies.append(pltpu.make_async_copy(chunk, target, sems.at[i]))
            at += chunk.shape[0]
        for copy in copies:
            copy.start()
        for copy in copies:
            copy.wait()


def layer(chunks, gain, bias, w_in, w_out):
    size = lax.axis_size("tensor")
    parts = len(chunks)
    rows = sum(c.shape[0] for c in chunks)
    wide, deep = w_in.shape[1], w_out.shape[0]
    width = w_in.shape[0]
    got = [held_inside(rotate(c, "tensor", j)) for j in range(1, size) for c in chunks]
    mine = call(
        functools.partial(own_qkv_kernel, parts),
        "own_qkv",
        inner((rows, wide)),
        VMEM,
        [VMEM] * (parts + 3),
        [*chunks, gain, bias, w_in],
        flops=2 * rows * width * wide,
        scratch=[inner((rows, width))],
    )
    far = (size - 1) * rows
    piece = rows // PARTS
    count = (size - 1) * PARTS
    theirs, *sends = call(
        functools.partial(others_kernel, len(got), count),
        "others",
        [inner((far, wide))] + [inner((piece, width))] * count,
        [VMEM] * (count + 1),
        [VMEM] * (len(got) + 5),
        [*got, gain, bias, w_in, w_out, mine],
        flops=2 * far * width * wide,
        scratch=[inner((far, width)), inner((far, deep))],
    )
    returned = [
        [held_inside(rotate(sends[(j - 1) * PARTS + i], "tensor", -j)) for j in range(1, size)]
        for i in range(PARTS)
    ]
    own = call(
        own_kernel,
        "own",
        inner((rows, width)),
        VMEM,
        [VMEM] * 3,
        [mine, theirs, w_out],
        flops=2 * rows * width * deep,
        scratch=[inner((rows, deep))],
    )
    return own, returned


def body(acts, fresh, order, ln_gain, ln_bias, wqkv, wo):
    rows, width = acts.shape[2:]
    piece = rows // PARTS
    ticks = fresh.shape[0]
    dma = pltpu.SemaphoreType.DMA
    current = call(pick_kernel, "pick", inner((rows, width)), VMEM, [SMEM, ANY], [order, acts], scratch=[dma])
    w_in, w_out = call(
        weights_kernel,
        "weights",
        [inner(wqkv.shape[1:]), inner(wo.shape[1:])],
        [VMEM, VMEM],
        [ANY, ANY],
        [wqkv, wo],
        scratch=[dma((5,))],
        limit=24,
        flops=1 << 30,
    )
    other = call(
        other_kernel,
        "other",
        inner((rows, width)),
        VMEM,
        [SMEM, ANY, ANY],
        [order, acts, fresh],
        scratch=[dma((2,))],
    )
    chunks = [current]
    section_out = held = None
    for tick in range(ticks):
        own, returned = layer(chunks, ln_gain, ln_bias, w_in, w_out)
        results, arrived = [], []
        for i in range(PARTS):
            if len(chunks) == 1:
                source, spec = chunks[0], None
            else:
                source = chunks[i]
            whole = len(chunks) == 1

            def combine(*refs, i=i, whole=whole):
                start = i * piece
                here = refs[0].at[pl.ds(start, piece)] if whole else refs[0]
                combine_kernel(start, here, *refs[1:])

            result = call(
                combine,
                "combine",
                inner((piece, width)),
                VMEM,
                [VMEM] * (2 + len(returned[i])),
                [source, own, *returned[i]],
            )
            results.append(result)
            arrived.append(held_inside(from_behind(result, "section")))
        if tick == 0:
            section_out = call(
                functools.partial(put_kernel, tick, PARTS),
                "put",
                jax.ShapeDtypeStruct((ticks, 1, rows, width), BF16),
                ANY,
                [VMEM] * PARTS,
                results,
                scratch=[dma((PARTS,))],
            )
            chunks = [
                call(
                    functools.partial(next_kernel, i * piece),
                    "next",
                    inner((piece, width)),
                    VMEM,
                    [SMEM, VMEM, VMEM],
                    [order, arrived[i], other],
                )
                for i in range(PARTS)
            ]
            held = call(
                functools.partial(held_kernel, PARTS),
                "held",
                jax.ShapeDtypeStruct(acts.shape, BF16),
                VMEM,
                [SMEM, VMEM, VMEM] + [VMEM] * PARTS,
                [order, acts, fresh, *arrived],
            )
        else:
            section_out = call(
                functools.partial(put_kernel, tick, PARTS),
                "put",
                jax.ShapeDtypeStruct((ticks, 1, rows, width), BF16),
                ANY,
                [VMEM] * PARTS + [ANY],
                [*results, section_out],
                scratch=[dma((PARTS,))],
                aliases={PARTS: 0},
            )
            held = call(
                functools.partial(last_kernel, PARTS),
                "last",
                jax.ShapeDtypeStruct(acts.shape, BF16),
                ANY,
                [SMEM] + [VMEM] * PARTS + [ANY],
                [order, *arrived, held],
                scratch=[dma((PARTS,))],
                aliases={PARTS + 1: 0},
            )
    return section_out, held


def solution(mesh):
    return jax.shard_map(
        body,
        mesh=mesh,
        in_specs=(
            P("section", "dp", "tensor", None),
            P("dp", "tensor", None),
            P("section", None),
            P("section", None),
            P("section", None),
            P("section", None, "tensor"),
            P("section", "tensor", None),
        ),
        out_specs=(P("dp", "section", "tensor", None), P("section", "dp", "tensor", None)),
        check_vma=False,
    )
```

time: 130 us -> 85.9 us (0.66)
  matrix products: 70.8 us -> 0 us
  Pallas kernels: 0 us -> 36.3 us
  other arithmetic: 10.8 us -> 0 us
  starting transfers between devices: 14.4 us -> 22.2 us
  local copies, waits for them, and re-layouts: 11 us -> 4.08 us
  waiting for transfers between devices: 16.8 us -> 22 us
  between operations: 4.62 us -> 1.02 us
    dot_general x16 -> x0, matrix products: 64.3 us -> none  [the longest x4 26.8 us: layer(): jnp.dot(normed(b, gain, bias), w_in, preferred_element_type=jnp.float32)]
    pallas_call x0 -> x19, Pallas kernels: none -> 36.3 us  [call(): pl.pallas_call(kernel, name=name, out_shape=outs, out_specs=out_specs, in...]
    ppermute x4 -> x7, waiting for transfers between devices: 9.39 us -> 21.4 us  [rotate(): lax.ppermute(block, axis, [(i, (i + shift) % size) for i in range(size)])]
    ppermute x2 -> x4, waiting for transfers between devices: 7.43 us -> 0.6 us  [from_behind(): return lax.ppermute(block, axis, [(i, i + 1) for i in range(size - 1)])]
    sub x4 -> x0, matrix products: 6.58 us -> none  [attend(): probs = jax.nn.softmax(scores, axis=-1).astype(jnp.bfloat16)]
    ppermute x2 -> x4, starting transfers between devices: 9.15 us -> 14.5 us  [from_behind(): return lax.ppermute(block, axis, [(i, i + 1) for i in range(size - 1)])]
    convert_element_type x4 -> x0, local copies, waits for them, and re-layouts: 4.65 us -> none  [layer(): jnp.dot(normed(b, gain, bias), w_in, preferred_element_type=jnp.float32)]
    concatenate x2 -> x0, local copies, waits for them, and re-layouts: 4.37 us -> none  [layer(): keys = jnp.concatenate(parts, axis=0)]
  transfers between devices with their start and end apart: 6 -> 11, of which waited for: 5 -> 7; matrix products, arithmetic and copies ran while one was open for 27% -> 0% of each run, Pallas kernels for 0% -> 21%
where the time goes in v2:
time: 85.9 us; the launch traced here: 85.6 us
  Pallas kernels  36.3 us (42%)
  starting transfers between devices  22.2 us (26%)
  waiting for transfers between devices  22 us (26%)
  local copies, waits for them, and re-layouts  4.08 us (5%)
  between operations  1.02 us (1%)
    pallas_call x19, Pallas kernels, call(): pl.pallas_call(kernel, name=name, out_shape=outs, out_specs=out_specs, in...  36.3 us
    ppermute x7, waiting for transfers between devices, rotate(): lax.ppermute(block, axis, [(i, (i + shift) % size) for i in range(size)])  21.4 us
    ppermute x4, starting transfers between devices, from_behind(): return lax.ppermute(block, axis, [(i, i + 1) for i in range(size - 1)])  14.5 us
    ppermute x7, starting transfers between devices, rotate(): lax.ppermute(block, axis, [(i, (i + shift) % size) for i in range(size)])  7.72 us
    unnamed x16, local copies, waits for them, and re-layouts  4.08 us
  transfers between devices with their start and end apart: 11, of which 7 were waited for; matrix products, arithmetic and copies ran while one was open for 0% of the time, Pallas kernels for 21%

profile of v2, /device:TPU:1, one launch (start us, length us, event | category | flops | bytes accessed | tf_op | source)
XLA Modules:
  0.0 85.6 jit_solution(9728322231596007827)
XLA Ops:
  3.1 2.1 %collective-permute-start = (bf16[128,2048]{1,0:T(8,128)(2,1)S(1)}, bf16[128,2048]{1,0:T(8,128)(2,1)S(1)}, u32[]{:S(2)}, u32[]{:S(2)}) collective-permute-start(bf16[128,2048]{1,0:T(8,128)(2,1)S(1)} %pick.1.refs_0_), channel_id=1, source_target_pairs={{0,4},{4,0},{1,5},{5,1},{2,6},{6,2},{3,7},{7,3},{8,12},{12,8},{9,1... | collective-permute-start | bytes 1572872 | tf_op jit(solution)/shard_map/ppermute | solution.py:50
  5.2 2.2 %copy-done.3 = bf16[1,1024,2048]{2,1,0:T(8,128)(2,1)S(1)} copy-done((bf16[1,1024,2048]{2,1,0:T(8,128)(2,1)S(1)}, bf16[1,1024,2048]{2,1,0:T(8,128)(2,1)}, u32[]{:S(2)}) %copy-start.3) | copy-done | bytes 4194328
  7.4 4.7 %weights.1 = (bf16[2048,3072]{1,0:T(8,128)(2,1)S(1)}, bf16[1024,2048]{1,0:T(8,128)(2,1)S(1)}) custom-call(bf16[1,2048,3072]{2,1,0:T(8,128)(2,1)} %w_in.1, bf16[1,1024,2048]{2,1,0:T(8,128)(2,1)S(1)} %copy-done.3), custom_call_target="tpu_custom_call" | custom-call | flops 1073741824 | bytes 65536 | tf_op jit(solution)/shard_map/weights/pallas_call | solution.py:30
  12.1 2.1 %own_qkv.2.refs_5_.mine = bf16[128,3072]{1,0:T(8,128)(2,1)S(1)} custom-call(bf16[128,2048]{1,0:T(8,128)(2,1)S(1)} %pick.1.refs_0_, f32[1,2048]{1,0:T(1,128)S(1)} %copy-done.4, f32[1,2048]{1,0:T(1,128)S(1)} %copy-done.5, bf16[2048,3072]{1,0:T(8,128)(2,1)S(1)} %get-tuple-element.10.refs_3_.refs_4_), custom_call_target="tpu_custom_call" | custom-call | flops 1610612736 | bytes 65536 | tf_op jit(solution)/shard_map/own_qkv/pallas_call | solution.py:30
  14.2 2.6 %collective-permute-done.refs_0_ = bf16[128,2048]{1,0:T(8,128)(2,1)S(1)} collective-permute-done((bf16[128,2048]{1,0:T(8,128)(2,1)S(1)}, bf16[128,2048]{1,0:T(8,128)(2,1)S(1)}, u32[]{:S(2)}, u32[]{:S(2)}) %collective-permute-start) | collective-permute-done | bytes 524320 | tf_op jit(solution)/shard_map/ppermute | solution.py:50
  16.8 8.1 %others.2 = (bf16[128,3072]{1,0:T(8,128)(2,1)S(1)}, bf16[64,2048]{1,0:T(8,128)(2,1)S(1)}, bf16[64,2048]{1,0:T(8,128)(2,1)S(1)}) custom-call(bf16[128,2048]{1,0:T(8,128)(2,1)S(1)} %collective-permute-done.refs_0_, f32[1,2048]{1,0:T(1,128)S(1)} %copy-done.4, f32[1,2048]{1,0:T(1,128)S(1)} %copy-done.5, ...), custom_call_target="tpu_custom_call" | custom-call | flops 1610612736 | bytes 65536 | tf_op jit(solution)/shard_map/others/pallas_call | solution.py:30
  26.5 1.7 %own.2.refs_1_ = bf16[128,2048]{1,0:T(8,128)(2,1)S(1)} custom-call(bf16[128,3072]{1,0:T(8,128)(2,1)S(1)} %own_qkv.2.refs_5_.mine, bf16[128,3072]{1,0:T(8,128)(2,1)S(1)} %get-tuple-element.12.theirs, bf16[1024,2048]{1,0:T(8,128)(2,1)S(1)} %get-tuple-element.11.refs_4_.w_out.refs_5_), custom_call_target="tpu_custom_call" | custom-call | flops 536870912 | bytes 65536 | tf_op jit(solution)/shard_map/own/pallas_call | solution.py:30
  28.2 3.4 %collective-permute-done.1.refs_2_ = bf16[64,2048]{1,0:T(8,128)(2,1)S(1)} collective-permute-done((bf16[64,2048]{1,0:T(8,128)(2,1)S(1)}, bf16[64,2048]{1,0:T(8,128)(2,1)S(1)}, u32[]{:S(2)}, u32[]{:S(2)}) %collective-permute-start.1) | collective-permute-done | bytes 262176 | tf_op jit(solution)/shard_map/ppermute | solution.py:50
  31.7 7.1 %collective-permute-start.2 = (bf16[64,2048]{1,0:T(8,128)(2,1)S(1)}, bf16[64,2048]{1,0:T(8,128)(2,1)S(1)}, u32[]{:S(2)}, u32[]{:S(2)}) collective-permute-start(bf16[64,2048]{1,0:T(8,128)(2,1)S(1)} %combine.4.refs_0_), channel_id=1, source_target_pairs={{0,8},{8,16},{16,24},{1,9},{9,17},{17,25},{2,10},{10,18},{18,26},{... | collective-permute-start | bytes 786440 | tf_op jit(solution)/shard_map/ppermute | solution.py:45
  39.0 3.5 %collective-permute-start.4 = (bf16[64,2048]{1,0:T(8,128)(2,1)S(1)}, bf16[64,2048]{1,0:T(8,128)(2,1)S(1)}, u32[]{:S(2)}, u32[]{:S(2)}) collective-permute-start(bf16[64,2048]{1,0:T(8,128)(2,1)S(1)} %combine.5.refs_1_), channel_id=1, source_target_pairs={{0,8},{8,16},{16,24},{1,9},{9,17},{17,25},{2,10},{10,18},{18,26},{... | collective-permute-start | bytes 786440 | tf_op jit(solution)/shard_map/ppermute | solution.py:45
  43.9 1.3 %collective-permute-start.5 = (bf16[64,2048]{1,0:T(8,128)(2,1)S(1)}, bf16[64,2048]{1,0:T(8,128)(2,1)S(1)}, u32[]{:S(2)}, u32[]{:S(2)}) collective-permute-start(bf16[64,2048]{1,0:T(8,128)(2,1)S(1)} %next.2.refs_0_), channel_id=1, source_target_pairs={{0,4},{4,0},{1,5},{5,1},{2,6},{6,2},{3,7},{7,3},{8,12},{12,8},{9,1... | collective-permute-start | bytes 786440 | tf_op jit(solution)/shard_map/ppermute | solution.py:50
  46.3 1.3 %collective-permute-start.6 = (bf16[64,2048]{1,0:T(8,128)(2,1)S(1)}, bf16[64,2048]{1,0:T(8,128)(2,1)S(1)}, u32[]{:S(2)}, u32[]{:S(2)}) collective-permute-start(bf16[64,2048]{1,0:T(8,128)(2,1)S(1)} %next.3.refs_1_.refs_0_), channel_id=1, source_target_pairs={{0,4},{4,0},{1,5},{5,1},{2,6},{6,2},{3,7},{7,3},{8,12},{12,8},{9,1... | collective-permute-start | bytes 786440 | tf_op jit(solution)/shard_map/ppermute | solution.py:50
  47.6 2.1 %own_qkv.3.refs_6_.mine = bf16[128,3072]{1,0:T(8,128)(2,1)S(1)} custom-call(bf16[64,2048]{1,0:T(8,128)(2,1)S(1)} %next.2.refs_0_, bf16[64,2048]{1,0:T(8,128)(2,1)S(1)} %next.3.refs_1_.refs_0_, f32[1,2048]{1,0:T(1,128)S(1)} %copy-done.4, f32[1,2048]{1,0:T(1,128)S(1)} %copy-done.5, bf16[2048,3072]{1,0:T(8,128)(2,1)S(1)} %get-tuple-element.10.refs_3_.refs_4_), custom_call_target="tpu_custom_call" | custom-call | flops 1610612736 | bytes 65536 | tf_op jit(solution)/shard_map/own_qkv/pallas_call | solution.py:30
  49.7 2.6 %collective-permute-done.5.refs_0_ = bf16[64,2048]{1,0:T(8,128)(2,1)S(1)} collective-permute-done((bf16[64,2048]{1,0:T(8,128)(2,1)S(1)}, bf16[64,2048]{1,0:T(8,128)(2,1)S(1)}, u32[]{:S(2)}, u32[]{:S(2)}) %collective-permute-start.5) | collective-permute-done | bytes 262176 | tf_op jit(solution)/shard_map/ppermute | solution.py:50
  52.3 4.7 %collective-permute-done.6.refs_1_ = bf16[64,2048]{1,0:T(8,128)(2,1)S(1)} collective-permute-done((bf16[64,2048]{1,0:T(8,128)(2,1)S(1)}, bf16[64,2048]{1,0:T(8,128)(2,1)S(1)}, u32[]{:S(2)}, u32[]{:S(2)}) %collective-permute-start.6) | collective-permute-done | bytes 262176 | tf_op jit(solution)/shard_map/ppermute | solution.py:50
  57.0 8.1 %others.3 = (bf16[128,3072]{1,0:T(8,128)(2,1)S(1)}, bf16[64,2048]{1,0:T(8,128)(2,1)S(1)}, bf16[64,2048]{1,0:T(8,128)(2,1)S(1)}) custom-call(bf16[64,2048]{1,0:T(8,128)(2,1)S(1)} %collective-permute-done.5.refs_0_, bf16[64,2048]{1,0:T(8,128)(2,1)S(1)} %collective-permute-done.6.refs_1_, f32[1,2048]{1,0:T(1,128)S(1)} %copy-done.4, f32[1,2048]{1,0:T(1,128)S(1)} %copy-done.5, ...), custom_call_target="tpu_custom_call" | custom-call | flops 1610612736 | bytes 65536 | tf_op jit(solution)/shard_map/others/pallas_call | solution.py:30
  65.1 1.3 %collective-permute-start.7 = (bf16[64,2048]{1,0:T(8,128)(2,1)S(1)}, bf16[64,2048]{1,0:T(8,128)(2,1)S(1)}, u32[]{:S(2)}, u32[]{:S(2)}) collective-permute-start(bf16[64,2048]{1,0:T(8,128)(2,1)S(1)} %get-tuple-element.16), channel_id=1, source_target_pairs={{0,4},{4,0},{1,5},{5,1},{2,6},{6,2},{3,7},{7,3},{8,12},{12,8},{9,1... | collective-permute-start | bytes 786440 | tf_op jit(solution)/shard_map/ppermute | solution.py:50
  66.6 1.7 %own.3.refs_1_ = bf16[128,2048]{1,0:T(8,128)(2,1)S(1)} custom-call(bf16[128,3072]{1,0:T(8,128)(2,1)S(1)} %own_qkv.3.refs_6_.mine, bf16[128,3072]{1,0:T(8,128)(2,1)S(1)} %get-tuple-element.15.theirs, bf16[1024,2048]{1,0:T(8,128)(2,1)S(1)} %get-tuple-element.11.refs_4_.w_out.refs_5_), custom_call_target="tpu_custom_call" | custom-call | flops 536870912 | bytes 65536 | tf_op jit(solution)/shard_map/own/pallas_call | solution.py:30
  68.4 4.6 %collective-permute-done.7.refs_2_ = bf16[64,2048]{1,0:T(8,128)(2,1)S(1)} collective-permute-done((bf16[64,2048]{1,0:T(8,128)(2,1)S(1)}, bf16[64,2048]{1,0:T(8,128)(2,1)S(1)}, u32[]{:S(2)}, u32[]{:S(2)}) %collective-permute-start.7) | collective-permute-done | bytes 262176 | tf_op jit(solution)/shard_map/ppermute | solution.py:50
  73.0 1.9 %collective-permute-start.9 = (bf16[64,2048]{1,0:T(8,128)(2,1)S(1)}, bf16[64,2048]{1,0:T(8,128)(2,1)S(1)}, u32[]{:S(2)}, u32[]{:S(2)}) collective-permute-start(bf16[64,2048]{1,0:T(8,128)(2,1)S(1)} %combine.6.refs_0_), channel_id=1, source_target_pairs={{0,8},{8,16},{16,24},{1,9},{9,17},{17,25},{2,10},{10,18},{18,26},{... | collective-permute-start | bytes 786440 | tf_op jit(solution)/shard_map/ppermute | solution.py:45
  75.0 3.6 %collective-permute-done.8.refs_2_ = bf16[64,2048]{1,0:T(8,128)(2,1)S(1)} collective-permute-done((bf16[64,2048]{1,0:T(8,128)(2,1)S(1)}, bf16[64,2048]{1,0:T(8,128)(2,1)S(1)}, u32[]{:S(2)}, u32[]{:S(2)}) %collective-permute-start.8) | collective-permute-done | bytes 262176 | tf_op jit(solution)/shard_map/ppermute | solution.py:50
  78.7 1.9 %collective-permute-start.10 = (bf16[64,2048]{1,0:T(8,128)(2,1)S(1)}, bf16[64,2048]{1,0:T(8,128)(2,1)S(1)}, u32[]{:S(2)}, u32[]{:S(2)}) collective-permute-start(bf16[64,2048]{1,0:T(8,128)(2,1)S(1)} %combine.7.refs_1_), channel_id=1, source_target_pairs={{0,8},{8,16},{16,24},{1,9},{9,17},{17,25},{2,10},{10,18},{18,26},{... | collective-permute-start | bytes 786440 | tf_op jit(solution)/shard_map/ppermute | solution.py:45
  81.4 1.8 %held.1.refs_2_ = bf16[1,2,128,2048]{3,2,1,0:T(8,128)(2,1)} custom-call(s32[1,2]{1,0:T(1,128)S(1)} %copy-done.7, bf16[1,2,128,2048]{3,2,1,0:T(8,128)(2,1)S(1)} %copy-done.1, bf16[2,128,2048]{2,1,0:T(8,128)(2,1)S(1)} %copy-done.2, bf16[64,2048]{1,0:T(8,128)(2,1)S(1)} %collective-permute-done.2.arriving.refs_0_, ...), custom_call_target="tpu_custom_call" | custom-call | flops 1048576 | bytes 65536 | tf_op jit(solution)/shard_map/held/pallas_call | solution.py:30
  84.1 1.4 %last.1 = bf16[1,2,128,2048]{3,2,1,0:T(8,128)(2,1)} custom-call(s32[1,2]{1,0:T(1,128)S(1)} %copy-done.7, bf16[64,2048]{1,0:T(8,128)(2,1)S(1)} %collective-permute-done.9.refs_0_, bf16[64,2048]{1,0:T(8,128)(2,1)S(1)} %collective-permute-done.10.refs_1_, bf16[1,2,128,2048]{3,2,1,0:T(8,128)(2,1)} %held.1.refs_2_), custom_call_target="tpu_custom_call", output_to_operand_aliasing={{}: (3, {})} | custom-call | flops 1048576 | bytes 65536 | tf_op jit(solution)/shard_map/last/pallas_call | solution.py:30
  (33 shorter events, 8.8 us)
Async XLA Ops:
  0.6 1.2 %copy-start = (bf16[1,2,128,2048]{3,2,1,0:T(8,128)(2,1)S(1)}, bf16[1,2,128,2048]{3,2,1,0:T(8,128)(2,1)}, u32[]{:S(2)}) copy-start(bf16[1,2,128,2048]{3,2,1,0:T(8,128)(2,1)} %acts.5) | copy-start | bytes 3145732
  1.9 0.7 copy-start.6
  2.5 9.6 %copy-start.4 = (f32[1,2048]{1,0:T(1,128)S(1)}, f32[1,2048]{1,0:T(1,128)}, u32[]{:S(2)}) copy-start(f32[1,2048]{1,0:T(1,128)} %refs_2_.7) | copy-start | bytes 24580
  2.5 9.6 %copy-start.5 = (f32[1,2048]{1,0:T(1,128)S(1)}, f32[1,2048]{1,0:T(1,128)}, u32[]{:S(2)}) copy-start(f32[1,2048]{1,0:T(1,128)} %refs_3_.3) | copy-start | bytes 24580
  3.1 13.7 %collective-permute-start = (bf16[128,2048]{1,0:T(8,128)(2,1)S(1)}, bf16[128,2048]{1,0:T(8,128)(2,1)S(1)}, u32[]{:S(2)}, u32[]{:S(2)}) collective-permute-start(bf16[128,2048]{1,0:T(8,128)(2,1)S(1)} %pick.1.refs_0_), channel_id=1, source_target_pairs={{0,4},{4,0},{1,5},{5,1},{2,6},{6,2},{3,7},{7,3},{8,12},{12,8},{9,1... | collective-permute-start | bytes 1572872 | tf_op jit(solution)/shard_map/ppermute | solution.py:50
  5.2 2.2 %copy-start.3 = (bf16[1,1024,2048]{2,1,0:T(8,128)(2,1)S(1)}, bf16[1,1024,2048]{2,1,0:T(8,128)(2,1)}, u32[]{:S(2)}) copy-start(bf16[1,1024,2048]{2,1,0:T(8,128)(2,1)} %w_out.1) | copy-start | bytes 12582916
  16.8 25.6 %copy-start.1 = (bf16[1,2,128,2048]{3,2,1,0:T(8,128)(2,1)S(1)}, bf16[1,2,128,2048]{3,2,1,0:T(8,128)(2,1)}, u32[]{:S(2)}) copy-start(bf16[1,2,128,2048]{3,2,1,0:T(8,128)(2,1)} %acts.5) | copy-start | bytes 3145732
  16.8 25.6 %copy-start.2 = (bf16[2,128,2048]{2,1,0:T(8,128)(2,1)S(1)}, bf16[2,128,2048]{2,1,0:T(8,128)(2,1)}, u32[]{:S(2)}) copy-start(bf16[2,128,2048]{2,1,0:T(8,128)(2,1)} %fresh.3) | copy-start | bytes 3145732
  16.8 25.6 %copy-start.7 = (s32[1,2]{1,0:T(1,128)S(1)}, s32[1,2]{1,0:T(1,128)}, u32[]{:S(2)}) copy-start(s32[1,2]{1,0:T(1,128)} %order.11) | copy-start | bytes 28
  25.0 6.7 %collective-permute-start.1 = (bf16[64,2048]{1,0:T(8,128)(2,1)S(1)}, bf16[64,2048]{1,0:T(8,128)(2,1)S(1)}, u32[]{:S(2)}, u32[]{:S(2)}) collective-permute-start(bf16[64,2048]{1,0:T(8,128)(2,1)S(1)} %get-tuple-element.13), channel_id=1, source_target_pairs={{0,4},{4,0},{1,5},{5,1},{2,6},{6,2},{3,7},{7,3},{8,12},{12,8},{9,1... | collective-permute-start | bytes 786440 | tf_op jit(solution)/shard_map/ppermute | solution.py:50
  26.2 12.6 %collective-permute-start.3 = (bf16[64,2048]{1,0:T(8,128)(2,1)S(1)}, bf16[64,2048]{1,0:T(8,128)(2,1)S(1)}, u32[]{:S(2)}, u32[]{:S(2)}) collective-permute-start(bf16[64,2048]{1,0:T(8,128)(2,1)S(1)} %get-tuple-element.14), channel_id=1, source_target_pairs={{0,4},{4,0},{1,5},{5,1},{2,6},{6,2},{3,7},{7,3},{8,12},{12,8},{9,1... | collective-permute-start | bytes 786440 | tf_op jit(solution)/shard_map/ppermute | solution.py:50
  31.7 11.6 %collective-permute-start.2 = (bf16[64,2048]{1,0:T(8,128)(2,1)S(1)}, bf16[64,2048]{1,0:T(8,128)(2,1)S(1)}, u32[]{:S(2)}, u32[]{:S(2)}) collective-permute-start(bf16[64,2048]{1,0:T(8,128)(2,1)S(1)} %combine.4.refs_0_), channel_id=1, source_target_pairs={{0,8},{8,16},{16,24},{1,9},{9,17},{17,25},{2,10},{10,18},{18,26},{... | collective-permute-start | bytes 786440 | tf_op jit(solution)/shard_map/ppermute | solution.py:45
  39.0 6.8 %collective-permute-start.4 = (bf16[64,2048]{1,0:T(8,128)(2,1)S(1)}, bf16[64,2048]{1,0:T(8,128)(2,1)S(1)}, u32[]{:S(2)}, u32[]{:S(2)}) collective-permute-start(bf16[64,2048]{1,0:T(8,128)(2,1)S(1)} %combine.5.refs_1_), channel_id=1, source_target_pairs={{0,8},{8,16},{16,24},{1,9},{9,17},{17,25},{2,10},{10,18},{18,26},{... | collective-permute-start | bytes 786440 | tf_op jit(solution)/shard_map/ppermute | solution.py:45
  43.9 8.4 %collective-permute-start.5 = (bf16[64,2048]{1,0:T(8,128)(2,1)S(1)}, bf16[64,2048]{1,0:T(8,128)(2,1)S(1)}, u32[]{:S(2)}, u32[]{:S(2)}) collective-permute-start(bf16[64,2048]{1,0:T(8,128)(2,1)S(1)} %next.2.refs_0_), channel_id=1, source_target_pairs={{0,4},{4,0},{1,5},{5,1},{2,6},{6,2},{3,7},{7,3},{8,12},{12,8},{9,1... | collective-permute-start | bytes 786440 | tf_op jit(solution)/shard_map/ppermute | solution.py:50
  46.3 10.6 %collective-permute-start.6 = (bf16[64,2048]{1,0:T(8,128)(2,1)S(1)}, bf16[64,2048]{1,0:T(8,128)(2,1)S(1)}, u32[]{:S(2)}, u32[]{:S(2)}) collective-permute-start(bf16[64,2048]{1,0:T(8,128)(2,1)S(1)} %next.3.refs_1_.refs_0_), channel_id=1, source_target_pairs={{0,4},{4,0},{1,5},{5,1},{2,6},{6,2},{3,7},{7,3},{8,12},{12,8},{9,1... | collective-permute-start | bytes 786440 | tf_op jit(solution)/shard_map/ppermute | solution.py:50
  65.1 7.9 %collective-permute-start.7 = (bf16[64,2048]{1,0:T(8,128)(2,1)S(1)}, bf16[64,2048]{1,0:T(8,128)(2,1)S(1)}, u32[]{:S(2)}, u32[]{:S(2)}) collective-permute-start(bf16[64,2048]{1,0:T(8,128)(2,1)S(1)} %get-tuple-element.16), channel_id=1, source_target_pairs={{0,4},{4,0},{1,5},{5,1},{2,6},{6,2},{3,7},{7,3},{8,12},{12,8},{9,1... | collective-permute-start | bytes 786440 | tf_op jit(solution)/shard_map/ppermute | solution.py:50
  66.4 12.2 %collective-permute-start.8 = (bf16[64,2048]{1,0:T(8,128)(2,1)S(1)}, bf16[64,2048]{1,0:T(8,128)(2,1)S(1)}, u32[]{:S(2)}, u32[]{:S(2)}) collective-permute-start(bf16[64,2048]{1,0:T(8,128)(2,1)S(1)} %get-tuple-element.17), channel_id=1, source_target_pairs={{0,4},{4,0},{1,5},{5,1},{2,6},{6,2},{3,7},{7,3},{8,12},{12,8},{9,1... | collective-permute-start | bytes 786440 | tf_op jit(solution)/shard_map/ppermute | solution.py:50
  73.0 11.0 %collective-permute-start.9 = (bf16[64,2048]{1,0:T(8,128)(2,1)S(1)}, bf16[64,2048]{1,0:T(8,128)(2,1)S(1)}, u32[]{:S(2)}, u32[]{:S(2)}) collective-permute-start(bf16[64,2048]{1,0:T(8,128)(2,1)S(1)} %combine.6.refs_0_), channel_id=1, source_target_pairs={{0,8},{8,16},{16,24},{1,9},{9,17},{17,25},{2,10},{10,18},{18,26},{... | collective-permute-start | bytes 786440 | tf_op jit(solution)/shard_map/ppermute | solution.py:45
  78.7 5.4 %collective-permute-start.10 = (bf16[64,2048]{1,0:T(8,128)(2,1)S(1)}, bf16[64,2048]{1,0:T(8,128)(2,1)S(1)}, u32[]{:S(2)}, u32[]{:S(2)}) collective-permute-start(bf16[64,2048]{1,0:T(8,128)(2,1)S(1)} %combine.7.refs_1_), channel_id=1, source_target_pairs={{0,8},{8,16},{16,24},{1,9},{9,17},{17,25},{2,10},{10,18},{18,26},{... | collective-permute-start | bytes 786440 | tf_op jit(solution)/shard_map/ppermute | solution.py:45

commit v3 on v2

--- a/solution.py
+++ b/solution.py
@@ -26,7 +26,19 @@
     return pltpu.with_memory_space_constraint(block, pltpu.VMEM)
 
 
-def call(kernel, name, outs, out_specs, in_specs, args, flops=0, scratch=(), aliases=None, limit=16):
+def outside(block):
+    return pltpu.with_memory_space_constraint(block, pltpu.HBM)
+
+
+def after(kernel, count):
+    return lambda *refs: kernel(*refs[count:])
+
+
+def call(kernel, name, outs, out_specs, in_specs, args, flops=0, scratch=(), aliases=None, limit=16, wait=()):
+    if wait:
+        kernel = after(kernel, len(wait))
+        in_specs, args = [ANY] * len(wait) + in_specs, [*wait, *args]
+        aliases = {k + len(wait): v for k, v in (aliases or {}).items()}
     return pl.pallas_call(
         kernel,
         name=name,
@@ -50,10 +62,14 @@
     return lax.ppermute(block, axis, [(i, (i + shift) % size) for i in range(size)])
 
 
-def pick_kernel(order, acts, current, sem):
-    copy = pltpu.make_async_copy(acts.at[0, order[0, 0]], current, sem)
-    copy.start()
-    copy.wait()
+def pick_kernel(order, acts, current, kept, slots, sems):
+    number = pltpu.make_async_copy(order, kept, sems.at[0])
+    blocks = pltpu.make_async_copy(acts.at[0], slots, sems.at[1])
+    number.start()
+    blocks.start()
+    number.wait()
+    blocks.wait()
+    current[...] = slots[kept[0, 0]]
 
 
 def weights_kernel(w_in, w_out, in_inside, out_inside, sems):
@@ -91,10 +107,14 @@
     return (centred * lax.rsqrt(spread + 1e-06) * gain + bias).astype(BF16)
 
 
-def project(rows, weights, target, width=1024):
+def project(rows, weights, *targets, width=1024):
     for start in range(0, weights.shape[1], width):
         columns = slice(start, min(start + width, weights.shape[1]))
-        target[:, columns] = jnp.dot(rows, weights[:, columns], preferred_element_type=F32).astype(BF16)
+        value = jnp.dot(rows, weights[:, columns], preferred_element_type=F32).astype(BF16)
+        at = 0
+        for target in targets:
+            target[:, columns] = value[at : at + target.shape[0]]
+            at += target.shape[0]
 
 
 def attend(q, blocks, rows, mixed):
@@ -134,12 +154,8 @@
         hidden[at : at + rows] = normed(chunk[...], gain[...], bias[...])
         at += rows
     project(hidden[...], w_in, qkv)
-    at = 0
-    for out in outs:
-        rows = slice(at, at + out.shape[0])
-        attend(qkv, (mine, qkv), rows, mixed)
-        project(mixed[rows], w_out, out)
-        at += out.shape[0]
+    attend(qkv, (mine, qkv), slice(0, at), mixed)
+    project(mixed[...], w_out, *outs)
 
 
 def own_kernel(mine, theirs, w_out, out, mixed):
@@ -210,7 +226,14 @@
             copy.wait()
 
 
-def layer(chunks, gain, bias, w_in, w_out):
+def cuts(rows):
+    units = rows // 16
+    parts = min(PARTS, units)
+    sizes = [(units // parts + (i < units % parts)) * 16 for i in range(parts)]
+    return [(sum(sizes[:i]), size) for i, size in enumerate(sizes)]
+
+
+def layer(chunks, gain, bias, w_in, w_out, early=(), late=None):
     size = lax.axis_size("tensor")
     parts = len(chunks)
     rows = sum(c.shape[0] for c in chunks)
@@ -228,21 +251,23 @@
         scratch=[inner((rows, width))],
     )
     far = (size - 1) * rows
-    piece = rows // PARTS
-    count = (size - 1) * PARTS
+    pieces = cuts(rows)
+    count = (size - 1) * len(pieces)
+    done = late(mine) if late else []
     theirs, *sends = call(
         functools.partial(others_kernel, len(got), count),
         "others",
-        [inner((far, wide))] + [inner((piece, width))] * count,
+        [inner((far, wide))] + [inner((n, width)) for _ in range(size - 1) for _, n in pieces],
         [VMEM] * (count + 1),
         [VMEM] * (len(got) + 5),
         [*got, gain, bias, w_in, w_out, mine],
         flops=2 * far * width * wide,
         scratch=[inner((far, width)), inner((far, deep))],
+        wait=[*early, *done],
     )
     returned = [
-        [held_inside(rotate(sends[(j - 1) * PARTS + i], "tensor", -j)) for j in range(1, size)]
-        for i in range(PARTS)
+        [held_inside(rotate(sends[(j - 1) * len(pieces) + i], "tensor", -j)) for j in range(1, size)]
+        for i in range(len(pieces))
     ]
     own = call(
         own_kernel,
@@ -254,7 +279,7 @@
         flops=2 * rows * width * deep,
         scratch=[inner((rows, deep))],
     )
-    return own, returned
+    return own, returned, done
 
 
 def body(acts, fresh, order, ln_gain, ln_bias, wqkv, wo):
@@ -262,7 +287,16 @@
     piece = rows // PARTS
     ticks = fresh.shape[0]
     dma = pltpu.SemaphoreType.DMA
-    current = call(pick_kernel, "pick", inner((rows, width)), VMEM, [SMEM, ANY], [order, acts], scratch=[dma])
+    acts, fresh, order, wqkv, wo = map(outside, (acts, fresh, order, wqkv, wo))
+    current, order = call(
+        pick_kernel,
+        "pick",
+        [inner((rows, width)), pltpu.SMEM(order.shape, order.dtype)],
+        [VMEM, SMEM],
+        [ANY, ANY],
+        [order, acts],
+        scratch=[inner(acts.shape[1:]), dma((2,))],
+    )
     w_in, w_out = call(
         weights_kernel,
         "weights",
@@ -284,81 +318,86 @@
         scratch=[dma((2,))],
     )
     chunks = [current]
-    section_out = held = None
+    pieces = cuts(rows)
+    parts = len(pieces)
+    section_out = held = late = None
+    early = [other]
     for tick in range(ticks):
-        own, returned = layer(chunks, ln_gain, ln_bias, w_in, w_out)
+        own, returned, done = layer(chunks, ln_gain, ln_bias, w_in, w_out, early, late)
         results, arrived = [], []
-        for i in range(PARTS):
-            if len(chunks) == 1:
-                source, spec = chunks[0], None
-            else:
-                source = chunks[i]
-            whole = len(chunks) == 1
-
-            def combine(*refs, i=i, whole=whole):
-                start = i * piece
-                here = refs[0].at[pl.ds(start, piece)] if whole else refs[0]
+        for i, (start, size) in enumerate(pieces):
+
+            def combine(*refs, start=start, size=size, whole=len(chunks) == 1):
+                here = refs[0].at[pl.ds(start, size)] if whole else refs[0]
                 combine_kernel(start, here, *refs[1:])
 
             result = call(
                 combine,
                 "combine",
-                inner((piece, width)),
+                inner((size, width)),
                 VMEM,
                 [VMEM] * (2 + len(returned[i])),
-                [source, own, *returned[i]],
+                [chunks[min(i, len(chunks) - 1)], own, *returned[i]],
             )
             results.append(result)
             arrived.append(held_inside(from_behind(result, "section")))
         if tick == 0:
-            section_out = call(
-                functools.partial(put_kernel, tick, PARTS),
-                "put",
-                jax.ShapeDtypeStruct((ticks, 1, rows, width), BF16),
-                ANY,
-                [VMEM] * PARTS,
-                results,
-                scratch=[dma((PARTS,))],
-            )
             chunks = [
                 call(
-                    functools.partial(next_kernel, i * piece),
+                    functools.partial(next_kernel, start),
                     "next",
-                    inner((piece, width)),
+                    inner((size, width)),
                     VMEM,
                     [SMEM, VMEM, VMEM],
                     [order, arrived[i], other],
                 )
-                for i in range(PARTS)
+                for i, (start, size) in enumerate(pieces)
             ]
-            held = call(
-                functools.partial(held_kernel, PARTS),
-                "held",
-                jax.ShapeDtypeStruct(acts.shape, BF16),
-                VMEM,
-                [SMEM, VMEM, VMEM] + [VMEM] * PARTS,
-                [order, acts, fresh, *arrived],
-            )
+            early = []
+
+            def late(mine, results=results, arrived=arrived):
+                put = call(
+                    functools.partial(put_kernel, 0, parts),
+                    "put",
+                    pltpu.HBM((ticks, 1, rows, width), BF16),
+                    ANY,
+                    [VMEM] * parts,
+                    results,
+                    scratch=[dma((parts,))],
+                    wait=[mine],
+                )
+                held = call(
+                    functools.partial(held_kernel, parts),
+                    "held",
+                    pltpu.HBM(acts.shape, BF16),
+                    VMEM,
+                    [SMEM, VMEM, VMEM] + [VMEM] * parts,
+                    [order, acts, fresh, *arrived],
+                    wait=[mine],
+                )
+                return [outside(put), outside(held)]
+
         else:
+            section_out, held = done
             section_out = call(
-                functools.partial(put_kernel, tick, PARTS),
+                functools.partial(put_kernel, tick, parts),
                 "put",
                 jax.ShapeDtypeStruct((ticks, 1, rows, width), BF16),
                 ANY,
-                [VMEM] * PARTS + [ANY],
+                [VMEM] * parts + [ANY],
                 [*results, section_out],
-                scratch=[dma((PARTS,))],
-                aliases={PARTS: 0},
+                scratch=[dma((parts,))],
+                aliases={parts: 0},
             )
             held = call(
-                functools.partial(last_kernel, PARTS),
+                functools.partial(last_kernel, parts),
                 "last",
                 jax.ShapeDtypeStruct(acts.shape, BF16),
                 ANY,
-                [SMEM] + [VMEM] * PARTS + [ANY],
+                [SMEM] + [VMEM] * parts + [ANY],
                 [order, *arrived, held],
-                scratch=[dma((PARTS,))],
-                aliases={PARTS + 1: 0},
+                scratch=[dma((parts,))],
+                aliases={parts + 1: 0},
             )
     return section_out, held
 

time: 85.9 us -> 73.5 us (0.86)
  Pallas kernels: 36.3 us -> 28.4 us
  local copies, waits for them, and re-layouts: 4.08 us -> 0.01 us
    pallas_call x19, Pallas kernels: 36.3 us -> 28.4 us  [call(): pl.pallas_call(kernel, name=name, out_shape=outs, out_specs=out_specs, in...]
    ppermute x7, waiting for transfers between devices: 21.4 us -> 17.2 us  [rotate(): lax.ppermute(block, axis, [(i, (i + shift) % size) for i in range(size)])]
    unnamed x16 -> x4, local copies, waits for them, and re-layouts: 4.08 us -> 0.01 us
    ppermute x4, waiting for transfers between devices: 0.6 us -> 4.26 us  [from_behind(): return lax.ppermute(block, axis, [(i, i + 1) for i in range(size - 1)])]
  transfers between devices with their start and end apart: 11 -> 11, of which waited for: 7 -> 7; matrix products, arithmetic and copies ran while one was open for 0% -> 0% of each run, Pallas kernels for 21% -> 27%
where the time goes in v3:
time: 73.5 us; the launch traced here: 73.2 us
  Pallas kernels  28.4 us (39%)
  starting transfers between devices  22.3 us (30%)
  waiting for transfers between devices  21.5 us (29%)
  between operations  0.99 us (1%)
    pallas_call x19, Pallas kernels, call(): pl.pallas_call(kernel, name=name, out_shape=outs, out_specs=out_specs, in...  28.4 us
    ppermute x7, waiting for transfers between devices, rotate(): lax.ppermute(block, axis, [(i, (i + shift) % size) for i in range(size)])  17.2 us
    ppermute x4, starting transfers between devices, from_behind(): return lax.ppermute(block, axis, [(i, i + 1) for i in range(size - 1)])  14.6 us
    ppermute x7, starting transfers between devices, rotate(): lax.ppermute(block, axis, [(i, (i + shift) % size) for i in range(size)])  7.71 us
    ppermute x4, waiting for transfers between devices, from_behind(): return lax.ppermute(block, axis, [(i, i + 1) for i in range(size - 1)])  4.26 us
  transfers between devices with their start and end apart: 11, of which 7 were waited for; matrix products, arithmetic and copies ran while one was open for 0% of the time, Pallas kernels for 27%

profile of v3, /device:TPU:1, one launch (start us, length us, event | category | flops | bytes accessed | tf_op | source)
XLA Modules:
  0.0 73.2 jit_solution(2807632974083443693)
XLA Ops:
  0.7 1.3 %pick.1 = (bf16[128,2048]{1,0:T(8,128)(2,1)S(1)}, s32[1,2]{1,0:T(1,128)S(4)}) custom-call(s32[1,2]{1,0:T(1,128)} %order.1, bf16[1,2,128,2048]{3,2,1,0:T(8,128)(2,1)} %refs_2_.7), custom_call_target="tpu_custom_call" | custom-call | flops 1048576 | bytes 65536 | tf_op jit(solution)/shard_map/pick/pallas_call | solution.py:42
  1.9 2.1 %collective-permute-start = (bf16[128,2048]{1,0:T(8,128)(2,1)S(1)}, bf16[128,2048]{1,0:T(8,128)(2,1)S(1)}, u32[]{:S(2)}, u32[]{:S(2)}) collective-permute-start(bf16[128,2048]{1,0:T(8,128)(2,1)S(1)} %get-tuple-element.13.refs_0_), channel_id=1, source_target_pairs={{0,4},{4,0},{1,5},{5,1},{2,6},{6,2},{3,7},{7,3},{8,12},{12,8},{9,1... | collective-permute-start | bytes 1572872 | tf_op jit(solution)/shard_map/ppermute | solution.py:62
  5.1 5.9 %weights.1 = (bf16[2048,3072]{1,0:T(8,128)(2,1)S(1)}, bf16[1024,2048]{1,0:T(8,128)(2,1)S(1)}) custom-call(bf16[1,2048,3072]{2,1,0:T(8,128)(2,1)} %w_in.1, bf16[1,1024,2048]{2,1,0:T(8,128)(2,1)} %w_out.1), custom_call_target="tpu_custom_call" | custom-call | flops 1073741824 | bytes 65536 | tf_op jit(solution)/shard_map/weights/pallas_call | solution.py:42
  11.0 2.1 %own_qkv.2.refs_6_.mine = bf16[128,3072]{1,0:T(8,128)(2,1)S(1)} custom-call(bf16[128,2048]{1,0:T(8,128)(2,1)S(1)} %get-tuple-element.13.refs_0_, f32[1,2048]{1,0:T(1,128)S(1)} %copy-done, f32[1,2048]{1,0:T(1,128)S(1)} %copy-done.1, bf16[2048,3072]{1,0:T(8,128)(2,1)S(1)} %get-tuple-element.14.refs_3_.refs_4_.refs_6_), custom_call_target="tpu_custom_call" | custom-call | flops 1610612736 | bytes 65536 | tf_op jit(solution)/shard_map/own_qkv/pallas_call | solution.py:42
  13.1 2.5 %collective-permute-done.refs_1_ = bf16[128,2048]{1,0:T(8,128)(2,1)S(1)} collective-permute-done((bf16[128,2048]{1,0:T(8,128)(2,1)S(1)}, bf16[128,2048]{1,0:T(8,128)(2,1)S(1)}, u32[]{:S(2)}, u32[]{:S(2)}) %collective-permute-start) | collective-permute-done | bytes 524320 | tf_op jit(solution)/shard_map/ppermute | solution.py:62
  15.7 3.4 %others.2 = (bf16[128,3072]{1,0:T(8,128)(2,1)S(1)}, bf16[64,2048]{1,0:T(8,128)(2,1)S(1)}, bf16[64,2048]{1,0:T(8,128)(2,1)S(1)}) custom-call(bf16[128,2048]{1,0:T(8,128)(2,1)S(1)} %other.1.refs_0_, bf16[128,2048]{1,0:T(8,128)(2,1)S(1)} %collective-permute-done.refs_1_, f32[1,2048]{1,0:T(1,128)S(1)} %copy-done, f32[1,2048]{1,0:T(1,128)S(1)} %copy-done.1, ...), custom_call_target="tpu_custom_call" | custom-call | flops 1610612736 | bytes 65536 | tf_op jit(solution)/shard_map/others/pallas_call | solution.py:42
  20.7 1.7 %own.2.refs_1_ = bf16[128,2048]{1,0:T(8,128)(2,1)S(1)} custom-call(bf16[128,3072]{1,0:T(8,128)(2,1)S(1)} %own_qkv.2.refs_6_.mine, bf16[128,3072]{1,0:T(8,128)(2,1)S(1)} %get-tuple-element.16.theirs, bf16[1024,2048]{1,0:T(8,128)(2,1)S(1)} %get-tuple-element.15.refs_5_.w_out.refs_7_), custom_call_target="tpu_custom_call" | custom-call | flops 536870912 | bytes 65536 | tf_op jit(solution)/shard_map/own/pallas_call | solution.py:42
  22.4 3.4 %collective-permute-done.1.refs_2_ = bf16[64,2048]{1,0:T(8,128)(2,1)S(1)} collective-permute-done((bf16[64,2048]{1,0:T(8,128)(2,1)S(1)}, bf16[64,2048]{1,0:T(8,128)(2,1)S(1)}, u32[]{:S(2)}, u32[]{:S(2)}) %collective-permute-start.1) | collective-permute-done | bytes 262176 | tf_op jit(solution)/shard_map/ppermute | solution.py:62
  25.9 7.1 %collective-permute-start.2 = (bf16[64,2048]{1,0:T(8,128)(2,1)S(1)}, bf16[64,2048]{1,0:T(8,128)(2,1)S(1)}, u32[]{:S(2)}, u32[]{:S(2)}) collective-permute-start(bf16[64,2048]{1,0:T(8,128)(2,1)S(1)} %combine.4.refs_1_), channel_id=1, source_target_pairs={{0,8},{8,16},{16,24},{1,9},{9,17},{17,25},{2,10},{10,18},{18,26},{... | collective-permute-start | bytes 786440 | tf_op jit(solution)/shard_map/ppermute | solution.py:57
  33.1 3.7 %collective-permute-start.4 = (bf16[64,2048]{1,0:T(8,128)(2,1)S(1)}, bf16[64,2048]{1,0:T(8,128)(2,1)S(1)}, u32[]{:S(2)}, u32[]{:S(2)}) collective-permute-start(bf16[64,2048]{1,0:T(8,128)(2,1)S(1)} %combine.5.refs_2_), channel_id=1, source_target_pairs={{0,8},{8,16},{16,24},{1,9},{9,17},{17,25},{2,10},{10,18},{18,26},{... | collective-permute-start | bytes 786440 | tf_op jit(solution)/shard_map/ppermute | solution.py:57
  36.9 1.3 %collective-permute-start.5 = (bf16[64,2048]{1,0:T(8,128)(2,1)S(1)}, bf16[64,2048]{1,0:T(8,128)(2,1)S(1)}, u32[]{:S(2)}, u32[]{:S(2)}) collective-permute-start(bf16[64,2048]{1,0:T(8,128)(2,1)S(1)} %next.2.refs_0_), channel_id=1, source_target_pairs={{0,4},{4,0},{1,5},{5,1},{2,6},{6,2},{3,7},{7,3},{8,12},{12,8},{9,1... | collective-permute-start | bytes 786440 | tf_op jit(solution)/shard_map/ppermute | solution.py:62
  38.1 1.8 %collective-permute-done.4.arriving.refs_5_ = bf16[64,2048]{1,0:T(8,128)(2,1)S(1)} collective-permute-done((bf16[64,2048]{1,0:T(8,128)(2,1)S(1)}, bf16[64,2048]{1,0:T(8,128)(2,1)S(1)}, u32[]{:S(2)}, u32[]{:S(2)}) %collective-permute-start.4) | collective-permute-done | bytes 262176 | tf_op jit(solution)/shard_map/ppermute | solution.py:57
  40.0 1.3 %collective-permute-start.6 = (bf16[64,2048]{1,0:T(8,128)(2,1)S(1)}, bf16[64,2048]{1,0:T(8,128)(2,1)S(1)}, u32[]{:S(2)}, u32[]{:S(2)}) collective-permute-start(bf16[64,2048]{1,0:T(8,128)(2,1)S(1)} %next.3.refs_1_.refs_0_), channel_id=1, source_target_pairs={{0,4},{4,0},{1,5},{5,1},{2,6},{6,2},{3,7},{7,3},{8,12},{12,8},{9,1... | collective-permute-start | bytes 786440 | tf_op jit(solution)/shard_map/ppermute | solution.py:62
  41.2 2.1 %own_qkv.3.refs_0_.refs_8_.mine = bf16[128,3072]{1,0:T(8,128)(2,1)S(1)} custom-call(bf16[64,2048]{1,0:T(8,128)(2,1)S(1)} %next.2.refs_0_, bf16[64,2048]{1,0:T(8,128)(2,1)S(1)} %next.3.refs_1_.refs_0_, f32[1,2048]{1,0:T(1,128)S(1)} %copy-done, f32[1,2048]{1,0:T(1,128)S(1)} %copy-done.1, bf16[2048,3072]{1,0:T(8,128)(2,1)S(1)} %get-tuple-element.14.refs_3_.refs_4_.refs_6_), custom_call_target="tpu_custom_call" | custom-call | flops 1610612736 | bytes 65536 | tf_op jit(solution)/shard_map/own_qkv/pallas_call | solution.py:42
  44.2 2.7 %held.1.refs_1_.refs_2_ = bf16[1,2,128,2048]{3,2,1,0:T(8,128)(2,1)} custom-call(bf16[128,3072]{1,0:T(8,128)(2,1)S(1)} %own_qkv.3.refs_0_.refs_8_.mine, s32[1,2]{1,0:T(1,128)S(4)} %get-tuple-element.12.order.refs_1_, bf16[1,2,128,2048]{3,2,1,0:T(8,128)(2,1)} %refs_2_.7, bf16[2,128,2048]{2,1,0:T(8,128)(2,1)} %refs_3_.5, ...), custom_call_target="tpu_custom_call" | custom-call | flops 1048576 | bytes 65536 | tf_op jit(solution)/shard_map/held/pallas_call | solution.py:42
  46.9 3.1 %collective-permute-done.6.refs_3_ = bf16[64,2048]{1,0:T(8,128)(2,1)S(1)} collective-permute-done((bf16[64,2048]{1,0:T(8,128)(2,1)S(1)}, bf16[64,2048]{1,0:T(8,128)(2,1)S(1)}, u32[]{:S(2)}, u32[]{:S(2)}) %collective-permute-start.6) | collective-permute-done | bytes 262176 | tf_op jit(solution)/shard_map/ppermute | solution.py:62
  50.0 3.4 %others.3 = (bf16[128,3072]{1,0:T(8,128)(2,1)S(1)}, bf16[64,2048]{1,0:T(8,128)(2,1)S(1)}, bf16[64,2048]{1,0:T(8,128)(2,1)S(1)}) custom-call(bf16[2,1,128,2048]{3,2,1,0:T(8,128)(2,1)} %put.2.refs_0_.refs_2_, bf16[1,2,128,2048]{3,2,1,0:T(8,128)(2,1)} %held.1.refs_1_.refs_2_, bf16[64,2048]{1,0:T(8,128)(2,1)S(1)} %collective-permute-done.5.refs_2_, ...), custom_call_target="tpu_custom_call" | custom-call | flops 1610612736 | bytes 65536 | tf_op jit(solution)/shard_map/others/pallas_call | solution.py:42
  53.4 1.3 %collective-permute-start.7 = (bf16[64,2048]{1,0:T(8,128)(2,1)S(1)}, bf16[64,2048]{1,0:T(8,128)(2,1)S(1)}, u32[]{:S(2)}, u32[]{:S(2)}) collective-permute-start(bf16[64,2048]{1,0:T(8,128)(2,1)S(1)} %get-tuple-element.20), channel_id=1, source_target_pairs={{0,4},{4,0},{1,5},{5,1},{2,6},{6,2},{3,7},{7,3},{8,12},{12,8},{9,1... | collective-permute-start | bytes 786440 | tf_op jit(solution)/shard_map/ppermute | solution.py:62
  55.0 1.7 %own.3.refs_1_ = bf16[128,2048]{1,0:T(8,128)(2,1)S(1)} custom-call(bf16[128,3072]{1,0:T(8,128)(2,1)S(1)} %own_qkv.3.refs_0_.refs_8_.mine, bf16[128,3072]{1,0:T(8,128)(2,1)S(1)} %get-tuple-element.19.theirs, bf16[1024,2048]{1,0:T(8,128)(2,1)S(1)} %get-tuple-element.15.refs_5_.w_out.refs_7_), custom_call_target="tpu_custom_call" | custom-call | flops 536870912 | bytes 65536 | tf_op jit(solution)/shard_map/own/pallas_call | solution.py:42
  56.7 4.6 %collective-permute-done.7.refs_2_ = bf16[64,2048]{1,0:T(8,128)(2,1)S(1)} collective-permute-done((bf16[64,2048]{1,0:T(8,128)(2,1)S(1)}, bf16[64,2048]{1,0:T(8,128)(2,1)S(1)}, u32[]{:S(2)}, u32[]{:S(2)}) %collective-permute-start.7) | collective-permute-done | bytes 262176 | tf_op jit(solution)/shard_map/ppermute | solution.py:62
  61.4 1.9 %collective-permute-start.9 = (bf16[64,2048]{1,0:T(8,128)(2,1)S(1)}, bf16[64,2048]{1,0:T(8,128)(2,1)S(1)}, u32[]{:S(2)}, u32[]{:S(2)}) collective-permute-start(bf16[64,2048]{1,0:T(8,128)(2,1)S(1)} %combine.6.refs_0_), channel_id=1, source_target_pairs={{0,8},{8,16},{16,24},{1,9},{9,17},{17,25},{2,10},{10,18},{18,26},{... | collective-permute-start | bytes 786440 | tf_op jit(solution)/shard_map/ppermute | solution.py:57
  63.3 3.6 %collective-permute-done.8.refs_2_ = bf16[64,2048]{1,0:T(8,128)(2,1)S(1)} collective-permute-done((bf16[64,2048]{1,0:T(8,128)(2,1)S(1)}, bf16[64,2048]{1,0:T(8,128)(2,1)S(1)}, u32[]{:S(2)}, u32[]{:S(2)}) %collective-permute-start.8) | collective-permute-done | bytes 262176 | tf_op jit(solution)/shard_map/ppermute | solution.py:62
  67.0 1.9 %collective-permute-start.10 = (bf16[64,2048]{1,0:T(8,128)(2,1)S(1)}, bf16[64,2048]{1,0:T(8,128)(2,1)S(1)}, u32[]{:S(2)}, u32[]{:S(2)}) collective-permute-start(bf16[64,2048]{1,0:T(8,128)(2,1)S(1)} %combine.7.refs_1_), channel_id=1, source_target_pairs={{0,8},{8,16},{16,24},{1,9},{9,17},{17,25},{2,10},{10,18},{18,26},{... | collective-permute-start | bytes 786440 | tf_op jit(solution)/shard_map/ppermute | solution.py:57
  69.8 2.5 %collective-permute-done.10.refs_1_ = bf16[64,2048]{1,0:T(8,128)(2,1)S(1)} collective-permute-done((bf16[64,2048]{1,0:T(8,128)(2,1)S(1)}, bf16[64,2048]{1,0:T(8,128)(2,1)S(1)}, u32[]{:S(2)}, u32[]{:S(2)}) %collective-permute-start.10) | collective-permute-done | bytes 262176 | tf_op jit(solution)/shard_map/ppermute | solution.py:57
  (21 shorter events, 5.8 us)
Async XLA Ops:
  0.6 10.4 %copy-start.1 = (f32[1,2048]{1,0:T(1,128)S(1)}, f32[1,2048]{1,0:T(1,128)}, u32[]{:S(2)}) copy-start(f32[1,2048]{1,0:T(1,128)} %refs_5_.1) | copy-start | bytes 24580
  0.6 10.4 %copy-start = (f32[1,2048]{1,0:T(1,128)S(1)}, f32[1,2048]{1,0:T(1,128)}, u32[]{:S(2)}) copy-start(f32[1,2048]{1,0:T(1,128)} %refs_4_.1) | copy-start | bytes 24580
  1.9 13.7 %collective-permute-start = (bf16[128,2048]{1,0:T(8,128)(2,1)S(1)}, bf16[128,2048]{1,0:T(8,128)(2,1)S(1)}, u32[]{:S(2)}, u32[]{:S(2)}) collective-permute-start(bf16[128,2048]{1,0:T(8,128)(2,1)S(1)} %get-tuple-element.13.refs_0_), channel_id=1, source_target_pairs={{0,4},{4,0},{1,5},{5,1},{2,6},{6,2},{3,7},{7,3},{8,12},{12,8},{9,1... | collective-permute-start | bytes 1572872 | tf_op jit(solution)/shard_map/ppermute | solution.py:62
  19.1 6.7 %collective-permute-start.1 = (bf16[64,2048]{1,0:T(8,128)(2,1)S(1)}, bf16[64,2048]{1,0:T(8,128)(2,1)S(1)}, u32[]{:S(2)}, u32[]{:S(2)}) collective-permute-start(bf16[64,2048]{1,0:T(8,128)(2,1)S(1)} %get-tuple-element.17), channel_id=1, source_target_pairs={{0,4},{4,0},{1,5},{5,1},{2,6},{6,2},{3,7},{7,3},{8,12},{12,8},{9,1... | collective-permute-start | bytes 786440 | tf_op jit(solution)/shard_map/ppermute | solution.py:62
  20.4 12.7 %collective-permute-start.3 = (bf16[64,2048]{1,0:T(8,128)(2,1)S(1)}, bf16[64,2048]{1,0:T(8,128)(2,1)S(1)}, u32[]{:S(2)}, u32[]{:S(2)}) collective-permute-start(bf16[64,2048]{1,0:T(8,128)(2,1)S(1)} %get-tuple-element.18), channel_id=1, source_target_pairs={{0,4},{4,0},{1,5},{5,1},{2,6},{6,2},{3,7},{7,3},{8,12},{12,8},{9,1... | collective-permute-start | bytes 786440 | tf_op jit(solution)/shard_map/ppermute | solution.py:62
  25.9 10.9 %collective-permute-start.2 = (bf16[64,2048]{1,0:T(8,128)(2,1)S(1)}, bf16[64,2048]{1,0:T(8,128)(2,1)S(1)}, u32[]{:S(2)}, u32[]{:S(2)}) collective-permute-start(bf16[64,2048]{1,0:T(8,128)(2,1)S(1)} %combine.4.refs_1_), channel_id=1, source_target_pairs={{0,8},{8,16},{16,24},{1,9},{9,17},{17,25},{2,10},{10,18},{18,26},{... | collective-permute-start | bytes 786440 | tf_op jit(solution)/shard_map/ppermute | solution.py:57
  33.1 6.8 %collective-permute-start.4 = (bf16[64,2048]{1,0:T(8,128)(2,1)S(1)}, bf16[64,2048]{1,0:T(8,128)(2,1)S(1)}, u32[]{:S(2)}, u32[]{:S(2)}) collective-permute-start(bf16[64,2048]{1,0:T(8,128)(2,1)S(1)} %combine.5.refs_2_), channel_id=1, source_target_pairs={{0,8},{8,16},{16,24},{1,9},{9,17},{17,25},{2,10},{10,18},{18,26},{... | collective-permute-start | bytes 786440 | tf_op jit(solution)/shard_map/ppermute | solution.py:57
  36.9 10.0 %collective-permute-start.5 = (bf16[64,2048]{1,0:T(8,128)(2,1)S(1)}, bf16[64,2048]{1,0:T(8,128)(2,1)S(1)}, u32[]{:S(2)}, u32[]{:S(2)}) collective-permute-start(bf16[64,2048]{1,0:T(8,128)(2,1)S(1)} %next.2.refs_0_), channel_id=1, source_target_pairs={{0,4},{4,0},{1,5},{5,1},{2,6},{6,2},{3,7},{7,3},{8,12},{12,8},{9,1... | collective-permute-start | bytes 786440 | tf_op jit(solution)/shard_map/ppermute | solution.py:62
  40.0 10.0 %collective-permute-start.6 = (bf16[64,2048]{1,0:T(8,128)(2,1)S(1)}, bf16[64,2048]{1,0:T(8,128)(2,1)S(1)}, u32[]{:S(2)}, u32[]{:S(2)}) collective-permute-start(bf16[64,2048]{1,0:T(8,128)(2,1)S(1)} %next.3.refs_1_.refs_0_), channel_id=1, source_target_pairs={{0,4},{4,0},{1,5},{5,1},{2,6},{6,2},{3,7},{7,3},{8,12},{12,8},{9,1... | collective-permute-start | bytes 786440 | tf_op jit(solution)/shard_map/ppermute | solution.py:62
  53.4 7.8 %collective-permute-start.7 = (bf16[64,2048]{1,0:T(8,128)(2,1)S(1)}, bf16[64,2048]{1,0:T(8,128)(2,1)S(1)}, u32[]{:S(2)}, u32[]{:S(2)}) collective-permute-start(bf16[64,2048]{1,0:T(8,128)(2,1)S(1)} %get-tuple-element.20), channel_id=1, source_target_pairs={{0,4},{4,0},{1,5},{5,1},{2,6},{6,2},{3,7},{7,3},{8,12},{12,8},{9,1... | collective-permute-start | bytes 786440 | tf_op jit(solution)/shard_map/ppermute | solution.py:62
  54.7 12.2 %collective-permute-start.8 = (bf16[64,2048]{1,0:T(8,128)(2,1)S(1)}, bf16[64,2048]{1,0:T(8,128)(2,1)S(1)}, u32[]{:S(2)}, u32[]{:S(2)}) collective-permute-start(bf16[64,2048]{1,0:T(8,128)(2,1)S(1)} %get-tuple-element.21), channel_id=1, source_target_pairs={{0,4},{4,0},{1,5},{5,1},{2,6},{6,2},{3,7},{7,3},{8,12},{12,8},{9,1... | collective-permute-start | bytes 786440 | tf_op jit(solution)/shard_map/ppermute | solution.py:62
  61.4 8.4 %collective-permute-start.9 = (bf16[64,2048]{1,0:T(8,128)(2,1)S(1)}, bf16[64,2048]{1,0:T(8,128)(2,1)S(1)}, u32[]{:S(2)}, u32[]{:S(2)}) collective-permute-start(bf16[64,2048]{1,0:T(8,128)(2,1)S(1)} %combine.6.refs_0_), channel_id=1, source_target_pairs={{0,8},{8,16},{16,24},{1,9},{9,17},{17,25},{2,10},{10,18},{18,26},{... | collective-permute-start | bytes 786440 | tf_op jit(solution)/shard_map/ppermute | solution.py:57
  67.0 5.2 %collective-permute-start.10 = (bf16[64,2048]{1,0:T(8,128)(2,1)S(1)}, bf16[64,2048]{1,0:T(8,128)(2,1)S(1)}, u32[]{:S(2)}, u32[]{:S(2)}) collective-permute-start(bf16[64,2048]{1,0:T(8,128)(2,1)S(1)} %combine.7.refs_1_), channel_id=1, source_target_pairs={{0,8},{8,16},{16,24},{1,9},{9,17},{17,25},{2,10},{10,18},{18,26},{... | collective-permute-start | bytes 786440 | tf_op jit(solution)/shard_map/ppermute | solution.py:57

commit v4 on v3

--- a/solution.py
+++ b/solution.py
@@ -7,6 +7,7 @@
 from jax.experimental.pallas import tpu as pltpu
 from jax.sharding import PartitionSpec as P
 
+
 HD = 128
 PARTS = 2
 MIB = 1 << 20
@@ -34,14 +35,13 @@
     return lambda *refs: kernel(*refs[count:])
 
 
-def call(kernel, name, outs, out_specs, in_specs, args, flops=0, scratch=(), aliases=None, limit=16, wait=()):
+def call(kernel, outs, out_specs, in_specs, args, flops=0, scratch=(), aliases=None, limit=16, wait=()):
     if wait:
         kernel = after(kernel, len(wait))
         in_specs, args = [ANY] * len(wait) + in_specs, [*wait, *args]
         aliases = {k + len(wait): v for k, v in (aliases or {}).items()}
     return pl.pallas_call(
         kernel,
-        name=name,
         out_shape=outs,
         out_specs=out_specs,
         in_specs=in_specs,
@@ -57,9 +57,10 @@
     return lax.ppermute(block, axis, [(i, i + 1) for i in range(size - 1)])
 
 
-def rotate(block, axis, shift):
-    size = lax.axis_size(axis)
-    return lax.ppermute(block, axis, [(i, (i + shift) % size) for i in range(size)])
+def rotate(block, shift, sections):
+    size = lax.axis_size("tensor")
+    route = [(s * size + i, s * size + (i + shift) % size) for s in sections for i in range(size)]
+    return held_inside(lax.ppermute(block, ("section", "tensor"), route))
 
 
 def pick_kernel(order, acts, current, kept, slots, sems):
@@ -142,8 +143,9 @@
     project(hidden[...], weights, qkv)
 
 
-def others_kernel(parts, pieces, *refs):
-    chunks = refs[:parts]
+def others_kernel(parts, pieces, spare, *refs):
+    chunks, alone, refs = refs[:parts], refs[parts : parts + spare], refs[:parts] + refs[parts + spare :]
+    first = lax.axis_index("section") == 0
     gain, bias, w_in, w_out, mine = refs[parts : parts + 5]
     qkv = refs[parts + 5]
     outs = refs[parts + 6 : parts + 6 + pieces]
@@ -151,7 +153,11 @@
     at = 0
     for chunk in chunks:
         rows = chunk.shape[0]
-        hidden[at : at + rows] = normed(chunk[...], gain[...], bias[...])
+        value = chunk[...]
+        if alone:
+            start = at % alone[0].shape[0]
+            value = jnp.where(first, alone[at // alone[0].shape[0]][start : start + rows], value)
+        hidden[at : at + rows] = normed(value, gain[...], bias[...])
         at += rows
     project(hidden[...], w_in, qkv)
     attend(qkv, (mine, qkv), slice(0, at), mixed)
@@ -233,16 +239,16 @@
     return [(sum(sizes[:i]), size) for i, size in enumerate(sizes)]
 
 
-def layer(chunks, gain, bias, w_in, w_out, early=(), late=None):
+def layer(chunks, gain, bias, w_in, w_out, alone=(), early=()):
     size = lax.axis_size("tensor")
+    sections = range(lax.axis_size("section"))
     parts = len(chunks)
     rows = sum(c.shape[0] for c in chunks)
     wide, deep = w_in.shape[1], w_out.shape[0]
     width = w_in.shape[0]
-    got = [held_inside(rotate(c, "tensor", j)) for j in range(1, size) for c in chunks]
+    got = [rotate(c, j, sections[1:] if alone else sections) for j in range(1, size) for c in chunks]
     mine = call(
         functools.partial(own_qkv_kernel, parts),
-        "own_qkv",
         inner((rows, wide)),
         VMEM,
         [VMEM] * (parts + 3),
@@ -253,25 +259,22 @@
     far = (size - 1) * rows
     pieces = cuts(rows)
     count = (size - 1) * len(pieces)
-    done = late(mine) if late else []
     theirs, *sends = call(
-        functools.partial(others_kernel, len(got), count),
-        "others",
+        functools.partial(others_kernel, len(got), count, len(alone)),
         [inner((far, wide))] + [inner((n, width)) for _ in range(size - 1) for _, n in pieces],
         [VMEM] * (count + 1),
-        [VMEM] * (len(got) + 5),
-        [*got, gain, bias, w_in, w_out, mine],
+        [VMEM] * (len(got) + len(alone) + 5),
+        [*got, *alone, gain, bias, w_in, w_out, mine],
         flops=2 * far * width * wide,
         scratch=[inner((far, width)), inner((far, deep))],
-        wait=[*early, *done],
+        wait=early,
     )
     returned = [
-        [held_inside(rotate(sends[(j - 1) * len(pieces) + i], "tensor", -j)) for j in range(1, size)]
+        [rotate(sends[(j - 1) * len(pieces) + i], -j, sections) for j in range(1, size)]
         for i in range(len(pieces))
     ]
     own = call(
         own_kernel,
-        "own",
         inner((rows, width)),
         VMEM,
         [VMEM] * 3,
@@ -279,27 +282,33 @@
         flops=2 * rows * width * deep,
         scratch=[inner((rows, deep))],
     )
-    return own, returned, done
+    return own, returned
 
 
 def body(acts, fresh, order, ln_gain, ln_bias, wqkv, wo):
     rows, width = acts.shape[2:]
-    piece = rows // PARTS
     ticks = fresh.shape[0]
     dma = pltpu.SemaphoreType.DMA
     acts, fresh, order, wqkv, wo = map(outside, (acts, fresh, order, wqkv, wo))
     current, order = call(
         pick_kernel,
-        "pick",
         [inner((rows, width)), pltpu.SMEM(order.shape, order.dtype)],
         [VMEM, SMEM],
         [ANY, ANY],
         [order, acts],
         scratch=[inner(acts.shape[1:]), dma((2,))],
     )
+    other = call(
+        other_kernel,
+        inner((rows, width)),
+        VMEM,
+        [SMEM, ANY, ANY],
+        [order, acts, fresh],
+        scratch=[dma((2,))],
+    )
+    alone = [rotate(other, j, [0]) for j in range(1, lax.axis_size("tensor"))]
     w_in, w_out = call(
         weights_kernel,
-        "weights",
         [inner(wqkv.shape[1:]), inner(wo.shape[1:])],
         [VMEM, VMEM],
         [ANY, ANY],
@@ -308,22 +317,33 @@
         limit=24,
         flops=1 << 30,
     )
-    other = call(
-        other_kernel,
-        "other",
-        inner((rows, width)),
-        VMEM,
-        [SMEM, ANY, ANY],
-        [order, acts, fresh],
-        scratch=[dma((2,))],
-    )
     chunks = [current]
     pieces = cuts(rows)
     parts = len(pieces)
-    section_out = held = late = None
-    early = [other]
+    section_out = held = None
     for tick in range(ticks):
-        own, returned, done = layer(chunks, ln_gain, ln_bias, w_in, w_out, early, late)
+        own, returned = layer(chunks, ln_gain, ln_bias, w_in, w_out, alone if tick else ())
+        ready = []
+        if tick:
+            section_out = call(
+                functools.partial(put_kernel, 0, parts),
+                pltpu.HBM((ticks, 1, rows, width), BF16),
+                ANY,
+                [VMEM] * parts,
+                results,
+                scratch=[dma((parts,))],
+                wait=[own],
+            )
+            held = call(
+                functools.partial(held_kernel, parts),
+                pltpu.HBM(acts.shape, BF16),
+                VMEM,
+                [SMEM, VMEM, VMEM] + [VMEM] * parts,
+                [order, acts, fresh, *arrived],
+                wait=[own],
+            )
+            section_out, held = outside(section_out), outside(held)
+            ready = [section_out, held]
         results, arrived = [], []
         for i, (start, size) in enumerate(pieces):
 
@@ -333,11 +353,11 @@
 
             result = call(
                 combine,
-                "combine",
                 inner((size, width)),
                 VMEM,
                 [VMEM] * (2 + len(returned[i])),
                 [chunks[min(i, len(chunks) - 1)], own, *returned[i]],
+                wait=ready,
             )
             results.append(result)
             arrived.append(held_inside(from_behind(result, "section")))
@@ -345,7 +365,6 @@
             chunks = [
                 call(
                     functools.partial(next_kernel, start),
-                    "next",
                     inner((size, width)),
                     VMEM,
                     [SMEM, VMEM, VMEM],
@@ -353,52 +372,24 @@
                 )
                 for i, (start, size) in enumerate(pieces)
             ]
-            early = []
-
-            def late(mine, results=results, arrived=arrived):
-                put = call(
-                    functools.partial(put_kernel, 0, parts),
-                    "put",
-                    pltpu.HBM((ticks, 1, rows, width), BF16),
-                    ANY,
-                    [VMEM] * parts,
-                    results,
-                    scratch=[dma((parts,))],
-                    wait=[mine],
-                )
-                held = call(
-                    functools.partial(held_kernel, parts),
-                    "held",
-                    pltpu.HBM(acts.shape, BF16),
-                    VMEM,
-                    [SMEM, VMEM, VMEM] + [VMEM] * parts,
-                    [order, acts, fresh, *arrived],
-                    wait=[mine],
-                )
-                return [outside(put), outside(held)]
-
-        else:
-            section_out, held = done
-            section_out = call(
-                functools.partial(put_kernel, tick, parts),
-                "put",
-                jax.ShapeDtypeStruct((ticks, 1, rows, width), BF16),
-                ANY,
-                [VMEM] * parts + [ANY],
-                [*results, section_out],
-                scratch=[dma((parts,))],
-                aliases={parts: 0},
-            )
-            held = call(
-                functools.partial(last_kernel, parts),
-                "last",
-                jax.ShapeDtypeStruct(acts.shape, BF16),
-                ANY,
-                [SMEM] + [VMEM] * parts + [ANY],
-                [order, *arrived, held],
-                scratch=[dma((parts,))],
-                aliases={parts + 1: 0},
-            )
+    section_out = call(
+        functools.partial(put_kernel, ticks - 1, parts),
+        jax.ShapeDtypeStruct((ticks, 1, rows, width), BF16),
+        ANY,
+        [VMEM] * parts + [ANY],
+        [*results, section_out],
+        scratch=[dma((parts,))],
+        aliases={parts: 0},
+    )
+    held = call(
+        functools.partial(last_kernel, parts),
+        jax.ShapeDtypeStruct(acts.shape, BF16),
+        ANY,
+        [SMEM] + [VMEM] * parts + [ANY],
+        [order, *arrived, held],
+        scratch=[dma((parts,))],
+        aliases={parts + 1: 0},
+    )
     return section_out, held
 
 

time: 73.5 us -> 76.3 us (1.038)
  starting transfers between devices: 22.3 us -> 25.8 us
    ppermute x7 -> x8, starting transfers between devices: 7.71 us -> 11.3 us  [rotate(): return held_inside(lax.ppermute(block, ('section', 'tensor'), route))]
    ppermute x4, waiting for transfers between devices: 4.26 us -> 2.47 us  [from_behind(): return lax.ppermute(block, axis, [(i, i + 1) for i in range(size - 1)])]
    ppermute x7 -> x8, waiting for transfers between devices: 17.2 us -> 18.3 us  [rotate(): return held_inside(lax.ppermute(block, ('section', 'tensor'), route))]
  transfers between devices with their start and end apart: 11 -> 12, of which waited for: 7 -> 7; matrix products, arithmetic and copies ran while one was open for 0% -> 0% of each run, Pallas kernels for 27% -> 26%
where the time goes in v4:
time: 76.3 us; the launch traced here: 76 us
  Pallas kernels  28.4 us (37%)
  starting transfers between devices  25.8 us (34%)
  waiting for transfers between devices  20.8 us (27%)
  between operations  1.04 us (1%)
    pallas_call x19, Pallas kernels, call(): pl.pallas_call(kernel, out_shape=outs, out_specs=out_specs, in_specs=in_s...  28.4 us
    ppermute x8, waiting for transfers between devices, rotate(): return held_inside(lax.ppermute(block, ('section', 'tensor'), route))  18.3 us
    ppermute x4, starting transfers between devices, from_behind(): return lax.ppermute(block, axis, [(i, i + 1) for i in range(size - 1)])  14.4 us
    ppermute x8, starting transfers between devices, rotate(): return held_inside(lax.ppermute(block, ('section', 'tensor'), route))  11.3 us
    ppermute x4, waiting for transfers between devices, from_behind(): return lax.ppermute(block, axis, [(i, i + 1) for i in range(size - 1)])  2.47 us
  transfers between devices with their start and end apart: 12, of which 7 were waited for; matrix products, arithmetic and copies ran while one was open for 0% of the time, Pallas kernels for 26%

profile of v4, /device:TPU:1, one launch (start us, length us, event | category | flops | bytes accessed | tf_op | source)
XLA Modules:
  0.0 76.0 jit_solution(18237900195744296404)
XLA Ops:
  0.7 1.3 %shard_map.86 = (bf16[128,2048]{1,0:T(8,128)(2,1)S(1)}, s32[1,2]{1,0:T(1,128)S(4)}) custom-call(s32[1,2]{1,0:T(1,128)} %order.1, bf16[1,2,128,2048]{3,2,1,0:T(8,128)(2,1)} %refs_2_.7), custom_call_target="tpu_custom_call" | custom-call | flops 1048576 | bytes 65536 | tf_op jit(solution)/shard_map/pallas_call | solution.py:43
  1.9 2.1 %collective-permute-start = (bf16[128,2048]{1,0:T(8,128)(2,1)S(1)}, bf16[128,2048]{1,0:T(8,128)(2,1)S(1)}, u32[]{:S(2)}, u32[]{:S(2)}) collective-permute-start(bf16[128,2048]{1,0:T(8,128)(2,1)S(1)} %get-tuple-element.13.refs_0_), channel_id=1, source_target_pairs={{0,4},{4,0},{8,12},{12,8},{16,20},{20,16},{24,28},{28,24},{1,5},{5... | collective-permute-start | bytes 1572872 | tf_op jit(solution)/shard_map/ppermute | solution.py:63
  4.0 5.9 %shard_map.87 = (bf16[2048,3072]{1,0:T(8,128)(2,1)S(1)}, bf16[1024,2048]{1,0:T(8,128)(2,1)S(1)}) custom-call(bf16[1,2048,3072]{2,1,0:T(8,128)(2,1)} %w_in.1, bf16[1,1024,2048]{2,1,0:T(8,128)(2,1)} %w_out.1), custom_call_target="tpu_custom_call" | custom-call | flops 1073741824 | bytes 65536 | tf_op jit(solution)/shard_map/pallas_call | solution.py:43
  10.0 2.1 %shard_map.88.refs_5_.mine = bf16[128,3072]{1,0:T(8,128)(2,1)S(1)} custom-call(bf16[128,2048]{1,0:T(8,128)(2,1)S(1)} %get-tuple-element.13.refs_0_, f32[1,2048]{1,0:T(1,128)S(1)} %copy-done, f32[1,2048]{1,0:T(1,128)S(1)} %copy-done.1, bf16[2048,3072]{1,0:T(8,128)(2,1)S(1)} %get-tuple-element.14.refs_3_.refs_4_.refs_5_), custom_call_target="tpu_custom_call" | custom-call | flops 1610612736 | bytes 65536 | tf_op jit(solution)/shard_map/pallas_call | solution.py:43
  12.1 3.6 %collective-permute-done.refs_0_ = bf16[128,2048]{1,0:T(8,128)(2,1)S(1)} collective-permute-done((bf16[128,2048]{1,0:T(8,128)(2,1)S(1)}, bf16[128,2048]{1,0:T(8,128)(2,1)S(1)}, u32[]{:S(2)}, u32[]{:S(2)}) %collective-permute-start) | collective-permute-done | bytes 524320 | tf_op jit(solution)/shard_map/ppermute | solution.py:63
  15.7 3.4 %shard_map.89 = (bf16[128,3072]{1,0:T(8,128)(2,1)S(1)}, bf16[64,2048]{1,0:T(8,128)(2,1)S(1)}, bf16[64,2048]{1,0:T(8,128)(2,1)S(1)}) custom-call(bf16[128,2048]{1,0:T(8,128)(2,1)S(1)} %collective-permute-done.refs_0_, f32[1,2048]{1,0:T(1,128)S(1)} %copy-done, f32[1,2048]{1,0:T(1,128)S(1)} %copy-done.1, ...), custom_call_target="tpu_custom_call" | custom-call | flops 1610612736 | bytes 65536 | tf_op jit(solution)/shard_map/pallas_call | solution.py:43
  20.7 1.7 %shard_map.90.refs_1_ = bf16[128,2048]{1,0:T(8,128)(2,1)S(1)} custom-call(bf16[128,3072]{1,0:T(8,128)(2,1)S(1)} %shard_map.88.refs_5_.mine, bf16[128,3072]{1,0:T(8,128)(2,1)S(1)} %get-tuple-element.16.theirs, bf16[1024,2048]{1,0:T(8,128)(2,1)S(1)} %get-tuple-element.15.refs_4_.w_out.refs_6_), custom_call_target="tpu_custom_call" | custom-call | flops 536870912 | bytes 65536 | tf_op jit(solution)/shard_map/pallas_call | solution.py:43
  22.4 3.4 %collective-permute-done.1.refs_2_ = bf16[64,2048]{1,0:T(8,128)(2,1)S(1)} collective-permute-done((bf16[64,2048]{1,0:T(8,128)(2,1)S(1)}, bf16[64,2048]{1,0:T(8,128)(2,1)S(1)}, u32[]{:S(2)}, u32[]{:S(2)}) %collective-permute-start.1) | collective-permute-done | bytes 262176 | tf_op jit(solution)/shard_map/ppermute | solution.py:63
  25.9 7.1 %collective-permute-start.2 = (bf16[64,2048]{1,0:T(8,128)(2,1)S(1)}, bf16[64,2048]{1,0:T(8,128)(2,1)S(1)}, u32[]{:S(2)}, u32[]{:S(2)}) collective-permute-start(bf16[64,2048]{1,0:T(8,128)(2,1)S(1)} %shard_map.91.refs_1_), channel_id=1, source_target_pairs={{0,8},{8,16},{16,24},{1,9},{9,17},{17,25},{2,10},{10,18},{18,26},{... | collective-permute-start | bytes 786440 | tf_op jit(solution)/shard_map/ppermute | solution.py:57
  33.1 3.5 %collective-permute-start.4 = (bf16[64,2048]{1,0:T(8,128)(2,1)S(1)}, bf16[64,2048]{1,0:T(8,128)(2,1)S(1)}, u32[]{:S(2)}, u32[]{:S(2)}) collective-permute-start(bf16[64,2048]{1,0:T(8,128)(2,1)S(1)} %shard_map.94.refs_2_), channel_id=1, source_target_pairs={{0,8},{8,16},{16,24},{1,9},{9,17},{17,25},{2,10},{10,18},{18,26},{... | collective-permute-start | bytes 786440 | tf_op jit(solution)/shard_map/ppermute | solution.py:57
  38.5 3.1 %collective-permute-start.5 = (bf16[64,2048]{1,0:T(8,128)(2,1)S(1)}, bf16[64,2048]{1,0:T(8,128)(2,1)S(1)}, u32[]{:S(2)}, u32[]{:S(2)}) collective-permute-start(bf16[64,2048]{1,0:T(8,128)(2,1)S(1)} %shard_map.93.refs_0_.refs_2_), channel_id=1, source_target_pairs={{8,12},{12,8},{16,20},{20,16},{24,28},{28,24},{9,13},{13,9},{17,21... | collective-permute-start | bytes 786440 | tf_op jit(solution)/shard_map/ppermute | solution.py:63
  41.6 2.3 %collective-permute-start.6 = (bf16[64,2048]{1,0:T(8,128)(2,1)S(1)}, bf16[64,2048]{1,0:T(8,128)(2,1)S(1)}, u32[]{:S(2)}, u32[]{:S(2)}) collective-permute-start(bf16[64,2048]{1,0:T(8,128)(2,1)S(1)} %shard_map.95.refs_1_.refs_2_), channel_id=1, source_target_pairs={{8,12},{12,8},{16,20},{20,16},{24,28},{28,24},{9,13},{13,9},{17,21... | collective-permute-start | bytes 786440 | tf_op jit(solution)/shard_map/ppermute | solution.py:63
  44.0 2.1 %shard_map.96.refs_7_.mine = bf16[128,3072]{1,0:T(8,128)(2,1)S(1)} custom-call(bf16[64,2048]{1,0:T(8,128)(2,1)S(1)} %shard_map.93.refs_0_.refs_2_, bf16[64,2048]{1,0:T(8,128)(2,1)S(1)} %shard_map.95.refs_1_.refs_2_, f32[1,2048]{1,0:T(1,128)S(1)} %copy-done, f32[1,2048]{1,0:T(1,128)S(1)} %copy-done.1, ...), custom_call_target="tpu_custom_call" | custom-call | flops 1610612736 | bytes 65536 | tf_op jit(solution)/shard_map/pallas_call | solution.py:43
  46.1 2.6 %collective-permute-done.5.refs_0_ = bf16[64,2048]{1,0:T(8,128)(2,1)S(1)} collective-permute-done((bf16[64,2048]{1,0:T(8,128)(2,1)S(1)}, bf16[64,2048]{1,0:T(8,128)(2,1)S(1)}, u32[]{:S(2)}, u32[]{:S(2)}) %collective-permute-start.5) | collective-permute-done | bytes 262176 | tf_op jit(solution)/shard_map/ppermute | solution.py:63
  48.7 4.0 %collective-permute-done.6.refs_1_ = bf16[64,2048]{1,0:T(8,128)(2,1)S(1)} collective-permute-done((bf16[64,2048]{1,0:T(8,128)(2,1)S(1)}, bf16[64,2048]{1,0:T(8,128)(2,1)S(1)}, u32[]{:S(2)}, u32[]{:S(2)}) %collective-permute-start.6) | collective-permute-done | bytes 262176 | tf_op jit(solution)/shard_map/ppermute | solution.py:63
  52.7 3.5 %shard_map.97 = (bf16[128,3072]{1,0:T(8,128)(2,1)S(1)}, bf16[64,2048]{1,0:T(8,128)(2,1)S(1)}, bf16[64,2048]{1,0:T(8,128)(2,1)S(1)}) custom-call(bf16[64,2048]{1,0:T(8,128)(2,1)S(1)} %collective-permute-done.5.refs_0_, bf16[64,2048]{1,0:T(8,128)(2,1)S(1)} %collective-permute-done.6.refs_1_, bf16[128,2048]{1,0:T(8,128)(2,1)S(1)} %collective-permute-done.7.refs_2_, ...), custom_call_target="tpu_custom_call" | custom-call | flops 1610612736 | bytes 65536 | tf_op jit(solution)/shard_map/pallas_call | solution.py:43
  56.1 1.3 %collective-permute-start.8 = (bf16[64,2048]{1,0:T(8,128)(2,1)S(1)}, bf16[64,2048]{1,0:T(8,128)(2,1)S(1)}, u32[]{:S(2)}, u32[]{:S(2)}) collective-permute-start(bf16[64,2048]{1,0:T(8,128)(2,1)S(1)} %get-tuple-element.20), channel_id=1, source_target_pairs={{0,4},{4,0},{8,12},{12,8},{16,20},{20,16},{24,28},{28,24},{1,5},{5... | collective-permute-start | bytes 786440 | tf_op jit(solution)/shard_map/ppermute | solution.py:63
  57.6 1.7 %shard_map.98.refs_0_.refs_3_ = bf16[128,2048]{1,0:T(8,128)(2,1)S(1)} custom-call(bf16[128,3072]{1,0:T(8,128)(2,1)S(1)} %shard_map.96.refs_7_.mine, bf16[128,3072]{1,0:T(8,128)(2,1)S(1)} %get-tuple-element.19.theirs, bf16[1024,2048]{1,0:T(8,128)(2,1)S(1)} %get-tuple-element.15.refs_4_.w_out.refs_6_), custom_call_target="tpu_custom_call" | custom-call | flops 536870912 | bytes 65536 | tf_op jit(solution)/shard_map/pallas_call | solution.py:43
  60.2 2.7 %shard_map.100.refs_1_.refs_2_ = bf16[1,2,128,2048]{3,2,1,0:T(8,128)(2,1)} custom-call(bf16[128,2048]{1,0:T(8,128)(2,1)S(1)} %shard_map.98.refs_0_.refs_3_, s32[1,2]{1,0:T(1,128)S(4)} %get-tuple-element.12.order.refs_1_, bf16[1,2,128,2048]{3,2,1,0:T(8,128)(2,1)} %refs_2_.7, bf16[2,128,2048]{2,1,0:T(8,128)(2,1)} %refs_3_.5, ...), custom_call_target="tpu_custom_call" | custom-call | flops 1048576 | bytes 65536 | tf_op jit(solution)/shard_map/pallas_call | solution.py:43
  62.9 1.6 %collective-permute-done.8.refs_4_ = bf16[64,2048]{1,0:T(8,128)(2,1)S(1)} collective-permute-done((bf16[64,2048]{1,0:T(8,128)(2,1)S(1)}, bf16[64,2048]{1,0:T(8,128)(2,1)S(1)}, u32[]{:S(2)}, u32[]{:S(2)}) %collective-permute-start.8) | collective-permute-done | bytes 262176 | tf_op jit(solution)/shard_map/ppermute | solution.py:63
  64.6 1.9 %collective-permute-start.10 = (bf16[64,2048]{1,0:T(8,128)(2,1)S(1)}, bf16[64,2048]{1,0:T(8,128)(2,1)S(1)}, u32[]{:S(2)}, u32[]{:S(2)}) collective-permute-start(bf16[64,2048]{1,0:T(8,128)(2,1)S(1)} %shard_map.101.refs_0_), channel_id=1, source_target_pairs={{0,8},{8,16},{16,24},{1,9},{9,17},{17,25},{2,10},{10,18},{18,26},{... | collective-permute-start | bytes 786440 | tf_op jit(solution)/shard_map/ppermute | solution.py:57
  66.5 3.2 %collective-permute-done.9.refs_4_ = bf16[64,2048]{1,0:T(8,128)(2,1)S(1)} collective-permute-done((bf16[64,2048]{1,0:T(8,128)(2,1)S(1)}, bf16[64,2048]{1,0:T(8,128)(2,1)S(1)}, u32[]{:S(2)}, u32[]{:S(2)}) %collective-permute-start.9) | collective-permute-done | bytes 262176 | tf_op jit(solution)/shard_map/ppermute | solution.py:63
  69.8 1.9 %collective-permute-start.11 = (bf16[64,2048]{1,0:T(8,128)(2,1)S(1)}, bf16[64,2048]{1,0:T(8,128)(2,1)S(1)}, u32[]{:S(2)}, u32[]{:S(2)}) collective-permute-start(bf16[64,2048]{1,0:T(8,128)(2,1)S(1)} %shard_map.102.refs_1_), channel_id=1, source_target_pairs={{0,8},{8,16},{16,24},{1,9},{9,17},{17,25},{2,10},{10,18},{18,26},{... | collective-permute-start | bytes 786440 | tf_op jit(solution)/shard_map/ppermute | solution.py:57
  72.6 2.5 %collective-permute-done.11.refs_1_ = bf16[64,2048]{1,0:T(8,128)(2,1)S(1)} collective-permute-done((bf16[64,2048]{1,0:T(8,128)(2,1)S(1)}, bf16[64,2048]{1,0:T(8,128)(2,1)S(1)}, u32[]{:S(2)}, u32[]{:S(2)}) %collective-permute-start.11) | collective-permute-done | bytes 262176 | tf_op jit(solution)/shard_map/ppermute | solution.py:57
  (23 shorter events, 6.5 us)
Async XLA Ops:
  0.6 9.3 %copy-start.1 = (f32[1,2048]{1,0:T(1,128)S(1)}, f32[1,2048]{1,0:T(1,128)}, u32[]{:S(2)}) copy-start(f32[1,2048]{1,0:T(1,128)} %refs_4_.1) | copy-start | bytes 24580
  0.6 9.3 %copy-start = (f32[1,2048]{1,0:T(1,128)S(1)}, f32[1,2048]{1,0:T(1,128)}, u32[]{:S(2)}) copy-start(f32[1,2048]{1,0:T(1,128)} %refs_3_.4) | copy-start | bytes 24580
  1.9 13.7 %collective-permute-start = (bf16[128,2048]{1,0:T(8,128)(2,1)S(1)}, bf16[128,2048]{1,0:T(8,128)(2,1)S(1)}, u32[]{:S(2)}, u32[]{:S(2)}) collective-permute-start(bf16[128,2048]{1,0:T(8,128)(2,1)S(1)} %get-tuple-element.13.refs_0_), channel_id=1, source_target_pairs={{0,4},{4,0},{8,12},{12,8},{16,20},{20,16},{24,28},{28,24},{1,5},{5... | collective-permute-start | bytes 1572872 | tf_op jit(solution)/shard_map/ppermute | solution.py:63
  19.1 6.7 %collective-permute-start.1 = (bf16[64,2048]{1,0:T(8,128)(2,1)S(1)}, bf16[64,2048]{1,0:T(8,128)(2,1)S(1)}, u32[]{:S(2)}, u32[]{:S(2)}) collective-permute-start(bf16[64,2048]{1,0:T(8,128)(2,1)S(1)} %get-tuple-element.17), channel_id=1, source_target_pairs={{0,4},{4,0},{8,12},{12,8},{16,20},{20,16},{24,28},{28,24},{1,5},{5... | collective-permute-start | bytes 786440 | tf_op jit(solution)/shard_map/ppermute | solution.py:63
  20.4 12.7 %collective-permute-start.3 = (bf16[64,2048]{1,0:T(8,128)(2,1)S(1)}, bf16[64,2048]{1,0:T(8,128)(2,1)S(1)}, u32[]{:S(2)}, u32[]{:S(2)}) collective-permute-start(bf16[64,2048]{1,0:T(8,128)(2,1)S(1)} %get-tuple-element.18), channel_id=1, source_target_pairs={{0,4},{4,0},{8,12},{12,8},{16,20},{20,16},{24,28},{28,24},{1,5},{5... | collective-permute-start | bytes 786440 | tf_op jit(solution)/shard_map/ppermute | solution.py:63
  25.9 12.5 %collective-permute-start.2 = (bf16[64,2048]{1,0:T(8,128)(2,1)S(1)}, bf16[64,2048]{1,0:T(8,128)(2,1)S(1)}, u32[]{:S(2)}, u32[]{:S(2)}) collective-permute-start(bf16[64,2048]{1,0:T(8,128)(2,1)S(1)} %shard_map.91.refs_1_), channel_id=1, source_target_pairs={{0,8},{8,16},{16,24},{1,9},{9,17},{17,25},{2,10},{10,18},{18,26},{... | collective-permute-start | bytes 786440 | tf_op jit(solution)/shard_map/ppermute | solution.py:57
  33.1 8.5 %collective-permute-start.4 = (bf16[64,2048]{1,0:T(8,128)(2,1)S(1)}, bf16[64,2048]{1,0:T(8,128)(2,1)S(1)}, u32[]{:S(2)}, u32[]{:S(2)}) collective-permute-start(bf16[64,2048]{1,0:T(8,128)(2,1)S(1)} %shard_map.94.refs_2_), channel_id=1, source_target_pairs={{0,8},{8,16},{16,24},{1,9},{9,17},{17,25},{2,10},{10,18},{18,26},{... | collective-permute-start | bytes 786440 | tf_op jit(solution)/shard_map/ppermute | solution.py:57
  37.7 8.4 %collective-permute-start.7 = (bf16[128,2048]{1,0:T(8,128)(2,1)S(1)}, bf16[128,2048]{1,0:T(8,128)(2,1)S(1)}, u32[]{:S(2)}, u32[]{:S(2)}) collective-permute-start(bf16[128,2048]{1,0:T(8,128)(2,1)S(1)} %shard_map.92.other), channel_id=1, source_target_pairs={{0,4},{4,0},{1,5},{5,1},{2,6},{6,2},{3,7},{7,3}} | collective-permute-start | bytes 1572872 | tf_op jit(solution)/shard_map/ppermute | solution.py:63
  38.5 10.2 %collective-permute-start.5 = (bf16[64,2048]{1,0:T(8,128)(2,1)S(1)}, bf16[64,2048]{1,0:T(8,128)(2,1)S(1)}, u32[]{:S(2)}, u32[]{:S(2)}) collective-permute-start(bf16[64,2048]{1,0:T(8,128)(2,1)S(1)} %shard_map.93.refs_0_.refs_2_), channel_id=1, source_target_pairs={{8,12},{12,8},{16,20},{20,16},{24,28},{28,24},{9,13},{13,9},{17,21... | collective-permute-start | bytes 786440 | tf_op jit(solution)/shard_map/ppermute | solution.py:63
  41.6 11.0 %collective-permute-start.6 = (bf16[64,2048]{1,0:T(8,128)(2,1)S(1)}, bf16[64,2048]{1,0:T(8,128)(2,1)S(1)}, u32[]{:S(2)}, u32[]{:S(2)}) collective-permute-start(bf16[64,2048]{1,0:T(8,128)(2,1)S(1)} %shard_map.95.refs_1_.refs_2_), channel_id=1, source_target_pairs={{8,12},{12,8},{16,20},{20,16},{24,28},{28,24},{9,13},{13,9},{17,21... | collective-permute-start | bytes 786440 | tf_op jit(solution)/shard_map/ppermute | solution.py:63
  56.1 8.4 %collective-permute-start.8 = (bf16[64,2048]{1,0:T(8,128)(2,1)S(1)}, bf16[64,2048]{1,0:T(8,128)(2,1)S(1)}, u32[]{:S(2)}, u32[]{:S(2)}) collective-permute-start(bf16[64,2048]{1,0:T(8,128)(2,1)S(1)} %get-tuple-element.20), channel_id=1, source_target_pairs={{0,4},{4,0},{8,12},{12,8},{16,20},{20,16},{24,28},{28,24},{1,5},{5... | collective-permute-start | bytes 786440 | tf_op jit(solution)/shard_map/ppermute | solution.py:63
  57.4 12.3 %collective-permute-start.9 = (bf16[64,2048]{1,0:T(8,128)(2,1)S(1)}, bf16[64,2048]{1,0:T(8,128)(2,1)S(1)}, u32[]{:S(2)}, u32[]{:S(2)}) collective-permute-start(bf16[64,2048]{1,0:T(8,128)(2,1)S(1)} %get-tuple-element.21), channel_id=1, source_target_pairs={{0,4},{4,0},{8,12},{12,8},{16,20},{20,16},{24,28},{28,24},{1,5},{5... | collective-permute-start | bytes 786440 | tf_op jit(solution)/shard_map/ppermute | solution.py:63
  64.6 8.0 %collective-permute-start.10 = (bf16[64,2048]{1,0:T(8,128)(2,1)S(1)}, bf16[64,2048]{1,0:T(8,128)(2,1)S(1)}, u32[]{:S(2)}, u32[]{:S(2)}) collective-permute-start(bf16[64,2048]{1,0:T(8,128)(2,1)S(1)} %shard_map.101.refs_0_), channel_id=1, source_target_pairs={{0,8},{8,16},{16,24},{1,9},{9,17},{17,25},{2,10},{10,18},{18,26},{... | collective-permute-start | bytes 786440 | tf_op jit(solution)/shard_map/ppermute | solution.py:57
  69.8 5.2 %collective-permute-start.11 = (bf16[64,2048]{1,0:T(8,128)(2,1)S(1)}, bf16[64,2048]{1,0:T(8,128)(2,1)S(1)}, u32[]{:S(2)}, u32[]{:S(2)}) collective-permute-start(bf16[64,2048]{1,0:T(8,128)(2,1)S(1)} %shard_map.102.refs_1_), channel_id=1, source_target_pairs={{0,8},{8,16},{16,24},{1,9},{9,17},{17,25},{2,10},{10,18},{18,26},{... | collective-permute-start | bytes 786440 | tf_op jit(solution)/shard_map/ppermute | solution.py:57

commit v5 on v4

--- a/solution.py
+++ b/solution.py
@@ -9,7 +9,7 @@
 
 
 HD = 128
-PARTS = 2
+SHARES = ((1, 1), (2, 1, 1))
 MIB = 1 << 20
 F32 = jnp.float32
 BF16 = jnp.bfloat16
@@ -54,13 +54,22 @@
 
 def from_behind(block, axis):
     size = lax.axis_size(axis)
-    return lax.ppermute(block, axis, [(i, i + 1) for i in range(size - 1)])
-
-
-def rotate(block, shift, sections):
-    size = lax.axis_size("tensor")
-    route = [(s * size + i, s * size + (i + shift) % size) for s in sections for i in range(size)]
-    return held_inside(lax.ppermute(block, ("section", "tensor"), route))
+    return lax.ppermute(block, axis, [(i, (i + 1) % size) for i in range(size)])
+
+
+def rotate(block, shift, sections, rest=False):
+    names = ("section", "tensor", "dp")
+    count, size, groups = map(lax.axis_size, names)
+    route = []
+    for s in range(count):
+        for i in range(size):
+            for d in range(groups):
+                here = (s * size + i) * groups + d
+                if s in sections:
+                    route.append((here, (s * size + (i + shift) % size) * groups + d))
+                elif rest and d ^ 1 < groups:
+                    route.append((here, here - d + (d ^ 1)))
+    return held_inside(lax.ppermute(block, names, route))
 
 
 def pick_kernel(order, acts, current, kept, slots, sems):
@@ -213,40 +222,33 @@
         copy.wait()
 
 
-def last_kernel(parts, order, *refs):
-    chunks, out, sems = refs[:parts], refs[-2], refs[-1]
-    first = lax.axis_index("section") == 0
-
-    @pl.when(jnp.logical_not(first))
+def last_kernel(pieces, order, *refs):
+    chunks, out, sems = refs[: len(pieces)], refs[-2], refs[-1]
+
+    @pl.when(lax.axis_index("section") > 0)
     def _():
         copies = []
-        at = 0
-        for i, chunk in enumerate(chunks):
-            rows = pl.ds(at, chunk.shape[0])
-            target = out.at[0, order[0, 1], rows]
+        for i, (chunk, (start, size)) in enumerate(zip(chunks, pieces)):
+            target = out.at[0, order[0, 1], pl.ds(start, size)]
             copies.append(pltpu.make_async_copy(chunk, target, sems.at[i]))
-            at += chunk.shape[0]
         for copy in copies:
             copy.start()
         for copy in copies:
             copy.wait()
 
 
-def cuts(rows):
-    units = rows // 16
-    parts = min(PARTS, units)
-    sizes = [(units // parts + (i < units % parts)) * 16 for i in range(parts)]
+def cuts(rows, shares):
+    sizes = [max(16, rows * share // sum(shares)) for share in shares]
     return [(sum(sizes[:i]), size) for i, size in enumerate(sizes)]
 
 
-def layer(chunks, gain, bias, w_in, w_out, alone=(), early=()):
+def layer(pieces, chunks, got, gain, bias, w_in, w_out, alone=()):
     size = lax.axis_size("tensor")
     sections = range(lax.axis_size("section"))
     parts = len(chunks)
     rows = sum(c.shape[0] for c in chunks)
     wide, deep = w_in.shape[1], w_out.shape[0]
     width = w_in.shape[0]
-    got = [rotate(c, j, sections[1:] if alone else sections) for j in range(1, size) for c in chunks]
     mine = call(
         functools.partial(own_qkv_kernel, parts),
         inner((rows, wide)),
@@ -257,7 +259,6 @@
         scratch=[inner((rows, width))],
     )
     far = (size - 1) * rows
-    pieces = cuts(rows)
     count = (size - 1) * len(pieces)
     theirs, *sends = call(
         functools.partial(others_kernel, len(got), count, len(alone)),
@@ -267,12 +268,11 @@
         [*got, *alone, gain, bias, w_in, w_out, mine],
         flops=2 * far * width * wide,
         scratch=[inner((far, width)), inner((far, deep))],
-        wait=early,
-    )
-    returned = [
-        [rotate(sends[(j - 1) * len(pieces) + i], -j, sections) for j in range(1, size)]
-        for i in range(len(pieces))
-    ]
+    )
+    returned = []
+    for i in range(len(pieces)):
+        parts_of_i = [rotate(sends[(j - 1) * len(pieces) + i], -j, sections) for j in range(1, size)]
+        returned.append(parts_of_i)
     own = call(
         own_kernel,
         inner((rows, width)),
@@ -298,15 +298,7 @@
         [order, acts],
         scratch=[inner(acts.shape[1:]), dma((2,))],
     )
-    other = call(
-        other_kernel,
-        inner((rows, width)),
-        VMEM,
-        [SMEM, ANY, ANY],
-        [order, acts, fresh],
-        scratch=[dma((2,))],
-    )
-    alone = [rotate(other, j, [0]) for j in range(1, lax.axis_size("tensor"))]
+    other = call(other_kernel, inner((rows, width)), VMEM, [SMEM, ANY, ANY], [order, acts, fresh], scratch=[dma((2,))])
     w_in, w_out = call(
         weights_kernel,
         [inner(wqkv.shape[1:]), inner(wo.shape[1:])],
@@ -317,12 +309,18 @@
         limit=24,
         flops=1 << 30,
     )
+    shifts = range(1, lax.axis_size("tensor"))
+    sections = range(lax.axis_size("section"))
     chunks = [current]
-    pieces = cuts(rows)
-    parts = len(pieces)
+    got = [rotate(current, j, sections) for j in shifts]
+    alone = [rotate(other, j, [0]) for j in shifts]
     section_out = held = None
     for tick in range(ticks):
-        own, returned = layer(chunks, ln_gain, ln_bias, w_in, w_out, alone if tick else ())
+        here_at = [sum(c.shape[0] for c in chunks[:i]) for i in range(len(chunks))]
+        if tick:
+            before, parts = arrived, len(arrived)
+        pieces = cuts(rows, SHARES[tick])
+        own, returned = layer(pieces, chunks, got, ln_gain, ln_bias, w_in, w_out, alone if tick else ())
         ready = []
         if tick:
             section_out = call(
@@ -339,7 +337,7 @@
                 pltpu.HBM(acts.shape, BF16),
                 VMEM,
                 [SMEM, VMEM, VMEM] + [VMEM] * parts,
-                [order, acts, fresh, *arrived],
+                [order, acts, fresh, *before],
                 wait=[own],
             )
             section_out, held = outside(section_out), outside(held)
@@ -347,49 +345,55 @@
         results, arrived = [], []
         for i, (start, size) in enumerate(pieces):
 
-            def combine(*refs, start=start, size=size, whole=len(chunks) == 1):
-                here = refs[0].at[pl.ds(start, size)] if whole else refs[0]
-                combine_kernel(start, here, *refs[1:])
+            holder = max(k for k, at in enumerate(here_at) if at <= start)
+
+            def combine(*refs, start=start, size=size, at=here_at[holder]):
+                combine_kernel(start, refs[0].at[pl.ds(start - at, size)], *refs[1:])
 
             result = call(
                 combine,
                 inner((size, width)),
                 VMEM,
                 [VMEM] * (2 + len(returned[i])),
-                [chunks[min(i, len(chunks) - 1)], own, *returned[i]],
+                [chunks[holder], own, *returned[i]],
                 wait=ready,
             )
             results.append(result)
             arrived.append(held_inside(from_behind(result, "section")))
         if tick == 0:
-            chunks = [
-                call(
-                    functools.partial(next_kernel, start),
-                    inner((size, width)),
-                    VMEM,
-                    [SMEM, VMEM, VMEM],
-                    [order, arrived[i], other],
+            chunks, swapped = [], []
+            for i, (start, size) in enumerate(pieces):
+                chunks.append(
+                    call(
+                        functools.partial(next_kernel, start),
+                        inner((size, width)),
+                        VMEM,
+                        [SMEM, VMEM, VMEM],
+                        [order, arrived[i], other],
+                    )
                 )
-                for i, (start, size) in enumerate(pieces)
-            ]
+                swapped.append([rotate(chunks[i], j, sections[1:], rest=True) for j in shifts])
+            got = [block for of_j in zip(*swapped) for block in of_j]
+    parts = len(pieces)
     section_out = call(
         functools.partial(put_kernel, ticks - 1, parts),
-        jax.ShapeDtypeStruct((ticks, 1, rows, width), BF16),
+        pltpu.HBM((ticks, 1, rows, width), BF16),
         ANY,
         [VMEM] * parts + [ANY],
         [*results, section_out],
         scratch=[dma((parts,))],
         aliases={parts: 0},
     )
-    held = call(
-        functools.partial(last_kernel, parts),
-        jax.ShapeDtypeStruct(acts.shape, BF16),
-        ANY,
-        [SMEM] + [VMEM] * parts + [ANY],
-        [order, *arrived, held],
-        scratch=[dma((parts,))],
-        aliases={parts + 1: 0},
-    )
+    for which in (range(parts - 1), range(parts - 1, parts)):
+        held = call(
+            functools.partial(last_kernel, [pieces[i] for i in which]),
+            pltpu.HBM(acts.shape, BF16),
+            ANY,
+            [SMEM] + [VMEM] * len(which) + [ANY],
+            [order, *(arrived[i] for i in which), outside(held)],
+            scratch=[dma((len(which),))],
+            aliases={len(which) + 1: 0},
+        )
     return section_out, held
 
 

time: 76.3 us -> 73.3 us (0.961)
  the two profiles are of different devices: /device:TPU:1 before, /device:TPU:0 now
where the time goes in v5:
time: 73.3 us; the launch traced here: 73 us
  waiting for transfers between devices  29.1 us (40%)
  Pallas kernels  27.7 us (38%)
  starting transfers between devices  15.2 us (21%)
  between operations  1.01 us (1%)
    pallas_call x21, Pallas kernels, call(): pl.pallas_call(kernel, out_shape=outs, out_specs=out_specs, in_specs=in_s...  27.7 us
    ppermute x9, waiting for transfers between devices, rotate(): return held_inside(lax.ppermute(block, names, route))  25.6 us
    ppermute x9, starting transfers between devices, rotate(): return held_inside(lax.ppermute(block, names, route))  15 us
    ppermute x5, waiting for transfers between devices, from_behind(): return lax.ppermute(block, axis, [(i, (i + 1) % size) for i in range(size)])  3.53 us
  transfers between devices with their start and end apart: 14, of which 9 were waited for; matrix products, arithmetic and copies ran while one was open for 0% of the time, Pallas kernels for 27%

profile of v5, /device:TPU:0, one launch (start us, length us, event | category | flops | bytes accessed | tf_op | source)
XLA Modules:
  0.0 73.0 jit_solution(7953539285415903730)
XLA Ops:
  0.7 1.3 %shard_map.86 = (bf16[128,2048]{1,0:T(8,128)(2,1)S(1)}, s32[1,2]{1,0:T(1,128)S(4)}) custom-call(s32[1,2]{1,0:T(1,128)} %order.1, bf16[1,2,128,2048]{3,2,1,0:T(8,128)(2,1)} %refs_2_.7), custom_call_target="tpu_custom_call" | custom-call | flops 1048576 | bytes 65536 | tf_op jit(solution)/shard_map/pallas_call | solution.py:43
  1.9 3.0 %collective-permute-start = (bf16[128,2048]{1,0:T(8,128)(2,1)S(1)}, bf16[128,2048]{1,0:T(8,128)(2,1)S(1)}, u32[]{:S(2)}, u32[]{:S(2)}) collective-permute-start(bf16[128,2048]{1,0:T(8,128)(2,1)S(1)} %get-tuple-element.14.refs_0_), channel_id=1, source_target_pairs={{0,4},{1,5},{2,6},{3,7},{4,0},{5,1},{6,2},{7,3},{8,12},{9,13},{10,... | collective-permute-start | bytes 1572872 | tf_op jit(solution)/shard_map/ppermute | solution.py:72
  5.0 5.9 %shard_map.87 = (bf16[2048,3072]{1,0:T(8,128)(2,1)S(1)}, bf16[1024,2048]{1,0:T(8,128)(2,1)S(1)}) custom-call(bf16[1,2048,3072]{2,1,0:T(8,128)(2,1)} %w_in.1, bf16[1,1024,2048]{2,1,0:T(8,128)(2,1)} %w_out.1), custom_call_target="tpu_custom_call" | custom-call | flops 1073741824 | bytes 65536 | tf_op jit(solution)/shard_map/pallas_call | solution.py:43
  10.9 2.1 %shard_map.88.refs_5_.mine = bf16[128,3072]{1,0:T(8,128)(2,1)S(1)} custom-call(bf16[128,2048]{1,0:T(8,128)(2,1)S(1)} %get-tuple-element.14.refs_0_, f32[1,2048]{1,0:T(1,128)S(1)} %copy-done, f32[1,2048]{1,0:T(1,128)S(1)} %copy-done.1, bf16[2048,3072]{1,0:T(8,128)(2,1)S(1)} %get-tuple-element.15.refs_3_.refs_4_.refs_5_), custom_call_target="tpu_custom_call" | custom-call | flops 1610612736 | bytes 65536 | tf_op jit(solution)/shard_map/pallas_call | solution.py:43
  13.0 3.9 %collective-permute-done.refs_0_ = bf16[128,2048]{1,0:T(8,128)(2,1)S(1)} collective-permute-done((bf16[128,2048]{1,0:T(8,128)(2,1)S(1)}, bf16[128,2048]{1,0:T(8,128)(2,1)S(1)}, u32[]{:S(2)}, u32[]{:S(2)}) %collective-permute-start) | collective-permute-done | bytes 524320 | tf_op jit(solution)/shard_map/ppermute | solution.py:72
  16.9 3.4 %shard_map.89 = (bf16[128,3072]{1,0:T(8,128)(2,1)S(1)}, bf16[64,2048]{1,0:T(8,128)(2,1)S(1)}, bf16[64,2048]{1,0:T(8,128)(2,1)S(1)}) custom-call(bf16[128,2048]{1,0:T(8,128)(2,1)S(1)} %collective-permute-done.refs_0_, f32[1,2048]{1,0:T(1,128)S(1)} %copy-done, f32[1,2048]{1,0:T(1,128)S(1)} %copy-done.1, ...), custom_call_target="tpu_custom_call" | custom-call | flops 1610612736 | bytes 65536 | tf_op jit(solution)/shard_map/pallas_call | solution.py:43
  20.4 1.8 %collective-permute-start.1 = (bf16[64,2048]{1,0:T(8,128)(2,1)S(1)}, bf16[64,2048]{1,0:T(8,128)(2,1)S(1)}, u32[]{:S(2)}, u32[]{:S(2)}) collective-permute-start(bf16[64,2048]{1,0:T(8,128)(2,1)S(1)} %get-tuple-element.18), channel_id=1, source_target_pairs={{0,4},{1,5},{2,6},{3,7},{4,0},{5,1},{6,2},{7,3},{8,12},{9,13},{10,... | collective-permute-start | bytes 786440 | tf_op jit(solution)/shard_map/ppermute | solution.py:72
  22.4 1.7 %shard_map.90.refs_1_ = bf16[128,2048]{1,0:T(8,128)(2,1)S(1)} custom-call(bf16[128,3072]{1,0:T(8,128)(2,1)S(1)} %shard_map.88.refs_5_.mine, bf16[128,3072]{1,0:T(8,128)(2,1)S(1)} %get-tuple-element.17.theirs, bf16[1024,2048]{1,0:T(8,128)(2,1)S(1)} %get-tuple-element.16.refs_4_.w_out.refs_6_), custom_call_target="tpu_custom_call" | custom-call | flops 536870912 | bytes 65536 | tf_op jit(solution)/shard_map/pallas_call | solution.py:43
  24.2 5.4 %collective-permute-done.1.refs_2_ = bf16[64,2048]{1,0:T(8,128)(2,1)S(1)} collective-permute-done((bf16[64,2048]{1,0:T(8,128)(2,1)S(1)}, bf16[64,2048]{1,0:T(8,128)(2,1)S(1)}, u32[]{:S(2)}, u32[]{:S(2)}) %collective-permute-start.1) | collective-permute-done | bytes 262176 | tf_op jit(solution)/shard_map/ppermute | solution.py:72
  29.8 3.7 %collective-permute-done.3.refs_2_ = bf16[64,2048]{1,0:T(8,128)(2,1)S(1)} collective-permute-done((bf16[64,2048]{1,0:T(8,128)(2,1)S(1)}, bf16[64,2048]{1,0:T(8,128)(2,1)S(1)}, u32[]{:S(2)}, u32[]{:S(2)}) %collective-permute-start.3) | collective-permute-done | bytes 262176 | tf_op jit(solution)/shard_map/ppermute | solution.py:72
  34.8 3.5 %collective-permute-start.7 = (bf16[128,2048]{1,0:T(8,128)(2,1)S(1)}, bf16[128,2048]{1,0:T(8,128)(2,1)S(1)}, u32[]{:S(2)}, u32[]{:S(2)}) collective-permute-start(bf16[128,2048]{1,0:T(8,128)(2,1)S(1)} %shard_map.92.other), channel_id=1, source_target_pairs={{0,4},{1,5},{2,6},{3,7},{4,0},{5,1},{6,2},{7,3}} | collective-permute-start | bytes 1572872 | tf_op jit(solution)/shard_map/ppermute | solution.py:72
  38.4 1.6 %collective-permute-start.5 = (bf16[64,2048]{1,0:T(8,128)(2,1)S(1)}, bf16[64,2048]{1,0:T(8,128)(2,1)S(1)}, u32[]{:S(2)}, u32[]{:S(2)}) collective-permute-start(bf16[64,2048]{1,0:T(8,128)(2,1)S(1)} %shard_map.93.refs_0_.refs_2_), channel_id=1, source_target_pairs={{0,1},{1,0},{2,3},{3,2},{4,5},{5,4},{6,7},{7,6},{8,12},{9,13},{10,... | collective-permute-start | bytes 786440 | tf_op jit(solution)/shard_map/ppermute | solution.py:72
  40.0 1.1 %collective-permute-start.6 = (bf16[64,2048]{1,0:T(8,128)(2,1)S(1)}, bf16[64,2048]{1,0:T(8,128)(2,1)S(1)}, u32[]{:S(2)}, u32[]{:S(2)}) collective-permute-start(bf16[64,2048]{1,0:T(8,128)(2,1)S(1)} %shard_map.95.refs_1_.refs_2_), channel_id=1, source_target_pairs={{0,1},{1,0},{2,3},{3,2},{4,5},{5,4},{6,7},{7,6},{8,12},{9,13},{10,... | collective-permute-start | bytes 786440 | tf_op jit(solution)/shard_map/ppermute | solution.py:72
  41.1 2.1 %shard_map.96.refs_7_.mine = bf16[128,3072]{1,0:T(8,128)(2,1)S(1)} custom-call(bf16[64,2048]{1,0:T(8,128)(2,1)S(1)} %shard_map.93.refs_0_.refs_2_, bf16[64,2048]{1,0:T(8,128)(2,1)S(1)} %shard_map.95.refs_1_.refs_2_, f32[1,2048]{1,0:T(1,128)S(1)} %copy-done, f32[1,2048]{1,0:T(1,128)S(1)} %copy-done.1, ...), custom_call_target="tpu_custom_call" | custom-call | flops 1610612736 | bytes 65536 | tf_op jit(solution)/shard_map/pallas_call | solution.py:43
  43.2 7.9 %collective-permute-done.7.refs_2_ = bf16[128,2048]{1,0:T(8,128)(2,1)S(1)} collective-permute-done((bf16[128,2048]{1,0:T(8,128)(2,1)S(1)}, bf16[128,2048]{1,0:T(8,128)(2,1)S(1)}, u32[]{:S(2)}, u32[]{:S(2)}) %collective-permute-start.7) | collective-permute-done | bytes 524320 | tf_op jit(solution)/shard_map/ppermute | solution.py:72
  51.2 3.5 %shard_map.97 = (bf16[128,3072]{1,0:T(8,128)(2,1)S(1)}, bf16[64,2048]{1,0:T(8,128)(2,1)S(1)}, bf16[32,2048]{1,0:T(8,128)(2,1)S(1)}, bf16[32,2048]{1,0:T(8,128)(2,1)S(1)}) custom-call(bf16[64,2048]{1,0:T(8,128)(2,1)S(1)} %collective-permute-done.5.refs_0_, bf16[64,2048]{1,0:T(8,128)(2,1)S(1)} %collective-permute-done.6.refs_1_, ...), custom_call_target="tpu_custom_call" | custom-call | flops 1610612736 | bytes 65536 | tf_op jit(solution)/shard_map/pallas_call | solution.py:43
  54.6 1.5 %collective-permute-start.8 = (bf16[64,2048]{1,0:T(8,128)(2,1)S(1)}, bf16[64,2048]{1,0:T(8,128)(2,1)S(1)}, u32[]{:S(2)}, u32[]{:S(2)}) collective-permute-start(bf16[64,2048]{1,0:T(8,128)(2,1)S(1)} %get-tuple-element.21), channel_id=1, source_target_pairs={{0,4},{1,5},{2,6},{3,7},{4,0},{5,1},{6,2},{7,3},{8,12},{9,13},{10,... | collective-permute-start | bytes 786440 | tf_op jit(solution)/shard_map/ppermute | solution.py:72
  56.7 1.5 %collective-permute-start.10 = (bf16[32,2048]{1,0:T(8,128)(2,1)S(1)}, bf16[32,2048]{1,0:T(8,128)(2,1)S(1)}, u32[]{:S(2)}, u32[]{:S(2)}) collective-permute-start(bf16[32,2048]{1,0:T(8,128)(2,1)S(1)} %get-tuple-element.23), channel_id=1, source_target_pairs={{0,4},{1,5},{2,6},{3,7},{4,0},{5,1},{6,2},{7,3},{8,12},{9,13},{10,... | collective-permute-start | bytes 393224 | tf_op jit(solution)/shard_map/ppermute | solution.py:72
  58.2 1.7 %shard_map.98.refs_0_.refs_3_ = bf16[128,2048]{1,0:T(8,128)(2,1)S(1)} custom-call(bf16[128,3072]{1,0:T(8,128)(2,1)S(1)} %shard_map.96.refs_7_.mine, bf16[128,3072]{1,0:T(8,128)(2,1)S(1)} %get-tuple-element.20.theirs, bf16[1024,2048]{1,0:T(8,128)(2,1)S(1)} %get-tuple-element.16.refs_4_.w_out.refs_6_), custom_call_target="tpu_custom_call" | custom-call | flops 536870912 | bytes 65536 | tf_op jit(solution)/shard_map/pallas_call | solution.py:43
  60.8 2.7 %shard_map.100.refs_1_.refs_2_ = bf16[1,2,128,2048]{3,2,1,0:T(8,128)(2,1)} custom-call(bf16[128,2048]{1,0:T(8,128)(2,1)S(1)} %shard_map.98.refs_0_.refs_3_, s32[1,2]{1,0:T(1,128)S(4)} %get-tuple-element.13.order.refs_1_, bf16[1,2,128,2048]{3,2,1,0:T(8,128)(2,1)} %refs_2_.7, bf16[2,128,2048]{2,1,0:T(8,128)(2,1)} %refs_3_.5, ...), custom_call_target="tpu_custom_call" | custom-call | flops 1048576 | bytes 65536 | tf_op jit(solution)/shard_map/pallas_call | solution.py:43
  64.0 2.6 %collective-permute-done.9.refs_4_ = bf16[32,2048]{1,0:T(8,128)(2,1)S(1)} collective-permute-done((bf16[32,2048]{1,0:T(8,128)(2,1)S(1)}, bf16[32,2048]{1,0:T(8,128)(2,1)S(1)}, u32[]{:S(2)}, u32[]{:S(2)}) %collective-permute-start.9) | collective-permute-done | bytes 131104 | tf_op jit(solution)/shard_map/ppermute | solution.py:72
  66.8 1.5 %collective-permute-done.10.refs_4_ = bf16[32,2048]{1,0:T(8,128)(2,1)S(1)} collective-permute-done((bf16[32,2048]{1,0:T(8,128)(2,1)S(1)}, bf16[32,2048]{1,0:T(8,128)(2,1)S(1)}, u32[]{:S(2)}, u32[]{:S(2)}) %collective-permute-start.10) | collective-permute-done | bytes 131104 | tf_op jit(solution)/shard_map/ppermute | solution.py:72
  69.3 2.0 %collective-permute-done.13.refs_1_ = bf16[32,2048]{1,0:T(8,128)(2,1)S(1)} collective-permute-done((bf16[32,2048]{1,0:T(8,128)(2,1)S(1)}, bf16[32,2048]{1,0:T(8,128)(2,1)S(1)}, u32[]{:S(2)}, u32[]{:S(2)}) %collective-permute-start.13) | collective-permute-done | bytes 131104 | tf_op jit(solution)/shard_map/ppermute | solution.py:57
  71.3 1.6 %collective-permute-done.11.refs_0_ = bf16[32,2048]{1,0:T(8,128)(2,1)S(1)} collective-permute-done((bf16[32,2048]{1,0:T(8,128)(2,1)S(1)}, bf16[32,2048]{1,0:T(8,128)(2,1)S(1)}, u32[]{:S(2)}, u32[]{:S(2)}) %collective-permute-start.11) | collective-permute-done | bytes 131104 | tf_op jit(solution)/shard_map/ppermute | solution.py:57
  (29 shorter events, 4.7 us)
Async XLA Ops:
  0.6 10.2 %copy-start.1 = (f32[1,2048]{1,0:T(1,128)S(1)}, f32[1,2048]{1,0:T(1,128)}, u32[]{:S(2)}) copy-start(f32[1,2048]{1,0:T(1,128)} %refs_4_.1) | copy-start | bytes 24580
  0.6 10.2 %copy-start = (f32[1,2048]{1,0:T(1,128)S(1)}, f32[1,2048]{1,0:T(1,128)}, u32[]{:S(2)}) copy-start(f32[1,2048]{1,0:T(1,128)} %refs_3_.4) | copy-start | bytes 24580
  1.9 15.0 %collective-permute-start = (bf16[128,2048]{1,0:T(8,128)(2,1)S(1)}, bf16[128,2048]{1,0:T(8,128)(2,1)S(1)}, u32[]{:S(2)}, u32[]{:S(2)}) collective-permute-start(bf16[128,2048]{1,0:T(8,128)(2,1)S(1)} %get-tuple-element.14.refs_0_), channel_id=1, source_target_pairs={{0,4},{1,5},{2,6},{3,7},{4,0},{5,1},{6,2},{7,3},{8,12},{9,13},{10,... | collective-permute-start | bytes 1572872 | tf_op jit(solution)/shard_map/ppermute | solution.py:72
  20.4 9.2 %collective-permute-start.1 = (bf16[64,2048]{1,0:T(8,128)(2,1)S(1)}, bf16[64,2048]{1,0:T(8,128)(2,1)S(1)}, u32[]{:S(2)}, u32[]{:S(2)}) collective-permute-start(bf16[64,2048]{1,0:T(8,128)(2,1)S(1)} %get-tuple-element.18), channel_id=1, source_target_pairs={{0,4},{1,5},{2,6},{3,7},{4,0},{5,1},{6,2},{7,3},{8,12},{9,13},{10,... | collective-permute-start | bytes 786440 | tf_op jit(solution)/shard_map/ppermute | solution.py:72
  22.2 11.3 %collective-permute-start.3 = (bf16[64,2048]{1,0:T(8,128)(2,1)S(1)}, bf16[64,2048]{1,0:T(8,128)(2,1)S(1)}, u32[]{:S(2)}, u32[]{:S(2)}) collective-permute-start(bf16[64,2048]{1,0:T(8,128)(2,1)S(1)} %get-tuple-element.19), channel_id=1, source_target_pairs={{0,4},{1,5},{2,6},{3,7},{4,0},{5,1},{6,2},{7,3},{8,12},{9,13},{10,... | collective-permute-start | bytes 786440 | tf_op jit(solution)/shard_map/ppermute | solution.py:72
  29.7 8.6 %collective-permute-start.2 = (bf16[64,2048]{1,0:T(8,128)(2,1)S(1)}, bf16[64,2048]{1,0:T(8,128)(2,1)S(1)}, u32[]{:S(2)}, u32[]{:S(2)}) collective-permute-start(bf16[64,2048]{1,0:T(8,128)(2,1)S(1)} %shard_map.91.refs_1_), channel_id=1, source_target_pairs={{0,8},{8,16},{16,24},{24,0},{1,9},{9,17},{17,25},{25,1},{2,10},{10... | collective-permute-start | bytes 786440 | tf_op jit(solution)/shard_map/ppermute | solution.py:57
  33.6 6.4 %collective-permute-start.4 = (bf16[64,2048]{1,0:T(8,128)(2,1)S(1)}, bf16[64,2048]{1,0:T(8,128)(2,1)S(1)}, u32[]{:S(2)}, u32[]{:S(2)}) collective-permute-start(bf16[64,2048]{1,0:T(8,128)(2,1)S(1)} %shard_map.94.refs_2_), channel_id=1, source_target_pairs={{0,8},{8,16},{16,24},{24,0},{1,9},{9,17},{17,25},{25,1},{2,10},{10... | collective-permute-start | bytes 786440 | tf_op jit(solution)/shard_map/ppermute | solution.py:57
  34.8 16.4 %collective-permute-start.7 = (bf16[128,2048]{1,0:T(8,128)(2,1)S(1)}, bf16[128,2048]{1,0:T(8,128)(2,1)S(1)}, u32[]{:S(2)}, u32[]{:S(2)}) collective-permute-start(bf16[128,2048]{1,0:T(8,128)(2,1)S(1)} %shard_map.92.other), channel_id=1, source_target_pairs={{0,4},{1,5},{2,6},{3,7},{4,0},{5,1},{6,2},{7,3}} | collective-permute-start | bytes 1572872 | tf_op jit(solution)/shard_map/ppermute | solution.py:72
  38.4 12.8 %collective-permute-start.5 = (bf16[64,2048]{1,0:T(8,128)(2,1)S(1)}, bf16[64,2048]{1,0:T(8,128)(2,1)S(1)}, u32[]{:S(2)}, u32[]{:S(2)}) collective-permute-start(bf16[64,2048]{1,0:T(8,128)(2,1)S(1)} %shard_map.93.refs_0_.refs_2_), channel_id=1, source_target_pairs={{0,1},{1,0},{2,3},{3,2},{4,5},{5,4},{6,7},{7,6},{8,12},{9,13},{10,... | collective-permute-start | bytes 786440 | tf_op jit(solution)/shard_map/ppermute | solution.py:72
  40.0 11.1 %collective-permute-start.6 = (bf16[64,2048]{1,0:T(8,128)(2,1)S(1)}, bf16[64,2048]{1,0:T(8,128)(2,1)S(1)}, u32[]{:S(2)}, u32[]{:S(2)}) collective-permute-start(bf16[64,2048]{1,0:T(8,128)(2,1)S(1)} %shard_map.95.refs_1_.refs_2_), channel_id=1, source_target_pairs={{0,1},{1,0},{2,3},{3,2},{4,5},{5,4},{6,7},{7,6},{8,12},{9,13},{10,... | collective-permute-start | bytes 786440 | tf_op jit(solution)/shard_map/ppermute | solution.py:72
  54.6 9.2 %collective-permute-start.8 = (bf16[64,2048]{1,0:T(8,128)(2,1)S(1)}, bf16[64,2048]{1,0:T(8,128)(2,1)S(1)}, u32[]{:S(2)}, u32[]{:S(2)}) collective-permute-start(bf16[64,2048]{1,0:T(8,128)(2,1)S(1)} %get-tuple-element.21), channel_id=1, source_target_pairs={{0,4},{1,5},{2,6},{3,7},{4,0},{5,1},{6,2},{7,3},{8,12},{9,13},{10,... | collective-permute-start | bytes 786440 | tf_op jit(solution)/shard_map/ppermute | solution.py:72
  56.2 10.5 %collective-permute-start.9 = (bf16[32,2048]{1,0:T(8,128)(2,1)S(1)}, bf16[32,2048]{1,0:T(8,128)(2,1)S(1)}, u32[]{:S(2)}, u32[]{:S(2)}) collective-permute-start(bf16[32,2048]{1,0:T(8,128)(2,1)S(1)} %get-tuple-element.22), channel_id=1, source_target_pairs={{0,4},{1,5},{2,6},{3,7},{4,0},{5,1},{6,2},{7,3},{8,12},{9,13},{10,... | collective-permute-start | bytes 393224 | tf_op jit(solution)/shard_map/ppermute | solution.py:72
  56.7 11.6 %collective-permute-start.10 = (bf16[32,2048]{1,0:T(8,128)(2,1)S(1)}, bf16[32,2048]{1,0:T(8,128)(2,1)S(1)}, u32[]{:S(2)}, u32[]{:S(2)}) collective-permute-start(bf16[32,2048]{1,0:T(8,128)(2,1)S(1)} %get-tuple-element.23), channel_id=1, source_target_pairs={{0,4},{1,5},{2,6},{3,7},{4,0},{5,1},{6,2},{7,3},{8,12},{9,13},{10,... | collective-permute-start | bytes 393224 | tf_op jit(solution)/shard_map/ppermute | solution.py:72
  64.0 7.3 %collective-permute-start.12 = (bf16[64,2048]{1,0:T(8,128)(2,1)S(1)}, bf16[64,2048]{1,0:T(8,128)(2,1)S(1)}, u32[]{:S(2)}, u32[]{:S(2)}) collective-permute-start(bf16[64,2048]{1,0:T(8,128)(2,1)S(1)} %shard_map.101.refs_0_), channel_id=1, source_target_pairs={{0,8},{8,16},{16,24},{24,0},{1,9},{9,17},{17,25},{25,1},{2,10},{10... | collective-permute-start | bytes 786440 | tf_op jit(solution)/shard_map/ppermute | solution.py:57
  66.7 4.5 %collective-permute-start.13 = (bf16[32,2048]{1,0:T(8,128)(2,1)S(1)}, bf16[32,2048]{1,0:T(8,128)(2,1)S(1)}, u32[]{:S(2)}, u32[]{:S(2)}) collective-permute-start(bf16[32,2048]{1,0:T(8,128)(2,1)S(1)} %shard_map.102.refs_1_), channel_id=1, source_target_pairs={{0,8},{8,16},{16,24},{24,0},{1,9},{9,17},{17,25},{25,1},{2,10},{10... | collective-permute-start | bytes 393224 | tf_op jit(solution)/shard_map/ppermute | solution.py:57
  68.4 4.4 %collective-permute-start.11 = (bf16[32,2048]{1,0:T(8,128)(2,1)S(1)}, bf16[32,2048]{1,0:T(8,128)(2,1)S(1)}, u32[]{:S(2)}, u32[]{:S(2)}) collective-permute-start(bf16[32,2048]{1,0:T(8,128)(2,1)S(1)} %shard_map.103.refs_2_), channel_id=1, source_target_pairs={{0,8},{8,16},{16,24},{24,0},{1,9},{9,17},{17,25},{25,1},{2,10},{10... | collective-permute-start | bytes 393224 | tf_op jit(solution)/shard_map/ppermute | solution.py:57

commit v6 on v5

--- a/solution.py
+++ b/solution.py
@@ -52,9 +52,12 @@
     )(*args)
 
 
-def from_behind(block, axis):
+RING = (False, True)
+
+
+def from_behind(block, axis, ring):
     size = lax.axis_size(axis)
-    return lax.ppermute(block, axis, [(i, (i + 1) % size) for i in range(size)])
+    return lax.ppermute(block, axis, [(i, (i + 1) % size) for i in range(size - 1 + ring)])
 
 
 def rotate(block, shift, sections, rest=False):
@@ -129,17 +132,16 @@
 
 def attend(q, blocks, rows, mixed):
     heads = q.shape[1] // (3 * HD)
+    ones = jnp.ones((sum(b.shape[0] for b in blocks), HD), BF16)
     for head in range(heads):
         at = [slice((head * 3 + j) * HD, (head * 3 + j + 1) * HD) for j in range(3)]
         query = q[rows, at[0]]
         keys = jnp.concatenate([b[:, at[1]] for b in blocks], axis=0)
         values = jnp.concatenate([b[:, at[2]] for b in blocks], axis=0)
         scores = lax.dot_general(query, keys, (((1,), (1,)), ((), ())), preferred_element_type=F32)
-        scores = scores * (1.0 / HD**0.5)
-        powers = jnp.exp(scores - jnp.max(scores, axis=-1, keepdims=True))
-        probs = (powers / jnp.sum(powers, axis=-1, keepdims=True)).astype(BF16)
-        out = jnp.dot(probs, values, preferred_element_type=F32)
-        mixed[rows, head * HD : (head + 1) * HD] = out.astype(BF16)
+        powers = jnp.exp((scores - jnp.max(scores, axis=-1, keepdims=True)) * (1.0 / HD**0.5)).astype(BF16)
+        out = jnp.dot(powers, jnp.concatenate([values, ones], axis=1), preferred_element_type=F32)
+        mixed[rows, head * HD : (head + 1) * HD] = (out[:, :HD] / out[:, HD:]).astype(BF16)
 
 
 def own_qkv_kernel(parts, *refs):
@@ -238,8 +240,9 @@
 
 
 def cuts(rows, shares):
-    sizes = [max(16, rows * share // sum(shares)) for share in shares]
-    return [(sum(sizes[:i]), size) for i, size in enumerate(sizes)]
+    units = rows // 16
+    edges = [units * sum(shares[:i]) // sum(shares) * 16 for i in range(len(shares))] + [rows]
+    return [(a, b - a) for a, b in zip(edges, edges[1:]) if b > a]
 
 
 def layer(pieces, chunks, got, gain, bias, w_in, w_out, alone=()):
@@ -359,7 +362,7 @@
                 wait=ready,
             )
             results.append(result)
-            arrived.append(held_inside(from_behind(result, "section")))
+            arrived.append(held_inside(from_behind(result, "section", RING[tick])))
         if tick == 0:
             chunks, swapped = [], []
             for i, (start, size) in enumerate(pieces):

time: 73.3 us -> 74.6 us (1.018)
  starting transfers between devices: 15.2 us -> 17.9 us
  Pallas kernels: 27.7 us -> 26.1 us
    ppermute x5, starting transfers between devices: 0.29 us -> 3.41 us  [from_behind(): lax.ppermute(block, axis, [(i, (i + 1) % size) for i in range(size - 1 +...]
    pallas_call x21, Pallas kernels: 27.7 us -> 26.1 us  [call(): pl.pallas_call(kernel, out_shape=outs, out_specs=out_specs, in_specs=in_s...]
  transfers between devices with their start and end apart: 14 -> 14, of which waited for: 9 -> 9; matrix products, arithmetic and copies ran while one was open for 0% -> 0% of each run, Pallas kernels for 27% -> 25%
where the time goes in v6:
time: 74.6 us; the launch traced here: 74.3 us
  waiting for transfers between devices  29.4 us (39%)
  Pallas kernels  26.1 us (35%)
  starting transfers between devices  17.9 us (24%)
  between operations  1.01 us (1%)
    pallas_call x21, Pallas kernels, call(): pl.pallas_call(kernel, out_shape=outs, out_specs=out_specs, in_specs=in_s...  26.1 us
    ppermute x9, waiting for transfers between devices, rotate(): return held_inside(lax.ppermute(block, names, route))  25.9 us
    ppermute x9, starting transfers between devices, rotate(): return held_inside(lax.ppermute(block, names, route))  14.4 us
    ppermute x5, waiting for transfers between devices, from_behind(): lax.ppermute(block, axis, [(i, (i + 1) % size) for i in range(size - 1 +...  3.53 us
    ppermute x5, starting transfers between devices, from_behind(): lax.ppermute(block, axis, [(i, (i + 1) % size) for i in range(size - 1 +...  3.41 us
  transfers between devices with their start and end apart: 14, of which 9 were waited for; matrix products, arithmetic and copies ran while one was open for 0% of the time, Pallas kernels for 25%

profile of v6, /device:TPU:0, one launch (start us, length us, event | category | flops | bytes accessed | tf_op | source)
XLA Modules:
  0.0 74.3 jit_solution(13214900007044873259)
XLA Ops:
  0.7 1.3 %shard_map.86 = (bf16[128,2048]{1,0:T(8,128)(2,1)S(1)}, s32[1,2]{1,0:T(1,128)S(4)}) custom-call(s32[1,2]{1,0:T(1,128)} %order.1, bf16[1,2,128,2048]{3,2,1,0:T(8,128)(2,1)} %refs_2_.7), custom_call_target="tpu_custom_call" | custom-call | flops 1048576 | bytes 65536 | tf_op jit(solution)/shard_map/pallas_call | solution.py:43
  1.9 3.0 %collective-permute-start = (bf16[128,2048]{1,0:T(8,128)(2,1)S(1)}, bf16[128,2048]{1,0:T(8,128)(2,1)S(1)}, u32[]{:S(2)}, u32[]{:S(2)}) collective-permute-start(bf16[128,2048]{1,0:T(8,128)(2,1)S(1)} %get-tuple-element.14.refs_0_), channel_id=1, source_target_pairs={{0,4},{1,5},{2,6},{3,7},{4,0},{5,1},{6,2},{7,3},{8,12},{9,13},{10,... | collective-permute-start | bytes 1572872 | tf_op jit(solution)/shard_map/ppermute | solution.py:75
  5.0 5.9 %shard_map.87 = (bf16[2048,3072]{1,0:T(8,128)(2,1)S(1)}, bf16[1024,2048]{1,0:T(8,128)(2,1)S(1)}) custom-call(bf16[1,2048,3072]{2,1,0:T(8,128)(2,1)} %w_in.1, bf16[1,1024,2048]{2,1,0:T(8,128)(2,1)} %w_out.1), custom_call_target="tpu_custom_call" | custom-call | flops 1073741824 | bytes 65536 | tf_op jit(solution)/shard_map/pallas_call | solution.py:43
  10.9 2.1 %shard_map.88.refs_5_.mine = bf16[128,3072]{1,0:T(8,128)(2,1)S(1)} custom-call(bf16[128,2048]{1,0:T(8,128)(2,1)S(1)} %get-tuple-element.14.refs_0_, f32[1,2048]{1,0:T(1,128)S(1)} %copy-done, f32[1,2048]{1,0:T(1,128)S(1)} %copy-done.1, bf16[2048,3072]{1,0:T(8,128)(2,1)S(1)} %get-tuple-element.15.refs_3_.refs_4_.refs_5_), custom_call_target="tpu_custom_call" | custom-call | flops 1610612736 | bytes 65536 | tf_op jit(solution)/shard_map/pallas_call | solution.py:43
  13.0 3.9 %collective-permute-done.refs_0_ = bf16[128,2048]{1,0:T(8,128)(2,1)S(1)} collective-permute-done((bf16[128,2048]{1,0:T(8,128)(2,1)S(1)}, bf16[128,2048]{1,0:T(8,128)(2,1)S(1)}, u32[]{:S(2)}, u32[]{:S(2)}) %collective-permute-start) | collective-permute-done | bytes 524320 | tf_op jit(solution)/shard_map/ppermute | solution.py:75
  16.9 3.2 %shard_map.89 = (bf16[128,3072]{1,0:T(8,128)(2,1)S(1)}, bf16[64,2048]{1,0:T(8,128)(2,1)S(1)}, bf16[64,2048]{1,0:T(8,128)(2,1)S(1)}) custom-call(bf16[128,2048]{1,0:T(8,128)(2,1)S(1)} %collective-permute-done.refs_0_, f32[1,2048]{1,0:T(1,128)S(1)} %copy-done, f32[1,2048]{1,0:T(1,128)S(1)} %copy-done.1, ...), custom_call_target="tpu_custom_call" | custom-call | flops 1610612736 | bytes 65536 | tf_op jit(solution)/shard_map/pallas_call | solution.py:43
  20.1 1.8 %collective-permute-start.1 = (bf16[64,2048]{1,0:T(8,128)(2,1)S(1)}, bf16[64,2048]{1,0:T(8,128)(2,1)S(1)}, u32[]{:S(2)}, u32[]{:S(2)}) collective-permute-start(bf16[64,2048]{1,0:T(8,128)(2,1)S(1)} %get-tuple-element.18), channel_id=1, source_target_pairs={{0,4},{1,5},{2,6},{3,7},{4,0},{5,1},{6,2},{7,3},{8,12},{9,13},{10,... | collective-permute-start | bytes 786440 | tf_op jit(solution)/shard_map/ppermute | solution.py:75
  22.2 1.2 %shard_map.90.refs_1_ = bf16[128,2048]{1,0:T(8,128)(2,1)S(1)} custom-call(bf16[128,3072]{1,0:T(8,128)(2,1)S(1)} %shard_map.88.refs_5_.mine, bf16[128,3072]{1,0:T(8,128)(2,1)S(1)} %get-tuple-element.17.theirs, bf16[1024,2048]{1,0:T(8,128)(2,1)S(1)} %get-tuple-element.16.refs_4_.w_out.refs_6_), custom_call_target="tpu_custom_call" | custom-call | flops 536870912 | bytes 65536 | tf_op jit(solution)/shard_map/pallas_call | solution.py:43
  23.4 5.9 %collective-permute-done.1.refs_2_ = bf16[64,2048]{1,0:T(8,128)(2,1)S(1)} collective-permute-done((bf16[64,2048]{1,0:T(8,128)(2,1)S(1)}, bf16[64,2048]{1,0:T(8,128)(2,1)S(1)}, u32[]{:S(2)}, u32[]{:S(2)}) %collective-permute-start.1) | collective-permute-done | bytes 262176 | tf_op jit(solution)/shard_map/ppermute | solution.py:75
  29.4 1.3 %collective-permute-start.2 = (bf16[64,2048]{1,0:T(8,128)(2,1)S(1)}, bf16[64,2048]{1,0:T(8,128)(2,1)S(1)}, u32[]{:S(2)}, u32[]{:S(2)}) collective-permute-start(bf16[64,2048]{1,0:T(8,128)(2,1)S(1)} %shard_map.91.refs_1_), channel_id=1, source_target_pairs={{0,8},{8,16},{16,24},{1,9},{9,17},{17,25},{2,10},{10,18},{18,26},{... | collective-permute-start | bytes 786440 | tf_op jit(solution)/shard_map/ppermute | solution.py:60
  30.7 2.5 %collective-permute-done.3.refs_2_ = bf16[64,2048]{1,0:T(8,128)(2,1)S(1)} collective-permute-done((bf16[64,2048]{1,0:T(8,128)(2,1)S(1)}, bf16[64,2048]{1,0:T(8,128)(2,1)S(1)}, u32[]{:S(2)}, u32[]{:S(2)}) %collective-permute-start.3) | collective-permute-done | bytes 262176 | tf_op jit(solution)/shard_map/ppermute | solution.py:75
  33.3 1.9 %collective-permute-start.4 = (bf16[64,2048]{1,0:T(8,128)(2,1)S(1)}, bf16[64,2048]{1,0:T(8,128)(2,1)S(1)}, u32[]{:S(2)}, u32[]{:S(2)}) collective-permute-start(bf16[64,2048]{1,0:T(8,128)(2,1)S(1)} %shard_map.94.refs_2_), channel_id=1, source_target_pairs={{0,8},{8,16},{16,24},{1,9},{9,17},{17,25},{2,10},{10,18},{18,26},{... | collective-permute-start | bytes 786440 | tf_op jit(solution)/shard_map/ppermute | solution.py:60
  36.4 3.6 %collective-permute-start.7 = (bf16[128,2048]{1,0:T(8,128)(2,1)S(1)}, bf16[128,2048]{1,0:T(8,128)(2,1)S(1)}, u32[]{:S(2)}, u32[]{:S(2)}) collective-permute-start(bf16[128,2048]{1,0:T(8,128)(2,1)S(1)} %shard_map.92.other), channel_id=1, source_target_pairs={{0,4},{1,5},{2,6},{3,7},{4,0},{5,1},{6,2},{7,3}} | collective-permute-start | bytes 1572872 | tf_op jit(solution)/shard_map/ppermute | solution.py:75
  40.0 1.6 %collective-permute-start.5 = (bf16[64,2048]{1,0:T(8,128)(2,1)S(1)}, bf16[64,2048]{1,0:T(8,128)(2,1)S(1)}, u32[]{:S(2)}, u32[]{:S(2)}) collective-permute-start(bf16[64,2048]{1,0:T(8,128)(2,1)S(1)} %shard_map.93.refs_0_.refs_2_), channel_id=1, source_target_pairs={{0,1},{1,0},{2,3},{3,2},{4,5},{5,4},{6,7},{7,6},{8,12},{9,13},{10,... | collective-permute-start | bytes 786440 | tf_op jit(solution)/shard_map/ppermute | solution.py:75
  42.2 2.1 %shard_map.96.refs_7_.mine = bf16[128,3072]{1,0:T(8,128)(2,1)S(1)} custom-call(bf16[64,2048]{1,0:T(8,128)(2,1)S(1)} %shard_map.93.refs_0_.refs_2_, bf16[64,2048]{1,0:T(8,128)(2,1)S(1)} %shard_map.95.refs_1_.refs_2_, f32[1,2048]{1,0:T(1,128)S(1)} %copy-done, f32[1,2048]{1,0:T(1,128)S(1)} %copy-done.1, ...), custom_call_target="tpu_custom_call" | custom-call | flops 1610612736 | bytes 65536 | tf_op jit(solution)/shard_map/pallas_call | solution.py:43
  44.3 8.5 %collective-permute-done.7.refs_2_ = bf16[128,2048]{1,0:T(8,128)(2,1)S(1)} collective-permute-done((bf16[128,2048]{1,0:T(8,128)(2,1)S(1)}, bf16[128,2048]{1,0:T(8,128)(2,1)S(1)}, u32[]{:S(2)}, u32[]{:S(2)}) %collective-permute-start.7) | collective-permute-done | bytes 524320 | tf_op jit(solution)/shard_map/ppermute | solution.py:75
  52.8 3.2 %shard_map.97 = (bf16[128,3072]{1,0:T(8,128)(2,1)S(1)}, bf16[64,2048]{1,0:T(8,128)(2,1)S(1)}, bf16[32,2048]{1,0:T(8,128)(2,1)S(1)}, bf16[32,2048]{1,0:T(8,128)(2,1)S(1)}) custom-call(bf16[64,2048]{1,0:T(8,128)(2,1)S(1)} %collective-permute-done.5.refs_0_, bf16[64,2048]{1,0:T(8,128)(2,1)S(1)} %collective-permute-done.6.refs_1_, ...), custom_call_target="tpu_custom_call" | custom-call | flops 1610612736 | bytes 65536 | tf_op jit(solution)/shard_map/pallas_call | solution.py:43
  56.0 1.6 %collective-permute-start.8 = (bf16[64,2048]{1,0:T(8,128)(2,1)S(1)}, bf16[64,2048]{1,0:T(8,128)(2,1)S(1)}, u32[]{:S(2)}, u32[]{:S(2)}) collective-permute-start(bf16[64,2048]{1,0:T(8,128)(2,1)S(1)} %get-tuple-element.21), channel_id=1, source_target_pairs={{0,4},{1,5},{2,6},{3,7},{4,0},{5,1},{6,2},{7,3},{8,12},{9,13},{10,... | collective-permute-start | bytes 786440 | tf_op jit(solution)/shard_map/ppermute | solution.py:75
  58.1 1.5 %collective-permute-start.10 = (bf16[32,2048]{1,0:T(8,128)(2,1)S(1)}, bf16[32,2048]{1,0:T(8,128)(2,1)S(1)}, u32[]{:S(2)}, u32[]{:S(2)}) collective-permute-start(bf16[32,2048]{1,0:T(8,128)(2,1)S(1)} %get-tuple-element.23), channel_id=1, source_target_pairs={{0,4},{1,5},{2,6},{3,7},{4,0},{5,1},{6,2},{7,3},{8,12},{9,13},{10,... | collective-permute-start | bytes 393224 | tf_op jit(solution)/shard_map/ppermute | solution.py:75
  61.6 2.7 %shard_map.100.refs_1_.refs_2_ = bf16[1,2,128,2048]{3,2,1,0:T(8,128)(2,1)} custom-call(bf16[128,2048]{1,0:T(8,128)(2,1)S(1)} %shard_map.98.refs_0_.refs_3_, s32[1,2]{1,0:T(1,128)S(4)} %get-tuple-element.13.order.refs_1_, bf16[1,2,128,2048]{3,2,1,0:T(8,128)(2,1)} %refs_2_.7, bf16[2,128,2048]{2,1,0:T(8,128)(2,1)} %refs_3_.5, ...), custom_call_target="tpu_custom_call" | custom-call | flops 1048576 | bytes 65536 | tf_op jit(solution)/shard_map/pallas_call | solution.py:43
  65.4 2.6 %collective-permute-done.9.refs_4_ = bf16[32,2048]{1,0:T(8,128)(2,1)S(1)} collective-permute-done((bf16[32,2048]{1,0:T(8,128)(2,1)S(1)}, bf16[32,2048]{1,0:T(8,128)(2,1)S(1)}, u32[]{:S(2)}, u32[]{:S(2)}) %collective-permute-start.9) | collective-permute-done | bytes 131104 | tf_op jit(solution)/shard_map/ppermute | solution.py:75
  68.1 1.5 %collective-permute-done.10.refs_4_ = bf16[32,2048]{1,0:T(8,128)(2,1)S(1)} collective-permute-done((bf16[32,2048]{1,0:T(8,128)(2,1)S(1)}, bf16[32,2048]{1,0:T(8,128)(2,1)S(1)}, u32[]{:S(2)}, u32[]{:S(2)}) %collective-permute-start.10) | collective-permute-done | bytes 131104 | tf_op jit(solution)/shard_map/ppermute | solution.py:75
  70.6 1.9 %collective-permute-done.13.refs_1_ = bf16[32,2048]{1,0:T(8,128)(2,1)S(1)} collective-permute-done((bf16[32,2048]{1,0:T(8,128)(2,1)S(1)}, bf16[32,2048]{1,0:T(8,128)(2,1)S(1)}, u32[]{:S(2)}, u32[]{:S(2)}) %collective-permute-start.13) | collective-permute-done | bytes 131104 | tf_op jit(solution)/shard_map/ppermute | solution.py:60
  72.6 1.6 %collective-permute-done.11.refs_0_ = bf16[32,2048]{1,0:T(8,128)(2,1)S(1)} collective-permute-done((bf16[32,2048]{1,0:T(8,128)(2,1)S(1)}, bf16[32,2048]{1,0:T(8,128)(2,1)S(1)}, u32[]{:S(2)}, u32[]{:S(2)}) %collective-permute-start.11) | collective-permute-done | bytes 131104 | tf_op jit(solution)/shard_map/ppermute | solution.py:60
  (29 shorter events, 6.8 us)
Async XLA Ops:
  0.6 10.2 %copy-start.1 = (f32[1,2048]{1,0:T(1,128)S(1)}, f32[1,2048]{1,0:T(1,128)}, u32[]{:S(2)}) copy-start(f32[1,2048]{1,0:T(1,128)} %refs_4_.1) | copy-start | bytes 24580
  0.6 10.2 %copy-start = (f32[1,2048]{1,0:T(1,128)S(1)}, f32[1,2048]{1,0:T(1,128)}, u32[]{:S(2)}) copy-start(f32[1,2048]{1,0:T(1,128)} %refs_3_.4) | copy-start | bytes 24580
  1.9 15.0 %collective-permute-start = (bf16[128,2048]{1,0:T(8,128)(2,1)S(1)}, bf16[128,2048]{1,0:T(8,128)(2,1)S(1)}, u32[]{:S(2)}, u32[]{:S(2)}) collective-permute-start(bf16[128,2048]{1,0:T(8,128)(2,1)S(1)} %get-tuple-element.14.refs_0_), channel_id=1, source_target_pairs={{0,4},{1,5},{2,6},{3,7},{4,0},{5,1},{6,2},{7,3},{8,12},{9,13},{10,... | collective-permute-start | bytes 1572872 | tf_op jit(solution)/shard_map/ppermute | solution.py:75
  20.1 9.2 %collective-permute-start.1 = (bf16[64,2048]{1,0:T(8,128)(2,1)S(1)}, bf16[64,2048]{1,0:T(8,128)(2,1)S(1)}, u32[]{:S(2)}, u32[]{:S(2)}) collective-permute-start(bf16[64,2048]{1,0:T(8,128)(2,1)S(1)} %get-tuple-element.18), channel_id=1, source_target_pairs={{0,4},{1,5},{2,6},{3,7},{4,0},{5,1},{6,2},{7,3},{8,12},{9,13},{10,... | collective-permute-start | bytes 786440 | tf_op jit(solution)/shard_map/ppermute | solution.py:75
  21.9 11.3 %collective-permute-start.3 = (bf16[64,2048]{1,0:T(8,128)(2,1)S(1)}, bf16[64,2048]{1,0:T(8,128)(2,1)S(1)}, u32[]{:S(2)}, u32[]{:S(2)}) collective-permute-start(bf16[64,2048]{1,0:T(8,128)(2,1)S(1)} %get-tuple-element.19), channel_id=1, source_target_pairs={{0,4},{1,5},{2,6},{3,7},{4,0},{5,1},{6,2},{7,3},{8,12},{9,13},{10,... | collective-permute-start | bytes 786440 | tf_op jit(solution)/shard_map/ppermute | solution.py:75
  29.4 10.5 %collective-permute-start.2 = (bf16[64,2048]{1,0:T(8,128)(2,1)S(1)}, bf16[64,2048]{1,0:T(8,128)(2,1)S(1)}, u32[]{:S(2)}, u32[]{:S(2)}) collective-permute-start(bf16[64,2048]{1,0:T(8,128)(2,1)S(1)} %shard_map.91.refs_1_), channel_id=1, source_target_pairs={{0,8},{8,16},{16,24},{1,9},{9,17},{17,25},{2,10},{10,18},{18,26},{... | collective-permute-start | bytes 786440 | tf_op jit(solution)/shard_map/ppermute | solution.py:60
  33.3 8.3 %collective-permute-start.4 = (bf16[64,2048]{1,0:T(8,128)(2,1)S(1)}, bf16[64,2048]{1,0:T(8,128)(2,1)S(1)}, u32[]{:S(2)}, u32[]{:S(2)}) collective-permute-start(bf16[64,2048]{1,0:T(8,128)(2,1)S(1)} %shard_map.94.refs_2_), channel_id=1, source_target_pairs={{0,8},{8,16},{16,24},{1,9},{9,17},{17,25},{2,10},{10,18},{18,26},{... | collective-permute-start | bytes 786440 | tf_op jit(solution)/shard_map/ppermute | solution.py:60
  36.4 16.4 %collective-permute-start.7 = (bf16[128,2048]{1,0:T(8,128)(2,1)S(1)}, bf16[128,2048]{1,0:T(8,128)(2,1)S(1)}, u32[]{:S(2)}, u32[]{:S(2)}) collective-permute-start(bf16[128,2048]{1,0:T(8,128)(2,1)S(1)} %shard_map.92.other), channel_id=1, source_target_pairs={{0,4},{1,5},{2,6},{3,7},{4,0},{5,1},{6,2},{7,3}} | collective-permute-start | bytes 1572872 | tf_op jit(solution)/shard_map/ppermute | solution.py:75
  40.0 12.8 %collective-permute-start.5 = (bf16[64,2048]{1,0:T(8,128)(2,1)S(1)}, bf16[64,2048]{1,0:T(8,128)(2,1)S(1)}, u32[]{:S(2)}, u32[]{:S(2)}) collective-permute-start(bf16[64,2048]{1,0:T(8,128)(2,1)S(1)} %shard_map.93.refs_0_.refs_2_), channel_id=1, source_target_pairs={{0,1},{1,0},{2,3},{3,2},{4,5},{5,4},{6,7},{7,6},{8,12},{9,13},{10,... | collective-permute-start | bytes 786440 | tf_op jit(solution)/shard_map/ppermute | solution.py:75
  41.7 11.1 %collective-permute-start.6 = (bf16[64,2048]{1,0:T(8,128)(2,1)S(1)}, bf16[64,2048]{1,0:T(8,128)(2,1)S(1)}, u32[]{:S(2)}, u32[]{:S(2)}) collective-permute-start(bf16[64,2048]{1,0:T(8,128)(2,1)S(1)} %shard_map.95.refs_1_.refs_2_), channel_id=1, source_target_pairs={{0,1},{1,0},{2,3},{3,2},{4,5},{5,4},{6,7},{7,6},{8,12},{9,13},{10,... | collective-permute-start | bytes 786440 | tf_op jit(solution)/shard_map/ppermute | solution.py:75
  56.0 9.2 %collective-permute-start.8 = (bf16[64,2048]{1,0:T(8,128)(2,1)S(1)}, bf16[64,2048]{1,0:T(8,128)(2,1)S(1)}, u32[]{:S(2)}, u32[]{:S(2)}) collective-permute-start(bf16[64,2048]{1,0:T(8,128)(2,1)S(1)} %get-tuple-element.21), channel_id=1, source_target_pairs={{0,4},{1,5},{2,6},{3,7},{4,0},{5,1},{6,2},{7,3},{8,12},{9,13},{10,... | collective-permute-start | bytes 786440 | tf_op jit(solution)/shard_map/ppermute | solution.py:75
  57.5 10.5 %collective-permute-start.9 = (bf16[32,2048]{1,0:T(8,128)(2,1)S(1)}, bf16[32,2048]{1,0:T(8,128)(2,1)S(1)}, u32[]{:S(2)}, u32[]{:S(2)}) collective-permute-start(bf16[32,2048]{1,0:T(8,128)(2,1)S(1)} %get-tuple-element.22), channel_id=1, source_target_pairs={{0,4},{1,5},{2,6},{3,7},{4,0},{5,1},{6,2},{7,3},{8,12},{9,13},{10,... | collective-permute-start | bytes 393224 | tf_op jit(solution)/shard_map/ppermute | solution.py:75
  58.1 11.6 %collective-permute-start.10 = (bf16[32,2048]{1,0:T(8,128)(2,1)S(1)}, bf16[32,2048]{1,0:T(8,128)(2,1)S(1)}, u32[]{:S(2)}, u32[]{:S(2)}) collective-permute-start(bf16[32,2048]{1,0:T(8,128)(2,1)S(1)} %get-tuple-element.23), channel_id=1, source_target_pairs={{0,4},{1,5},{2,6},{3,7},{4,0},{5,1},{6,2},{7,3},{8,12},{9,13},{10,... | collective-permute-start | bytes 393224 | tf_op jit(solution)/shard_map/ppermute | solution.py:75
  65.3 7.3 %collective-permute-start.12 = (bf16[64,2048]{1,0:T(8,128)(2,1)S(1)}, bf16[64,2048]{1,0:T(8,128)(2,1)S(1)}, u32[]{:S(2)}, u32[]{:S(2)}) collective-permute-start(bf16[64,2048]{1,0:T(8,128)(2,1)S(1)} %shard_map.101.refs_0_), channel_id=1, source_target_pairs={{0,8},{8,16},{16,24},{24,0},{1,9},{9,17},{17,25},{25,1},{2,10},{10... | collective-permute-start | bytes 786440 | tf_op jit(solution)/shard_map/ppermute | solution.py:60
  68.1 4.5 %collective-permute-start.13 = (bf16[32,2048]{1,0:T(8,128)(2,1)S(1)}, bf16[32,2048]{1,0:T(8,128)(2,1)S(1)}, u32[]{:S(2)}, u32[]{:S(2)}) collective-permute-start(bf16[32,2048]{1,0:T(8,128)(2,1)S(1)} %shard_map.102.refs_1_), channel_id=1, source_target_pairs={{0,8},{8,16},{16,24},{24,0},{1,9},{9,17},{17,25},{25,1},{2,10},{10... | collective-permute-start | bytes 393224 | tf_op jit(solution)/shard_map/ppermute | solution.py:60
  69.7 4.4 %collective-permute-start.11 = (bf16[32,2048]{1,0:T(8,128)(2,1)S(1)}, bf16[32,2048]{1,0:T(8,128)(2,1)S(1)}, u32[]{:S(2)}, u32[]{:S(2)}) collective-permute-start(bf16[32,2048]{1,0:T(8,128)(2,1)S(1)} %shard_map.103.refs_2_), channel_id=1, source_target_pairs={{0,8},{8,16},{16,24},{24,0},{1,9},{9,17},{17,25},{25,1},{2,10},{10... | collective-permute-start | bytes 393224 | tf_op jit(solution)/shard_map/ppermute | solution.py:60

commit v7 on v6

--- a/solution.py
+++ b/solution.py
@@ -75,14 +75,18 @@
     return held_inside(lax.ppermute(block, names, route))
 
 
-def pick_kernel(order, acts, current, kept, slots, sems):
+def pick_kernel(parts, order, acts, *refs):
+    chunks, (kept, slots, sems) = refs[:parts], refs[parts:]
     number = pltpu.make_async_copy(order, kept, sems.at[0])
     blocks = pltpu.make_async_copy(acts.at[0], slots, sems.at[1])
     number.start()
     blocks.start()
     number.wait()
     blocks.wait()
-    current[...] = slots[kept[0, 0]]
+    at = 0
+    for chunk in chunks:
+        chunk[...] = slots[kept[0, 0], at : at + chunk.shape[0]]
+        at += chunk.shape[0]
 
 
 def weights_kernel(w_in, w_out, in_inside, out_inside, sems):
@@ -154,24 +158,35 @@
     project(hidden[...], weights, qkv)
 
 
-def others_kernel(parts, pieces, spare, *refs):
-    chunks, alone, refs = refs[:parts], refs[parts : parts + spare], refs[:parts] + refs[parts + spare :]
-    first = lax.axis_index("section") == 0
-    gain, bias, w_in, w_out, mine = refs[parts : parts + 5]
-    qkv = refs[parts + 5]
-    outs = refs[parts + 6 : parts + 6 + pieces]
-    hidden, mixed = refs[parts + 6 + pieces :]
-    at = 0
-    for chunk in chunks:
+def chosen(chunk, alone, j, start):
+    value = chunk[...]
+    if alone:
+        mine = alone[j][start : start + chunk.shape[0]]
+        value = jnp.where(lax.axis_index("section") == 0, mine, value)
+    return value
+
+
+def ahead_kernel(blocks, spare, *refs):
+    firsts, alone, (gain, bias, hidden) = refs[:blocks], refs[blocks : blocks + spare], refs[blocks + spare :]
+    for j, chunk in enumerate(firsts):
         rows = chunk.shape[0]
-        value = chunk[...]
-        if alone:
-            start = at % alone[0].shape[0]
-            value = jnp.where(first, alone[at // alone[0].shape[0]][start : start + rows], value)
-        hidden[at : at + rows] = normed(value, gain[...], bias[...])
-        at += rows
+        hidden[j * rows : (j + 1) * rows] = normed(chosen(chunk, alone, j, 0), gain[...], bias[...])
+
+
+def others_kernel(blocks, parts, spare, *refs):
+    count = blocks * (parts - 1)
+    ready, chunks, alone = refs[0], refs[1 : 1 + count], refs[1 + count : 1 + count + spare]
+    gain, bias, w_in, w_out, mine, qkv, *outs, hidden, mixed = refs[1 + count + spare :]
+    rows, first = hidden.shape[0] // blocks, ready.shape[0] // blocks
+    for j in range(blocks):
+        hidden[j * rows : j * rows + first] = ready[j * first : (j + 1) * first]
+        at = first
+        for chunk in chunks[j * (parts - 1) : (j + 1) * (parts - 1)]:
+            here = slice(j * rows + at, j * rows + at + chunk.shape[0])
+            hidden[here] = normed(chosen(chunk, alone, j, at), gain[...], bias[...])
+            at += chunk.shape[0]
     project(hidden[...], w_in, qkv)
-    attend(qkv, (mine, qkv), slice(0, at), mixed)
+    attend(qkv, (mine, qkv), slice(0, hidden.shape[0]), mixed)
     project(mixed[...], w_out, *outs)
 
 
@@ -263,12 +278,24 @@
     )
     far = (size - 1) * rows
     count = (size - 1) * len(pieces)
+    blocks = size - 1
+    each = len(got) // blocks
+    firsts = got[::each]
+    rest = [block for i, block in enumerate(got) if i % each]
+    ready = call(
+        functools.partial(ahead_kernel, blocks, len(alone)),
+        inner((sum(block.shape[0] for block in firsts), width)),
+        VMEM,
+        [VMEM] * (blocks + len(alone) + 2),
+        [*firsts, *alone, gain, bias],
+        wait=[mine],
+    )
     theirs, *sends = call(
-        functools.partial(others_kernel, len(got), count, len(alone)),
+        functools.partial(others_kernel, blocks, each, len(alone)),
         [inner((far, wide))] + [inner((n, width)) for _ in range(size - 1) for _, n in pieces],
         [VMEM] * (count + 1),
-        [VMEM] * (len(got) + len(alone) + 5),
-        [*got, *alone, gain, bias, w_in, w_out, mine],
+        [VMEM] * (len(rest) + len(alone) + 6),
+        [ready, *rest, *alone, gain, bias, w_in, w_out, mine],
         flops=2 * far * width * wide,
         scratch=[inner((far, width)), inner((far, deep))],
     )
@@ -293,10 +320,11 @@
     ticks = fresh.shape[0]
     dma = pltpu.SemaphoreType.DMA
     acts, fresh, order, wqkv, wo = map(outside, (acts, fresh, order, wqkv, wo))
-    current, order = call(
-        pick_kernel,
-        [inner((rows, width)), pltpu.SMEM(order.shape, order.dtype)],
-        [VMEM, SMEM],
+    pieces = cuts(rows, (1,))
+    *chunks, order = call(
+        functools.partial(pick_kernel, len(pieces)),
+        [*(inner((size, width)) for _, size in pieces), pltpu.SMEM(order.shape, order.dtype)],
+        [VMEM] * len(pieces) + [SMEM],
         [ANY, ANY],
         [order, acts],
         scratch=[inner(acts.shape[1:]), dma((2,))],
@@ -314,8 +342,7 @@
     )
     shifts = range(1, lax.axis_size("tensor"))
     sections = range(lax.axis_size("section"))
-    chunks = [current]
-    got = [rotate(current, j, sections) for j in shifts]
+    got = [rotate(chunk, j, sections) for j in shifts for chunk in chunks]
     alone = [rotate(other, j, [0]) for j in shifts]
     section_out = held = None
     for tick in range(ticks):

time: 74.6 us -> 68 us (0.912)
  the two profiles are of different devices: /device:TPU:0 before, /device:TPU:1 now
where the time goes in v7:
time: 68 us; the launch traced here: 67.7 us
  Pallas kernels  27.8 us (41%)
  starting transfers between devices  24.8 us (36%)
  waiting for transfers between devices  14.1 us (21%)
  between operations  1.04 us (2%)
    pallas_call x23, Pallas kernels, call(): pl.pallas_call(kernel, out_shape=outs, out_specs=out_specs, in_specs=in_s...  27.8 us
    ppermute x5, starting transfers between devices, from_behind(): lax.ppermute(block, axis, [(i, (i + 1) % size) for i in range(size - 1 +...  15.2 us
    ppermute x9, starting transfers between devices, rotate(): return held_inside(lax.ppermute(block, names, route))  9.61 us
    ppermute x9, waiting for transfers between devices, rotate(): return held_inside(lax.ppermute(block, names, route))  9.13 us
    ppermute x5, waiting for transfers between devices, from_behind(): lax.ppermute(block, axis, [(i, (i + 1) % size) for i in range(size - 1 +...  4.95 us
  transfers between devices with their start and end apart: 14, of which 8 were waited for; matrix products, arithmetic and copies ran while one was open for 0% of the time, Pallas kernels for 29%

profile of v7, /device:TPU:1, one launch (start us, length us, event | category | flops | bytes accessed | tf_op | source)
XLA Modules:
  0.0 67.7 jit_solution(10705652165603492558)
XLA Ops:
  0.7 1.3 %shard_map.86 = (bf16[128,2048]{1,0:T(8,128)(2,1)S(1)}, s32[1,2]{1,0:T(1,128)S(4)}) custom-call(s32[1,2]{1,0:T(1,128)} %order.1, bf16[1,2,128,2048]{3,2,1,0:T(8,128)(2,1)} %refs_2_.9), custom_call_target="tpu_custom_call" | custom-call | flops 1048576 | bytes 65536 | tf_op jit(solution)/shard_map/pallas_call | solution.py:43
  1.9 2.1 %collective-permute-start = (bf16[128,2048]{1,0:T(8,128)(2,1)S(1)}, bf16[128,2048]{1,0:T(8,128)(2,1)S(1)}, u32[]{:S(2)}, u32[]{:S(2)}) collective-permute-start(bf16[128,2048]{1,0:T(8,128)(2,1)S(1)} %get-tuple-element.14.refs_0_), channel_id=1, source_target_pairs={{0,4},{1,5},{2,6},{3,7},{4,0},{5,1},{6,2},{7,3},{8,12},{9,13},{10,... | collective-permute-start | bytes 1572872 | tf_op jit(solution)/shard_map/ppermute | solution.py:75
  4.0 5.9 %shard_map.87 = (bf16[2048,3072]{1,0:T(8,128)(2,1)S(1)}, bf16[1024,2048]{1,0:T(8,128)(2,1)S(1)}) custom-call(bf16[1,2048,3072]{2,1,0:T(8,128)(2,1)} %w_in.1, bf16[1,1024,2048]{2,1,0:T(8,128)(2,1)} %w_out.1), custom_call_target="tpu_custom_call" | custom-call | flops 1073741824 | bytes 65536 | tf_op jit(solution)/shard_map/pallas_call | solution.py:43
  10.0 2.1 %shard_map.88.refs_0_.refs_5_.mine = bf16[128,3072]{1,0:T(8,128)(2,1)S(1)} custom-call(bf16[128,2048]{1,0:T(8,128)(2,1)S(1)} %get-tuple-element.14.refs_0_, f32[1,2048]{1,0:T(1,128)S(1)} %copy-done, f32[1,2048]{1,0:T(1,128)S(1)} %copy-done.1, bf16[2048,3072]{1,0:T(8,128)(2,1)S(1)} %get-tuple-element.15.refs_3_.refs_4_.refs_5_), custom_call_target="tpu_custom_call" | custom-call | flops 1610612736 | bytes 65536 | tf_op jit(solution)/shard_map/pallas_call | solution.py:43
  12.1 3.6 %collective-permute-done.refs_1_ = bf16[128,2048]{1,0:T(8,128)(2,1)S(1)} collective-permute-done((bf16[128,2048]{1,0:T(8,128)(2,1)S(1)}, bf16[128,2048]{1,0:T(8,128)(2,1)S(1)}, u32[]{:S(2)}, u32[]{:S(2)}) %collective-permute-start) | collective-permute-done | bytes 524320 | tf_op jit(solution)/shard_map/ppermute | solution.py:75
  16.1 2.9 %shard_map.90 = (bf16[128,3072]{1,0:T(8,128)(2,1)S(1)}, bf16[64,2048]{1,0:T(8,128)(2,1)S(1)}, bf16[64,2048]{1,0:T(8,128)(2,1)S(1)}) custom-call(bf16[128,2048]{1,0:T(8,128)(2,1)S(1)} %shard_map.89.refs_0_, f32[1,2048]{1,0:T(1,128)S(1)} %copy-done, f32[1,2048]{1,0:T(1,128)S(1)} %copy-done.1, bf16[2048,3072]{1,0:T(8,128)(2,1)S(1)} %get-tuple-element.15.refs_3_.refs_4_.refs_5_, ...), custom_call_target="tpu_custom_call" | custom-call | flops 1610612736 | bytes 65536 | tf_op jit(solution)/shard_map/pallas_call | solution.py:43
  19.0 1.2 %collective-permute-start.1 = (bf16[64,2048]{1,0:T(8,128)(2,1)S(1)}, bf16[64,2048]{1,0:T(8,128)(2,1)S(1)}, u32[]{:S(2)}, u32[]{:S(2)}) collective-permute-start(bf16[64,2048]{1,0:T(8,128)(2,1)S(1)} %get-tuple-element.18), channel_id=1, source_target_pairs={{0,4},{1,5},{2,6},{3,7},{4,0},{5,1},{6,2},{7,3},{8,12},{9,13},{10,... | collective-permute-start | bytes 786440 | tf_op jit(solution)/shard_map/ppermute | solution.py:75
  22.3 1.2 %shard_map.91.refs_1_ = bf16[128,2048]{1,0:T(8,128)(2,1)S(1)} custom-call(bf16[128,3072]{1,0:T(8,128)(2,1)S(1)} %shard_map.88.refs_0_.refs_5_.mine, bf16[128,3072]{1,0:T(8,128)(2,1)S(1)} %get-tuple-element.17.theirs, bf16[1024,2048]{1,0:T(8,128)(2,1)S(1)} %get-tuple-element.16.refs_4_.w_out.refs_6_), custom_call_target="tpu_custom_call" | custom-call | flops 536870912 | bytes 65536 | tf_op jit(solution)/shard_map/pallas_call | solution.py:43
  23.5 2.1 %collective-permute-done.1.refs_2_ = bf16[64,2048]{1,0:T(8,128)(2,1)S(1)} collective-permute-done((bf16[64,2048]{1,0:T(8,128)(2,1)S(1)}, bf16[64,2048]{1,0:T(8,128)(2,1)S(1)}, u32[]{:S(2)}, u32[]{:S(2)}) %collective-permute-start.1) | collective-permute-done | bytes 262176 | tf_op jit(solution)/shard_map/ppermute | solution.py:75
  25.8 7.1 %collective-permute-start.2 = (bf16[64,2048]{1,0:T(8,128)(2,1)S(1)}, bf16[64,2048]{1,0:T(8,128)(2,1)S(1)}, u32[]{:S(2)}, u32[]{:S(2)}) collective-permute-start(bf16[64,2048]{1,0:T(8,128)(2,1)S(1)} %shard_map.92.refs_1_), channel_id=1, source_target_pairs={{0,8},{8,16},{16,24},{1,9},{9,17},{17,25},{2,10},{10,18},{18,26},{... | collective-permute-start | bytes 786440 | tf_op jit(solution)/shard_map/ppermute | solution.py:60
  33.0 3.7 %collective-permute-start.4 = (bf16[64,2048]{1,0:T(8,128)(2,1)S(1)}, bf16[64,2048]{1,0:T(8,128)(2,1)S(1)}, u32[]{:S(2)}, u32[]{:S(2)}) collective-permute-start(bf16[64,2048]{1,0:T(8,128)(2,1)S(1)} %shard_map.95.refs_2_), channel_id=1, source_target_pairs={{0,8},{8,16},{16,24},{1,9},{9,17},{17,25},{2,10},{10,18},{18,26},{... | collective-permute-start | bytes 786440 | tf_op jit(solution)/shard_map/ppermute | solution.py:60
  36.7 1.3 %collective-permute-start.5 = (bf16[64,2048]{1,0:T(8,128)(2,1)S(1)}, bf16[64,2048]{1,0:T(8,128)(2,1)S(1)}, u32[]{:S(2)}, u32[]{:S(2)}) collective-permute-start(bf16[64,2048]{1,0:T(8,128)(2,1)S(1)} %shard_map.94.refs_0_.refs_2_), channel_id=1, source_target_pairs={{0,1},{1,0},{2,3},{3,2},{4,5},{5,4},{6,7},{7,6},{8,12},{9,13},{10,... | collective-permute-start | bytes 786440 | tf_op jit(solution)/shard_map/ppermute | solution.py:75
  38.0 1.8 %collective-permute-done.4.arriving.refs_5_ = bf16[64,2048]{1,0:T(8,128)(2,1)S(1)} collective-permute-done((bf16[64,2048]{1,0:T(8,128)(2,1)S(1)}, bf16[64,2048]{1,0:T(8,128)(2,1)S(1)}, u32[]{:S(2)}, u32[]{:S(2)}) %collective-permute-start.4) | collective-permute-done | bytes 262176 | tf_op jit(solution)/shard_map/ppermute | solution.py:60
  39.8 1.3 %collective-permute-start.7 = (bf16[64,2048]{1,0:T(8,128)(2,1)S(1)}, bf16[64,2048]{1,0:T(8,128)(2,1)S(1)}, u32[]{:S(2)}, u32[]{:S(2)}) collective-permute-start(bf16[64,2048]{1,0:T(8,128)(2,1)S(1)} %shard_map.96.refs_1_.refs_2_), channel_id=1, source_target_pairs={{0,1},{1,0},{2,3},{3,2},{4,5},{5,4},{6,7},{7,6},{8,12},{9,13},{10,... | collective-permute-start | bytes 786440 | tf_op jit(solution)/shard_map/ppermute | solution.py:75
  41.1 2.1 %shard_map.97.refs_0_.refs_7_.mine = bf16[128,3072]{1,0:T(8,128)(2,1)S(1)} custom-call(bf16[64,2048]{1,0:T(8,128)(2,1)S(1)} %shard_map.94.refs_0_.refs_2_, bf16[64,2048]{1,0:T(8,128)(2,1)S(1)} %shard_map.96.refs_1_.refs_2_, f32[1,2048]{1,0:T(1,128)S(1)} %copy-done, f32[1,2048]{1,0:T(1,128)S(1)} %copy-done.1, ...), custom_call_target="tpu_custom_call" | custom-call | flops 1610612736 | bytes 65536 | tf_op jit(solution)/shard_map/pallas_call | solution.py:43
  43.5 1.6 %collective-permute-done.7.refs_1_ = bf16[64,2048]{1,0:T(8,128)(2,1)S(1)} collective-permute-done((bf16[64,2048]{1,0:T(8,128)(2,1)S(1)}, bf16[64,2048]{1,0:T(8,128)(2,1)S(1)}, u32[]{:S(2)}, u32[]{:S(2)}) %collective-permute-start.7) | collective-permute-done | bytes 262176 | tf_op jit(solution)/shard_map/ppermute | solution.py:75
  45.1 3.1 %shard_map.99 = (bf16[128,3072]{1,0:T(8,128)(2,1)S(1)}, bf16[64,2048]{1,0:T(8,128)(2,1)S(1)}, bf16[32,2048]{1,0:T(8,128)(2,1)S(1)}, bf16[32,2048]{1,0:T(8,128)(2,1)S(1)}) custom-call(bf16[64,2048]{1,0:T(8,128)(2,1)S(1)} %shard_map.98.refs_0_, bf16[64,2048]{1,0:T(8,128)(2,1)S(1)} %collective-permute-done.7.refs_1_, ...), custom_call_target="tpu_custom_call" | custom-call | flops 1610612736 | bytes 65536 | tf_op jit(solution)/shard_map/pallas_call | solution.py:43
  48.2 1.3 %collective-permute-start.8 = (bf16[64,2048]{1,0:T(8,128)(2,1)S(1)}, bf16[64,2048]{1,0:T(8,128)(2,1)S(1)}, u32[]{:S(2)}, u32[]{:S(2)}) collective-permute-start(bf16[64,2048]{1,0:T(8,128)(2,1)S(1)} %get-tuple-element.21), channel_id=1, source_target_pairs={{0,4},{1,5},{2,6},{3,7},{4,0},{5,1},{6,2},{7,3},{8,12},{9,13},{10,... | collective-permute-start | bytes 786440 | tf_op jit(solution)/shard_map/ppermute | solution.py:75
  49.7 1.2 %collective-permute-start.10 = (bf16[32,2048]{1,0:T(8,128)(2,1)S(1)}, bf16[32,2048]{1,0:T(8,128)(2,1)S(1)}, u32[]{:S(2)}, u32[]{:S(2)}) collective-permute-start(bf16[32,2048]{1,0:T(8,128)(2,1)S(1)} %get-tuple-element.23), channel_id=1, source_target_pairs={{0,4},{1,5},{2,6},{3,7},{4,0},{5,1},{6,2},{7,3},{8,12},{9,13},{10,... | collective-permute-start | bytes 393224 | tf_op jit(solution)/shard_map/ppermute | solution.py:75
  51.0 1.2 %shard_map.100.refs_0_.refs_3_ = bf16[128,2048]{1,0:T(8,128)(2,1)S(1)} custom-call(bf16[128,3072]{1,0:T(8,128)(2,1)S(1)} %shard_map.97.refs_0_.refs_7_.mine, bf16[128,3072]{1,0:T(8,128)(2,1)S(1)} %get-tuple-element.20.theirs, bf16[1024,2048]{1,0:T(8,128)(2,1)S(1)} %get-tuple-element.16.refs_4_.w_out.refs_6_), custom_call_target="tpu_custom_call" | custom-call | flops 536870912 | bytes 65536 | tf_op jit(solution)/shard_map/pallas_call | solution.py:43
  53.0 2.7 %shard_map.102.refs_1_.refs_2_ = bf16[1,2,128,2048]{3,2,1,0:T(8,128)(2,1)} custom-call(bf16[128,2048]{1,0:T(8,128)(2,1)S(1)} %shard_map.100.refs_0_.refs_3_, s32[1,2]{1,0:T(1,128)S(4)} %get-tuple-element.13.order.refs_1_, bf16[1,2,128,2048]{3,2,1,0:T(8,128)(2,1)} %refs_2_.9, bf16[2,128,2048]{2,1,0:T(8,128)(2,1)} %refs_3_.9, ...), custom_call_target="tpu_custom_call" | custom-call | flops 1048576 | bytes 65536 | tf_op jit(solution)/shard_map/pallas_call | solution.py:43
  56.5 4.3 %collective-permute-start.12 = (bf16[64,2048]{1,0:T(8,128)(2,1)S(1)}, bf16[64,2048]{1,0:T(8,128)(2,1)S(1)}, u32[]{:S(2)}, u32[]{:S(2)}) collective-permute-start(bf16[64,2048]{1,0:T(8,128)(2,1)S(1)} %shard_map.103.refs_0_), channel_id=1, source_target_pairs={{0,8},{8,16},{16,24},{24,0},{1,9},{9,17},{17,25},{25,1},{2,10},{10... | collective-permute-start | bytes 786440 | tf_op jit(solution)/shard_map/ppermute | solution.py:60
  60.9 1.1 %collective-permute-done.10.refs_4_ = bf16[32,2048]{1,0:T(8,128)(2,1)S(1)} collective-permute-done((bf16[32,2048]{1,0:T(8,128)(2,1)S(1)}, bf16[32,2048]{1,0:T(8,128)(2,1)S(1)}, u32[]{:S(2)}, u32[]{:S(2)}) %collective-permute-start.10) | collective-permute-done | bytes 131104 | tf_op jit(solution)/shard_map/ppermute | solution.py:75
  62.9 2.5 %collective-permute-done.13.refs_1_ = bf16[32,2048]{1,0:T(8,128)(2,1)S(1)} collective-permute-done((bf16[32,2048]{1,0:T(8,128)(2,1)S(1)}, bf16[32,2048]{1,0:T(8,128)(2,1)S(1)}, u32[]{:S(2)}, u32[]{:S(2)}) %collective-permute-start.13) | collective-permute-done | bytes 131104 | tf_op jit(solution)/shard_map/ppermute | solution.py:60
  (31 shorter events, 8.0 us)
Async XLA Ops:
  0.6 9.3 %copy-start.1 = (f32[1,2048]{1,0:T(1,128)S(1)}, f32[1,2048]{1,0:T(1,128)}, u32[]{:S(2)}) copy-start(f32[1,2048]{1,0:T(1,128)} %refs_4_.3) | copy-start | bytes 24580
  0.6 9.3 %copy-start = (f32[1,2048]{1,0:T(1,128)S(1)}, f32[1,2048]{1,0:T(1,128)}, u32[]{:S(2)}) copy-start(f32[1,2048]{1,0:T(1,128)} %refs_3_.8) | copy-start | bytes 24580
  1.9 13.7 %collective-permute-start = (bf16[128,2048]{1,0:T(8,128)(2,1)S(1)}, bf16[128,2048]{1,0:T(8,128)(2,1)S(1)}, u32[]{:S(2)}, u32[]{:S(2)}) collective-permute-start(bf16[128,2048]{1,0:T(8,128)(2,1)S(1)} %get-tuple-element.14.refs_0_), channel_id=1, source_target_pairs={{0,4},{1,5},{2,6},{3,7},{4,0},{5,1},{6,2},{7,3},{8,12},{9,13},{10,... | collective-permute-start | bytes 1572872 | tf_op jit(solution)/shard_map/ppermute | solution.py:75
  19.0 6.7 %collective-permute-start.1 = (bf16[64,2048]{1,0:T(8,128)(2,1)S(1)}, bf16[64,2048]{1,0:T(8,128)(2,1)S(1)}, u32[]{:S(2)}, u32[]{:S(2)}) collective-permute-start(bf16[64,2048]{1,0:T(8,128)(2,1)S(1)} %get-tuple-element.18), channel_id=1, source_target_pairs={{0,4},{1,5},{2,6},{3,7},{4,0},{5,1},{6,2},{7,3},{8,12},{9,13},{10,... | collective-permute-start | bytes 786440 | tf_op jit(solution)/shard_map/ppermute | solution.py:75
  20.2 12.6 %collective-permute-start.3 = (bf16[64,2048]{1,0:T(8,128)(2,1)S(1)}, bf16[64,2048]{1,0:T(8,128)(2,1)S(1)}, u32[]{:S(2)}, u32[]{:S(2)}) collective-permute-start(bf16[64,2048]{1,0:T(8,128)(2,1)S(1)} %get-tuple-element.19), channel_id=1, source_target_pairs={{0,4},{1,5},{2,6},{3,7},{4,0},{5,1},{6,2},{7,3},{8,12},{9,13},{10,... | collective-permute-start | bytes 786440 | tf_op jit(solution)/shard_map/ppermute | solution.py:75
  21.6 21.6 %collective-permute-start.6 = (bf16[128,2048]{1,0:T(8,128)(2,1)S(1)}, bf16[128,2048]{1,0:T(8,128)(2,1)S(1)}, u32[]{:S(2)}, u32[]{:S(2)}) collective-permute-start(bf16[128,2048]{1,0:T(8,128)(2,1)S(1)} %shard_map.93.other), channel_id=1, source_target_pairs={{0,4},{1,5},{2,6},{3,7},{4,0},{5,1},{6,2},{7,3}} | collective-permute-start | bytes 1572872 | tf_op jit(solution)/shard_map/ppermute | solution.py:75
  25.8 10.9 %collective-permute-start.2 = (bf16[64,2048]{1,0:T(8,128)(2,1)S(1)}, bf16[64,2048]{1,0:T(8,128)(2,1)S(1)}, u32[]{:S(2)}, u32[]{:S(2)}) collective-permute-start(bf16[64,2048]{1,0:T(8,128)(2,1)S(1)} %shard_map.92.refs_1_), channel_id=1, source_target_pairs={{0,8},{8,16},{16,24},{1,9},{9,17},{17,25},{2,10},{10,18},{18,26},{... | collective-permute-start | bytes 786440 | tf_op jit(solution)/shard_map/ppermute | solution.py:60
  33.0 6.8 %collective-permute-start.4 = (bf16[64,2048]{1,0:T(8,128)(2,1)S(1)}, bf16[64,2048]{1,0:T(8,128)(2,1)S(1)}, u32[]{:S(2)}, u32[]{:S(2)}) collective-permute-start(bf16[64,2048]{1,0:T(8,128)(2,1)S(1)} %shard_map.95.refs_2_), channel_id=1, source_target_pairs={{0,8},{8,16},{16,24},{1,9},{9,17},{17,25},{2,10},{10,18},{18,26},{... | collective-permute-start | bytes 786440 | tf_op jit(solution)/shard_map/ppermute | solution.py:60
  36.7 6.5 %collective-permute-start.5 = (bf16[64,2048]{1,0:T(8,128)(2,1)S(1)}, bf16[64,2048]{1,0:T(8,128)(2,1)S(1)}, u32[]{:S(2)}, u32[]{:S(2)}) collective-permute-start(bf16[64,2048]{1,0:T(8,128)(2,1)S(1)} %shard_map.94.refs_0_.refs_2_), channel_id=1, source_target_pairs={{0,1},{1,0},{2,3},{3,2},{4,5},{5,4},{6,7},{7,6},{8,12},{9,13},{10,... | collective-permute-start | bytes 786440 | tf_op jit(solution)/shard_map/ppermute | solution.py:75
  39.8 5.3 %collective-permute-start.7 = (bf16[64,2048]{1,0:T(8,128)(2,1)S(1)}, bf16[64,2048]{1,0:T(8,128)(2,1)S(1)}, u32[]{:S(2)}, u32[]{:S(2)}) collective-permute-start(bf16[64,2048]{1,0:T(8,128)(2,1)S(1)} %shard_map.96.refs_1_.refs_2_), channel_id=1, source_target_pairs={{0,1},{1,0},{2,3},{3,2},{4,5},{5,4},{6,7},{7,6},{8,12},{9,13},{10,... | collective-permute-start | bytes 786440 | tf_op jit(solution)/shard_map/ppermute | solution.py:75
  48.2 8.2 %collective-permute-start.8 = (bf16[64,2048]{1,0:T(8,128)(2,1)S(1)}, bf16[64,2048]{1,0:T(8,128)(2,1)S(1)}, u32[]{:S(2)}, u32[]{:S(2)}) collective-permute-start(bf16[64,2048]{1,0:T(8,128)(2,1)S(1)} %get-tuple-element.21), channel_id=1, source_target_pairs={{0,4},{1,5},{2,6},{3,7},{4,0},{5,1},{6,2},{7,3},{8,12},{9,13},{10,... | collective-permute-start | bytes 786440 | tf_op jit(solution)/shard_map/ppermute | solution.py:75
  49.5 11.2 %collective-permute-start.9 = (bf16[32,2048]{1,0:T(8,128)(2,1)S(1)}, bf16[32,2048]{1,0:T(8,128)(2,1)S(1)}, u32[]{:S(2)}, u32[]{:S(2)}) collective-permute-start(bf16[32,2048]{1,0:T(8,128)(2,1)S(1)} %get-tuple-element.22), channel_id=1, source_target_pairs={{0,4},{1,5},{2,6},{3,7},{4,0},{5,1},{6,2},{7,3},{8,12},{9,13},{10,... | collective-permute-start | bytes 393224 | tf_op jit(solution)/shard_map/ppermute | solution.py:75
  49.7 12.2 %collective-permute-start.10 = (bf16[32,2048]{1,0:T(8,128)(2,1)S(1)}, bf16[32,2048]{1,0:T(8,128)(2,1)S(1)}, u32[]{:S(2)}, u32[]{:S(2)}) collective-permute-start(bf16[32,2048]{1,0:T(8,128)(2,1)S(1)} %get-tuple-element.23), channel_id=1, source_target_pairs={{0,4},{1,5},{2,6},{3,7},{4,0},{5,1},{6,2},{7,3},{8,12},{9,13},{10,... | collective-permute-start | bytes 393224 | tf_op jit(solution)/shard_map/ppermute | solution.py:75
  56.5 9.0 %collective-permute-start.12 = (bf16[64,2048]{1,0:T(8,128)(2,1)S(1)}, bf16[64,2048]{1,0:T(8,128)(2,1)S(1)}, u32[]{:S(2)}, u32[]{:S(2)}) collective-permute-start(bf16[64,2048]{1,0:T(8,128)(2,1)S(1)} %shard_map.103.refs_0_), channel_id=1, source_target_pairs={{0,8},{8,16},{16,24},{24,0},{1,9},{9,17},{17,25},{25,1},{2,10},{10... | collective-permute-start | bytes 786440 | tf_op jit(solution)/shard_map/ppermute | solution.py:60
  60.8 4.7 %collective-permute-start.13 = (bf16[32,2048]{1,0:T(8,128)(2,1)S(1)}, bf16[32,2048]{1,0:T(8,128)(2,1)S(1)}, u32[]{:S(2)}, u32[]{:S(2)}) collective-permute-start(bf16[32,2048]{1,0:T(8,128)(2,1)S(1)} %shard_map.104.refs_1_), channel_id=1, source_target_pairs={{0,8},{8,16},{16,24},{24,0},{1,9},{9,17},{17,25},{25,1},{2,10},{10... | collective-permute-start | bytes 393224 | tf_op jit(solution)/shard_map/ppermute | solution.py:60
  62.0 4.8 %collective-permute-start.11 = (bf16[32,2048]{1,0:T(8,128)(2,1)S(1)}, bf16[32,2048]{1,0:T(8,128)(2,1)S(1)}, u32[]{:S(2)}, u32[]{:S(2)}) collective-permute-start(bf16[32,2048]{1,0:T(8,128)(2,1)S(1)} %shard_map.105.refs_2_), channel_id=1, source_target_pairs={{0,8},{8,16},{16,24},{24,0},{1,9},{9,17},{17,25},{25,1},{2,10},{10... | collective-permute-start | bytes 393224 | tf_op jit(solution)/shard_map/ppermute | solution.py:60

commit v8 on v6

--- a/solution.py
+++ b/solution.py
@@ -99,18 +99,12 @@
         copy.wait()
 
 
-def other_kernel(order, acts, fresh, other, sems):
-    first = lax.axis_index("section") == 0
-    repeated = order[0, 0] == order[0, 1]
-    copy = pltpu.make_async_copy(acts.at[0, order[0, 1]], other, sems.at[0])
+def other_kernel(order, slots, fresh, other, entering, sem):
+    copy = pltpu.make_async_copy(fresh, entering, sem)
     copy.start()
     copy.wait()
-
-    @pl.when(jnp.logical_and(first, repeated))
-    def _():
-        again = pltpu.make_async_copy(fresh.at[0], other, sems.at[1])
-        again.start()
-        again.wait()
+    again = jnp.logical_and(lax.axis_index("section") == 0, order[0, 0] == order[0, 1])
+    other[...] = jnp.where(again, entering[0], slots[order[0, 1]])
 
 
 def normed(rows, gain, bias):
@@ -196,18 +190,32 @@
     following[...] = jnp.where(take, arriving[...], other[rows])
 
 
-def held_kernel(parts, order, acts, fresh, *refs):
-    arrived, held = refs[:parts], refs[parts]
+def held_kernel(order, slots, entering, *refs):
+    arrived, held, sems = refs[:-2], refs[-2], refs[-1]
     first = lax.axis_index("section") == 0
-    for slot in range(acts.shape[1]):
+    later = jnp.logical_not(first)
+
+    def write(condition, slot, blocks):
+        @pl.when(condition)
+        def _():
+            copies = []
+            at = 0
+            for i, block in enumerate(blocks):
+                target = held.at[0, slot, pl.ds(at, block.shape[0])]
+                copies.append(pltpu.make_async_copy(block, target, sems.at[i]))
+                at += block.shape[0]
+            for copy in copies:
+                copy.start()
+            for copy in copies:
+                copy.wait()
+
+    for slot in range(slots.shape[0]):
         old, new = order[0, 0] == slot, order[0, 1] == slot
-        at = 0
-        for chunk in arrived:
-            rows = slice(at, at + chunk.shape[0])
-            value = jnp.where(first, fresh[0, rows], chunk[...])
-            value = jnp.where(old, value, acts[0, slot, rows])
-            held[0, slot, rows] = jnp.where(new, fresh[1, rows], value)
-            at += chunk.shape[0]
+        stays = jnp.logical_not(new)
+        write(jnp.logical_and(first, new), slot, [entering.at[1]])
+        write(jnp.logical_and(first, jnp.logical_and(stays, old)), slot, [entering.at[0]])
+        write(jnp.logical_and(later, jnp.logical_and(stays, old)), slot, arrived)
+        write(jnp.logical_and(stays, jnp.logical_not(old)), slot, [slots.at[slot]])
 
 
 def put_kernel(tick, parts, *refs):
@@ -293,15 +301,22 @@
     ticks = fresh.shape[0]
     dma = pltpu.SemaphoreType.DMA
     acts, fresh, order, wqkv, wo = map(outside, (acts, fresh, order, wqkv, wo))
-    current, order = call(
+    current, order, slots = call(
         pick_kernel,
-        [inner((rows, width)), pltpu.SMEM(order.shape, order.dtype)],
-        [VMEM, SMEM],
+        [inner((rows, width)), pltpu.SMEM(order.shape, order.dtype), inner(acts.shape[1:])],
+        [VMEM, SMEM, VMEM],
         [ANY, ANY],
         [order, acts],
-        scratch=[inner(acts.shape[1:]), dma((2,))],
-    )
-    other = call(other_kernel, inner((rows, width)), VMEM, [SMEM, ANY, ANY], [order, acts, fresh], scratch=[dma((2,))])
+        scratch=[dma((2,))],
+    )
+    other, entering = call(
+        other_kernel,
+        [inner((rows, width)), inner(fresh.shape)],
+        [VMEM, VMEM],
+        [SMEM, VMEM, ANY],
+        [order, slots, fresh],
+        scratch=[dma],
+    )
     w_in, w_out = call(
         weights_kernel,
         [inner(wqkv.shape[1:]), inner(wo.shape[1:])],
@@ -336,11 +351,12 @@
                 wait=[own],
             )
             held = call(
-                functools.partial(held_kernel, parts),
+                held_kernel,
                 pltpu.HBM(acts.shape, BF16),
-                VMEM,
+                ANY,
                 [SMEM, VMEM, VMEM] + [VMEM] * parts,
-                [order, acts, fresh, *before],
+                [order, slots, entering, *before],
+                scratch=[dma((parts,))],
                 wait=[own],
             )
             section_out, held = outside(section_out), outside(held)

time: 74.6 us -> 73.5 us (0.985)
  Pallas kernels: 26.1 us -> 25.2 us
    pallas_call x21, Pallas kernels: 26.1 us -> 25.2 us  [call(): pl.pallas_call(kernel, out_shape=outs, out_specs=out_specs, in_specs=in_s...]
  transfers between devices with their start and end apart: 14 -> 14, of which waited for: 9 -> 9; matrix products, arithmetic and copies ran while one was open for 0% -> 0% of each run, Pallas kernels for 25% -> 24%
where the time goes in v8:
time: 73.5 us; the launch traced here: 73.3 us
  waiting for transfers between devices  29.2 us (40%)
  Pallas kernels  25.2 us (34%)
  starting transfers between devices  17.8 us (24%)
  between operations  1.02 us (1%)
    ppermute x9, waiting for transfers between devices, rotate(): return held_inside(lax.ppermute(block, names, route))  25.7 us
    pallas_call x21, Pallas kernels, call(): pl.pallas_call(kernel, out_shape=outs, out_specs=out_specs, in_specs=in_s...  25.2 us
    ppermute x9, starting transfers between devices, rotate(): return held_inside(lax.ppermute(block, names, route))  14.4 us
    ppermute x5, waiting for transfers between devices, from_behind(): lax.ppermute(block, axis, [(i, (i + 1) % size) for i in range(size - 1 +...  3.53 us
    ppermute x5, starting transfers between devices, from_behind(): lax.ppermute(block, axis, [(i, (i + 1) % size) for i in range(size - 1 +...  3.41 us
  transfers between devices with their start and end apart: 14, of which 9 were waited for; matrix products, arithmetic and copies ran while one was open for 0% of the time, Pallas kernels for 24%

profile of v8, /device:TPU:0, one launch (start us, length us, event | category | flops | bytes accessed | tf_op | source)
XLA Modules:
  0.0 73.3 jit_solution(7769909376612969331)
XLA Ops:
  1.9 3.0 %collective-permute-start = (bf16[128,2048]{1,0:T(8,128)(2,1)S(1)}, bf16[128,2048]{1,0:T(8,128)(2,1)S(1)}, u32[]{:S(2)}, u32[]{:S(2)}) collective-permute-start(bf16[128,2048]{1,0:T(8,128)(2,1)S(1)} %get-tuple-element.17.refs_0_), channel_id=1, source_target_pairs={{0,4},{1,5},{2,6},{3,7},{4,0},{5,1},{6,2},{7,3},{8,12},{9,13},{10,... | collective-permute-start | bytes 1572872 | tf_op jit(solution)/shard_map/ppermute | solution.py:75
  5.0 5.9 %shard_map.87 = (bf16[2048,3072]{1,0:T(8,128)(2,1)S(1)}, bf16[1024,2048]{1,0:T(8,128)(2,1)S(1)}) custom-call(bf16[1,2048,3072]{2,1,0:T(8,128)(2,1)} %w_in.1, bf16[1,1024,2048]{2,1,0:T(8,128)(2,1)} %w_out.1), custom_call_target="tpu_custom_call" | custom-call | flops 1073741824 | bytes 65536 | tf_op jit(solution)/shard_map/pallas_call | solution.py:43
  10.9 2.1 %shard_map.88.refs_5_.mine = bf16[128,3072]{1,0:T(8,128)(2,1)S(1)} custom-call(bf16[128,2048]{1,0:T(8,128)(2,1)S(1)} %get-tuple-element.17.refs_0_, f32[1,2048]{1,0:T(1,128)S(1)} %copy-done, f32[1,2048]{1,0:T(1,128)S(1)} %copy-done.1, bf16[2048,3072]{1,0:T(8,128)(2,1)S(1)} %get-tuple-element.18.refs_3_.refs_4_.refs_5_), custom_call_target="tpu_custom_call" | custom-call | flops 1610612736 | bytes 65536 | tf_op jit(solution)/shard_map/pallas_call | solution.py:43
  13.0 3.9 %collective-permute-done.refs_0_ = bf16[128,2048]{1,0:T(8,128)(2,1)S(1)} collective-permute-done((bf16[128,2048]{1,0:T(8,128)(2,1)S(1)}, bf16[128,2048]{1,0:T(8,128)(2,1)S(1)}, u32[]{:S(2)}, u32[]{:S(2)}) %collective-permute-start) | collective-permute-done | bytes 524320 | tf_op jit(solution)/shard_map/ppermute | solution.py:75
  16.9 3.2 %shard_map.89 = (bf16[128,3072]{1,0:T(8,128)(2,1)S(1)}, bf16[64,2048]{1,0:T(8,128)(2,1)S(1)}, bf16[64,2048]{1,0:T(8,128)(2,1)S(1)}) custom-call(bf16[128,2048]{1,0:T(8,128)(2,1)S(1)} %collective-permute-done.refs_0_, f32[1,2048]{1,0:T(1,128)S(1)} %copy-done, f32[1,2048]{1,0:T(1,128)S(1)} %copy-done.1, ...), custom_call_target="tpu_custom_call" | custom-call | flops 1610612736 | bytes 65536 | tf_op jit(solution)/shard_map/pallas_call | solution.py:43
  20.1 1.8 %collective-permute-start.1 = (bf16[64,2048]{1,0:T(8,128)(2,1)S(1)}, bf16[64,2048]{1,0:T(8,128)(2,1)S(1)}, u32[]{:S(2)}, u32[]{:S(2)}) collective-permute-start(bf16[64,2048]{1,0:T(8,128)(2,1)S(1)} %get-tuple-element.21), channel_id=1, source_target_pairs={{0,4},{1,5},{2,6},{3,7},{4,0},{5,1},{6,2},{7,3},{8,12},{9,13},{10,... | collective-permute-start | bytes 786440 | tf_op jit(solution)/shard_map/ppermute | solution.py:75
  22.2 1.3 %shard_map.92 = (bf16[128,2048]{1,0:T(8,128)(2,1)S(1)}, bf16[2,128,2048]{2,1,0:T(8,128)(2,1)S(1)}) custom-call(s32[1,2]{1,0:T(1,128)S(4)} %get-tuple-element.16.order.refs_1_, bf16[2,128,2048]{2,1,0:T(8,128)(2,1)S(1)} %get-tuple-element.22.slots.refs_2_, bf16[2,128,2048]{2,1,0:T(8,128)(2,1)} %fresh.1), custom_call_target="tpu_custom_call" | custom-call | flops 1048576 | bytes 65536 | tf_op jit(solution)/shard_map/pallas_call | solution.py:43
  24.7 4.6 %collective-permute-done.1.refs_2_ = bf16[64,2048]{1,0:T(8,128)(2,1)S(1)} collective-permute-done((bf16[64,2048]{1,0:T(8,128)(2,1)S(1)}, bf16[64,2048]{1,0:T(8,128)(2,1)S(1)}, u32[]{:S(2)}, u32[]{:S(2)}) %collective-permute-start.1) | collective-permute-done | bytes 262176 | tf_op jit(solution)/shard_map/ppermute | solution.py:75
  29.4 1.3 %collective-permute-start.2 = (bf16[64,2048]{1,0:T(8,128)(2,1)S(1)}, bf16[64,2048]{1,0:T(8,128)(2,1)S(1)}, u32[]{:S(2)}, u32[]{:S(2)}) collective-permute-start(bf16[64,2048]{1,0:T(8,128)(2,1)S(1)} %shard_map.91.refs_1_), channel_id=1, source_target_pairs={{0,8},{8,16},{16,24},{1,9},{9,17},{17,25},{2,10},{10,18},{18,26},{... | collective-permute-start | bytes 786440 | tf_op jit(solution)/shard_map/ppermute | solution.py:60
  30.7 2.5 %collective-permute-done.3.refs_2_ = bf16[64,2048]{1,0:T(8,128)(2,1)S(1)} collective-permute-done((bf16[64,2048]{1,0:T(8,128)(2,1)S(1)}, bf16[64,2048]{1,0:T(8,128)(2,1)S(1)}, u32[]{:S(2)}, u32[]{:S(2)}) %collective-permute-start.3) | collective-permute-done | bytes 262176 | tf_op jit(solution)/shard_map/ppermute | solution.py:75
  33.3 1.9 %collective-permute-start.4 = (bf16[64,2048]{1,0:T(8,128)(2,1)S(1)}, bf16[64,2048]{1,0:T(8,128)(2,1)S(1)}, u32[]{:S(2)}, u32[]{:S(2)}) collective-permute-start(bf16[64,2048]{1,0:T(8,128)(2,1)S(1)} %shard_map.94.refs_2_), channel_id=1, source_target_pairs={{0,8},{8,16},{16,24},{1,9},{9,17},{17,25},{2,10},{10,18},{18,26},{... | collective-permute-start | bytes 786440 | tf_op jit(solution)/shard_map/ppermute | solution.py:60
  35.3 3.6 %collective-permute-start.7 = (bf16[128,2048]{1,0:T(8,128)(2,1)S(1)}, bf16[128,2048]{1,0:T(8,128)(2,1)S(1)}, u32[]{:S(2)}, u32[]{:S(2)}) collective-permute-start(bf16[128,2048]{1,0:T(8,128)(2,1)S(1)} %get-tuple-element.23.other), channel_id=1, source_target_pairs={{0,4},{1,5},{2,6},{3,7},{4,0},{5,1},{6,2},{7,3}} | collective-permute-start | bytes 1572872 | tf_op jit(solution)/shard_map/ppermute | solution.py:75
  38.9 1.6 %collective-permute-start.5 = (bf16[64,2048]{1,0:T(8,128)(2,1)S(1)}, bf16[64,2048]{1,0:T(8,128)(2,1)S(1)}, u32[]{:S(2)}, u32[]{:S(2)}) collective-permute-start(bf16[64,2048]{1,0:T(8,128)(2,1)S(1)} %shard_map.93.refs_0_.refs_2_), channel_id=1, source_target_pairs={{0,1},{1,0},{2,3},{3,2},{4,5},{5,4},{6,7},{7,6},{8,12},{9,13},{10,... | collective-permute-start | bytes 786440 | tf_op jit(solution)/shard_map/ppermute | solution.py:75
  41.1 2.1 %shard_map.96.refs_7_.mine = bf16[128,3072]{1,0:T(8,128)(2,1)S(1)} custom-call(bf16[64,2048]{1,0:T(8,128)(2,1)S(1)} %shard_map.93.refs_0_.refs_2_, bf16[64,2048]{1,0:T(8,128)(2,1)S(1)} %shard_map.95.refs_1_.refs_2_, f32[1,2048]{1,0:T(1,128)S(1)} %copy-done, f32[1,2048]{1,0:T(1,128)S(1)} %copy-done.1, ...), custom_call_target="tpu_custom_call" | custom-call | flops 1610612736 | bytes 65536 | tf_op jit(solution)/shard_map/pallas_call | solution.py:43
  43.2 8.5 %collective-permute-done.7.refs_2_ = bf16[128,2048]{1,0:T(8,128)(2,1)S(1)} collective-permute-done((bf16[128,2048]{1,0:T(8,128)(2,1)S(1)}, bf16[128,2048]{1,0:T(8,128)(2,1)S(1)}, u32[]{:S(2)}, u32[]{:S(2)}) %collective-permute-start.7) | collective-permute-done | bytes 524320 | tf_op jit(solution)/shard_map/ppermute | solution.py:75
  51.7 3.2 %shard_map.97 = (bf16[128,3072]{1,0:T(8,128)(2,1)S(1)}, bf16[64,2048]{1,0:T(8,128)(2,1)S(1)}, bf16[32,2048]{1,0:T(8,128)(2,1)S(1)}, bf16[32,2048]{1,0:T(8,128)(2,1)S(1)}) custom-call(bf16[64,2048]{1,0:T(8,128)(2,1)S(1)} %collective-permute-done.5.refs_0_, bf16[64,2048]{1,0:T(8,128)(2,1)S(1)} %collective-permute-done.6.refs_1_, ...), custom_call_target="tpu_custom_call" | custom-call | flops 1610612736 | bytes 65536 | tf_op jit(solution)/shard_map/pallas_call | solution.py:43
  54.9 1.5 %collective-permute-start.8 = (bf16[64,2048]{1,0:T(8,128)(2,1)S(1)}, bf16[64,2048]{1,0:T(8,128)(2,1)S(1)}, u32[]{:S(2)}, u32[]{:S(2)}) collective-permute-start(bf16[64,2048]{1,0:T(8,128)(2,1)S(1)} %get-tuple-element.27), channel_id=1, source_target_pairs={{0,4},{1,5},{2,6},{3,7},{4,0},{5,1},{6,2},{7,3},{8,12},{9,13},{10,... | collective-permute-start | bytes 786440 | tf_op jit(solution)/shard_map/ppermute | solution.py:75
  57.0 1.5 %collective-permute-start.10 = (bf16[32,2048]{1,0:T(8,128)(2,1)S(1)}, bf16[32,2048]{1,0:T(8,128)(2,1)S(1)}, u32[]{:S(2)}, u32[]{:S(2)}) collective-permute-start(bf16[32,2048]{1,0:T(8,128)(2,1)S(1)} %get-tuple-element.29), channel_id=1, source_target_pairs={{0,4},{1,5},{2,6},{3,7},{4,0},{5,1},{6,2},{7,3},{8,12},{9,13},{10,... | collective-permute-start | bytes 393224 | tf_op jit(solution)/shard_map/ppermute | solution.py:75
  60.5 1.6 %shard_map.100.refs_1_.refs_2_ = bf16[1,2,128,2048]{3,2,1,0:T(8,128)(2,1)} custom-call(bf16[128,2048]{1,0:T(8,128)(2,1)S(1)} %shard_map.98.refs_0_.refs_3_, s32[1,2]{1,0:T(1,128)S(4)} %get-tuple-element.16.order.refs_1_, bf16[2,128,2048]{2,1,0:T(8,128)(2,1)S(1)} %get-tuple-element.22.slots.refs_2_, bf16[2,128,2048]{2,1,0:T(8,128)(2,1)S(1)} %get-tuple-element.26.refs_3_, ...), custom_call_target="tpu_custom_call" | custom-call | flops 1048576 | bytes 65536 | tf_op jit(solution)/shard_map/pallas_call | solution.py:43
  62.1 2.0 %collective-permute-done.8.refs_4_ = bf16[64,2048]{1,0:T(8,128)(2,1)S(1)} collective-permute-done((bf16[64,2048]{1,0:T(8,128)(2,1)S(1)}, bf16[64,2048]{1,0:T(8,128)(2,1)S(1)}, u32[]{:S(2)}, u32[]{:S(2)}) %collective-permute-start.8) | collective-permute-done | bytes 262176 | tf_op jit(solution)/shard_map/ppermute | solution.py:75
  64.3 2.6 %collective-permute-done.9.refs_4_ = bf16[32,2048]{1,0:T(8,128)(2,1)S(1)} collective-permute-done((bf16[32,2048]{1,0:T(8,128)(2,1)S(1)}, bf16[32,2048]{1,0:T(8,128)(2,1)S(1)}, u32[]{:S(2)}, u32[]{:S(2)}) %collective-permute-start.9) | collective-permute-done | bytes 131104 | tf_op jit(solution)/shard_map/ppermute | solution.py:75
  67.1 1.5 %collective-permute-done.10.refs_4_ = bf16[32,2048]{1,0:T(8,128)(2,1)S(1)} collective-permute-done((bf16[32,2048]{1,0:T(8,128)(2,1)S(1)}, bf16[32,2048]{1,0:T(8,128)(2,1)S(1)}, u32[]{:S(2)}, u32[]{:S(2)}) %collective-permute-start.10) | collective-permute-done | bytes 131104 | tf_op jit(solution)/shard_map/ppermute | solution.py:75
  69.5 1.9 %collective-permute-done.13.refs_1_ = bf16[32,2048]{1,0:T(8,128)(2,1)S(1)} collective-permute-done((bf16[32,2048]{1,0:T(8,128)(2,1)S(1)}, bf16[32,2048]{1,0:T(8,128)(2,1)S(1)}, u32[]{:S(2)}, u32[]{:S(2)}) %collective-permute-start.13) | collective-permute-done | bytes 131104 | tf_op jit(solution)/shard_map/ppermute | solution.py:60
  71.5 1.6 %collective-permute-done.11.refs_0_ = bf16[32,2048]{1,0:T(8,128)(2,1)S(1)} collective-permute-done((bf16[32,2048]{1,0:T(8,128)(2,1)S(1)}, bf16[32,2048]{1,0:T(8,128)(2,1)S(1)}, u32[]{:S(2)}, u32[]{:S(2)}) %collective-permute-start.11) | collective-permute-done | bytes 131104 | tf_op jit(solution)/shard_map/ppermute | solution.py:60
  (29 shorter events, 7.4 us)
Async XLA Ops:
  0.6 10.2 %copy-start.1 = (f32[1,2048]{1,0:T(1,128)S(1)}, f32[1,2048]{1,0:T(1,128)}, u32[]{:S(2)}) copy-start(f32[1,2048]{1,0:T(1,128)} %refs_4_.1) | copy-start | bytes 24580
  0.6 10.2 %copy-start = (f32[1,2048]{1,0:T(1,128)S(1)}, f32[1,2048]{1,0:T(1,128)}, u32[]{:S(2)}) copy-start(f32[1,2048]{1,0:T(1,128)} %refs_3_.3) | copy-start | bytes 24580
  1.9 15.0 %collective-permute-start = (bf16[128,2048]{1,0:T(8,128)(2,1)S(1)}, bf16[128,2048]{1,0:T(8,128)(2,1)S(1)}, u32[]{:S(2)}, u32[]{:S(2)}) collective-permute-start(bf16[128,2048]{1,0:T(8,128)(2,1)S(1)} %get-tuple-element.17.refs_0_), channel_id=1, source_target_pairs={{0,4},{1,5},{2,6},{3,7},{4,0},{5,1},{6,2},{7,3},{8,12},{9,13},{10,... | collective-permute-start | bytes 1572872 | tf_op jit(solution)/shard_map/ppermute | solution.py:75
  20.1 9.2 %collective-permute-start.1 = (bf16[64,2048]{1,0:T(8,128)(2,1)S(1)}, bf16[64,2048]{1,0:T(8,128)(2,1)S(1)}, u32[]{:S(2)}, u32[]{:S(2)}) collective-permute-start(bf16[64,2048]{1,0:T(8,128)(2,1)S(1)} %get-tuple-element.21), channel_id=1, source_target_pairs={{0,4},{1,5},{2,6},{3,7},{4,0},{5,1},{6,2},{7,3},{8,12},{9,13},{10,... | collective-permute-start | bytes 786440 | tf_op jit(solution)/shard_map/ppermute | solution.py:75
  21.9 11.3 %collective-permute-start.3 = (bf16[64,2048]{1,0:T(8,128)(2,1)S(1)}, bf16[64,2048]{1,0:T(8,128)(2,1)S(1)}, u32[]{:S(2)}, u32[]{:S(2)}) collective-permute-start(bf16[64,2048]{1,0:T(8,128)(2,1)S(1)} %get-tuple-element.24), channel_id=1, source_target_pairs={{0,4},{1,5},{2,6},{3,7},{4,0},{5,1},{6,2},{7,3},{8,12},{9,13},{10,... | collective-permute-start | bytes 786440 | tf_op jit(solution)/shard_map/ppermute | solution.py:75
  29.4 9.4 %collective-permute-start.2 = (bf16[64,2048]{1,0:T(8,128)(2,1)S(1)}, bf16[64,2048]{1,0:T(8,128)(2,1)S(1)}, u32[]{:S(2)}, u32[]{:S(2)}) collective-permute-start(bf16[64,2048]{1,0:T(8,128)(2,1)S(1)} %shard_map.91.refs_1_), channel_id=1, source_target_pairs={{0,8},{8,16},{16,24},{1,9},{9,17},{17,25},{2,10},{10,18},{18,26},{... | collective-permute-start | bytes 786440 | tf_op jit(solution)/shard_map/ppermute | solution.py:60
  33.3 7.2 %collective-permute-start.4 = (bf16[64,2048]{1,0:T(8,128)(2,1)S(1)}, bf16[64,2048]{1,0:T(8,128)(2,1)S(1)}, u32[]{:S(2)}, u32[]{:S(2)}) collective-permute-start(bf16[64,2048]{1,0:T(8,128)(2,1)S(1)} %shard_map.94.refs_2_), channel_id=1, source_target_pairs={{0,8},{8,16},{16,24},{1,9},{9,17},{17,25},{2,10},{10,18},{18,26},{... | collective-permute-start | bytes 786440 | tf_op jit(solution)/shard_map/ppermute | solution.py:60
  35.3 16.4 %collective-permute-start.7 = (bf16[128,2048]{1,0:T(8,128)(2,1)S(1)}, bf16[128,2048]{1,0:T(8,128)(2,1)S(1)}, u32[]{:S(2)}, u32[]{:S(2)}) collective-permute-start(bf16[128,2048]{1,0:T(8,128)(2,1)S(1)} %get-tuple-element.23.other), channel_id=1, source_target_pairs={{0,4},{1,5},{2,6},{3,7},{4,0},{5,1},{6,2},{7,3}} | collective-permute-start | bytes 1572872 | tf_op jit(solution)/shard_map/ppermute | solution.py:75
  38.9 12.8 %collective-permute-start.5 = (bf16[64,2048]{1,0:T(8,128)(2,1)S(1)}, bf16[64,2048]{1,0:T(8,128)(2,1)S(1)}, u32[]{:S(2)}, u32[]{:S(2)}) collective-permute-start(bf16[64,2048]{1,0:T(8,128)(2,1)S(1)} %shard_map.93.refs_0_.refs_2_), channel_id=1, source_target_pairs={{0,1},{1,0},{2,3},{3,2},{4,5},{5,4},{6,7},{7,6},{8,12},{9,13},{10,... | collective-permute-start | bytes 786440 | tf_op jit(solution)/shard_map/ppermute | solution.py:75
  40.6 11.1 %collective-permute-start.6 = (bf16[64,2048]{1,0:T(8,128)(2,1)S(1)}, bf16[64,2048]{1,0:T(8,128)(2,1)S(1)}, u32[]{:S(2)}, u32[]{:S(2)}) collective-permute-start(bf16[64,2048]{1,0:T(8,128)(2,1)S(1)} %shard_map.95.refs_1_.refs_2_), channel_id=1, source_target_pairs={{0,1},{1,0},{2,3},{3,2},{4,5},{5,4},{6,7},{7,6},{8,12},{9,13},{10,... | collective-permute-start | bytes 786440 | tf_op jit(solution)/shard_map/ppermute | solution.py:75
  54.9 9.2 %collective-permute-start.8 = (bf16[64,2048]{1,0:T(8,128)(2,1)S(1)}, bf16[64,2048]{1,0:T(8,128)(2,1)S(1)}, u32[]{:S(2)}, u32[]{:S(2)}) collective-permute-start(bf16[64,2048]{1,0:T(8,128)(2,1)S(1)} %get-tuple-element.27), channel_id=1, source_target_pairs={{0,4},{1,5},{2,6},{3,7},{4,0},{5,1},{6,2},{7,3},{8,12},{9,13},{10,... | collective-permute-start | bytes 786440 | tf_op jit(solution)/shard_map/ppermute | solution.py:75
  56.4 10.5 %collective-permute-start.9 = (bf16[32,2048]{1,0:T(8,128)(2,1)S(1)}, bf16[32,2048]{1,0:T(8,128)(2,1)S(1)}, u32[]{:S(2)}, u32[]{:S(2)}) collective-permute-start(bf16[32,2048]{1,0:T(8,128)(2,1)S(1)} %get-tuple-element.28), channel_id=1, source_target_pairs={{0,4},{1,5},{2,6},{3,7},{4,0},{5,1},{6,2},{7,3},{8,12},{9,13},{10,... | collective-permute-start | bytes 393224 | tf_op jit(solution)/shard_map/ppermute | solution.py:75
  57.0 11.6 %collective-permute-start.10 = (bf16[32,2048]{1,0:T(8,128)(2,1)S(1)}, bf16[32,2048]{1,0:T(8,128)(2,1)S(1)}, u32[]{:S(2)}, u32[]{:S(2)}) collective-permute-start(bf16[32,2048]{1,0:T(8,128)(2,1)S(1)} %get-tuple-element.29), channel_id=1, source_target_pairs={{0,4},{1,5},{2,6},{3,7},{4,0},{5,1},{6,2},{7,3},{8,12},{9,13},{10,... | collective-permute-start | bytes 393224 | tf_op jit(solution)/shard_map/ppermute | solution.py:75
  64.2 7.3 %collective-permute-start.12 = (bf16[64,2048]{1,0:T(8,128)(2,1)S(1)}, bf16[64,2048]{1,0:T(8,128)(2,1)S(1)}, u32[]{:S(2)}, u32[]{:S(2)}) collective-permute-start(bf16[64,2048]{1,0:T(8,128)(2,1)S(1)} %shard_map.101.refs_0_), channel_id=1, source_target_pairs={{0,8},{8,16},{16,24},{24,0},{1,9},{9,17},{17,25},{25,1},{2,10},{10... | collective-permute-start | bytes 786440 | tf_op jit(solution)/shard_map/ppermute | solution.py:60
  67.0 4.5 %collective-permute-start.13 = (bf16[32,2048]{1,0:T(8,128)(2,1)S(1)}, bf16[32,2048]{1,0:T(8,128)(2,1)S(1)}, u32[]{:S(2)}, u32[]{:S(2)}) collective-permute-start(bf16[32,2048]{1,0:T(8,128)(2,1)S(1)} %shard_map.102.refs_1_), channel_id=1, source_target_pairs={{0,8},{8,16},{16,24},{24,0},{1,9},{9,17},{17,25},{25,1},{2,10},{10... | collective-permute-start | bytes 393224 | tf_op jit(solution)/shard_map/ppermute | solution.py:60
  68.7 4.4 %collective-permute-start.11 = (bf16[32,2048]{1,0:T(8,128)(2,1)S(1)}, bf16[32,2048]{1,0:T(8,128)(2,1)S(1)}, u32[]{:S(2)}, u32[]{:S(2)}) collective-permute-start(bf16[32,2048]{1,0:T(8,128)(2,1)S(1)} %shard_map.103.refs_2_), channel_id=1, source_target_pairs={{0,8},{8,16},{16,24},{24,0},{1,9},{9,17},{17,25},{25,1},{2,10},{10... | collective-permute-start | bytes 393224 | tf_op jit(solution)/shard_map/ppermute | solution.py:60
